TPU v7x, 8 devices: a whole 2x2x1 slice. The times are simulated.
8 devices in a mesh: dz: 2 (over z, y), dy: 2 (over x), dx: 2 (over core).
Axes of the slice: x: 2, y: 2, z: 1, core: 2. Of those that a mesh axis runs over, the one named last changes fastest.
Arguments:
- x: bfloat16 [32768, 1280], P(('dx', 'dy', 'dz'))
- g: bfloat16 [32768, 1280], P(('dx', 'dy', 'dz'))
- w1: bfloat16 [1280, 5120], replicated
- w2: bfloat16 [5120, 1280], replicated
- w3: bfloat16 [1280, 5120], replicated
- w4: bfloat16 [5120, 1280], replicated
- m1: float32 [1280, 5120], P(('dx', 'dy', 'dz'))
- m2: float32 [5120, 1280], P(('dx', 'dy', 'dz'))
- m3: float32 [1280, 5120], P(('dx', 'dy', 'dz'))
- m4: float32 [5120, 1280], P(('dx', 'dy', 'dz'))
Outputs:
- output 1: bfloat16 [32768, 1280], P(('dx', 'dy', 'dz'))
- output 2: bfloat16 [1280, 5120], replicated
- output 3: bfloat16 [5120, 1280], replicated
- output 4: bfloat16 [1280, 5120], replicated
- output 5: bfloat16 [5120, 1280], replicated
- output 6: float32 [1280, 5120], P(('dx', 'dy', 'dz'))
- output 7: float32 [5120, 1280], P(('dx', 'dy', 'dz'))
- output 8: float32 [1280, 5120], P(('dx', 'dy', 'dz'))
- output 9: float32 [5120, 1280], P(('dx', 'dy', 'dz'))
All inputs are finite; a program needn't handle non-finite values.
Results may differ from a plain program's by a relative error of at most 0.0121537.
Values are sent between devices in bfloat16 or wider.
A program may use at most 1 GiB of HBM per device.

v0:
```python
import jax
import jax.numpy as jnp
from jax import lax
from jax.sharding import PartitionSpec as P

LR = 0.0005
MU = 0.9
DATA = ("dx", "dy", "dz")


def _gelu(z):
    return jax.nn.gelu(z, approximate=True)


def _gelu_grad(z, dh):
    return jax.vjp(_gelu, z.astype(jnp.float32))[1](dh.astype(jnp.float32))[0]


def solution(mesh):
    ndy, ndz = mesh.shape["dy"], mesh.shape["dz"]
    n = mesh.shape["dx"] * ndy * ndz
    f32, bf = jnp.float32, jnp.bfloat16

    def reduce_scatter(s):
        for ax in DATA:
            s = lax.psum_scatter(s, ax, scatter_dimension=0, tiled=True)
        return s

    def all_gather(w):
        for ax in reversed(DATA):
            w = lax.all_gather(w, ax, axis=0, tiled=True)
        return w

    def update(w, m, s):
        idx = (lax.axis_index("dx") * ndy + lax.axis_index("dy")) * ndz + lax.axis_index("dz")
        rows = m.shape[0]
        w_loc = lax.dynamic_slice_in_dim(w, idx * rows, rows, 0).astype(f32)
        m_new = MU * m + s / n
        return all_gather((w_loc - LR * m_new).astype(bf)), m_new

    def local(x, g, w1, w2, w3, w4, m1, m2, m3, m4):
        z1 = jnp.dot(x, w1, preferred_element_type=f32).astype(bf)
        h1 = _gelu(z1.astype(f32)).astype(bf)
        h2 = (jnp.dot(h1, w2, preferred_element_type=f32) + x.astype(f32)).astype(bf)
        z3 = jnp.dot(h2, w3, preferred_element_type=f32).astype(bf)
        h3 = _gelu(z3.astype(f32)).astype(bf)
        s4 = reduce_scatter(jnp.dot(h3.T, g, preferred_element_type=f32))
        dh3 = jnp.dot(g, w4.T, preferred_element_type=f32).astype(bf)
        dz3 = _gelu_grad(z3, dh3).astype(bf)
        s3 = reduce_scatter(jnp.dot(h2.T, dz3, preferred_element_type=f32))
        dh2 = (jnp.dot(dz3, w3.T, preferred_element_type=f32) + g.astype(f32)).astype(bf)
        s2 = reduce_scatter(jnp.dot(h1.T, dh2, preferred_element_type=f32))
        dh1 = jnp.dot(dh2, w2.T, preferred_element_type=f32).astype(bf)
        dz1 = _gelu_grad(z1, dh1).astype(bf)
        s1 = reduce_scatter(jnp.dot(x.T, dz1, preferred_element_type=f32))
        dx = (jnp.dot(dz1, w1.T, preferred_element_type=f32) + dh2.astype(f32)).astype(bf)
        w4n, m4n = update(w4, m4, s4)
        w3n, m3n = update(w3, m3, s3)
        w2n, m2n = update(w2, m2, s2)
        w1n, m1n = update(w1, m1, s1)
        return (dx, w1n, w2n, w3n, w4n, m1n, m2n, m3n, m4n)

    row, rep = P(DATA, None), P()
    return jax.shard_map(local, mesh=mesh,
                         in_specs=(row, row, rep, rep, rep, rep, row, row, row, row),
                         out_specs=(row, rep, rep, rep, rep, row, row, row, row),
                         check_vma=False)
```

profile of v0, /device:TPU:0, one launch (start us, length us, event | category | flops | bytes accessed | tf_op | source)
XLA Modules:
  0.0 2399.6 jit_solution(18190288066193139063)
XLA Ops:
  7.2 63.2 %convolution_convert_fusion.1 = bf16[4096,5120]{1,0:T(8,128)(2,1)} fusion(bf16[4096,1280]{1,0:T(8,128)(2,1)} %param.10, bf16[1280,5120]{1,0:T(8,128)(2,1)} %param.12), kind=kOutput, calls=%fused_computation.36 | convolution fusion | flops 53708062720 | bytes 65536000 | tf_op jit(solution)/shard_map/dot_general | solution.py:42
  70.4 77.9 %add_convert_fusion.2 = bf16[4096,1280]{1,0:T(8,128)(2,1)} fusion(bf16[4096,1280]{1,0:T(8,128)(2,1)} %param.10, bf16[5120,1280]{1,0:T(8,128)(2,1)S(1)} %copy-done.2, bf16[4096,5120]{1,0:T(8,128)(2,1)} %convolution_convert_fusion.1), kind=kOutput, calls=%fused_computation.40 | convolution fusion | flops 53912535040 | bytes 76021760 | tf_op jit(solution)/shard_map/dot_general | solution.py:44
  148.3 63.1 %convolution_convert_fusion = bf16[4096,5120]{1,0:T(8,128)(2,1)} fusion(bf16[4096,1280]{1,0:T(8,128)(2,1)} %add_convert_fusion.2, bf16[1280,5120]{1,0:T(8,128)(2,1)} %param.14), kind=kOutput, calls=%fused_computation.35 | convolution fusion | flops 53708062720 | bytes 65536000 | tf_op jit(solution)/shard_map/dot_general | solution.py:45
  211.5 86.1 %fusion.22 = f32[5120,1280]{1,0:T(8,128)} fusion(bf16[4096,1280]{1,0:T(8,128)(2,1)} %param.11, bf16[4096,5120]{1,0:T(8,128)(2,1)} %convolution_convert_fusion), kind=kOutput, calls=%fused_computation.34 | convolution fusion | flops 53896806400 | bytes 78643200 | tf_op jit(solution)/shard_map/dot_general | solution.py:47
  297.7 115.7 %fusion.4 = bf16[4096,5120]{1,0:T(8,128)(2,1)} fusion(bf16[4096,5120]{1,0:T(8,128)(2,1)} %convolution_convert_fusion, bf16[4096,1280]{1,0:T(8,128)(2,1)} %param.11, bf16[5120,1280]{1,0:T(8,128)(2,1)} %param.15), kind=kOutput, calls=%fused_computation.16 | convolution fusion | flops 54169436160 | bytes 107479040 | tf_op jit(solution)/shard_map/dot_general | solution.py:48
  413.3 61.4 %fusion.31 = f32[1280,5120]{1,0:T(8,128)} fusion(bf16[4096,1280]{1,0:T(8,128)(2,1)S(1)} %copy-done.4, bf16[4096,5120]{1,0:T(8,128)(2,1)} %fusion.4), kind=kOutput, calls=%fused_computation.56 | convolution fusion | flops 53687091200 | bytes 78643200 | tf_op jit(solution)/shard_map/dot_general | solution.py:50
  474.8 63.5 %add_convert_fusion.1 = bf16[4096,1280]{1,0:T(8,128)(2,1)} fusion(bf16[4096,1280]{1,0:T(8,128)(2,1)} %param.11, bf16[4096,5120]{1,0:T(8,128)(2,1)} %fusion.4, bf16[1280,5120]{1,0:T(8,128)(2,1)} %param.14), kind=kOutput, calls=%fused_computation.39 | convolution fusion | flops 53702819840 | bytes 76021760 | tf_op jit(solution)/shard_map/dot_general | solution.py:51
  538.4 76.9 %fusion.28 = f32[5120,1280]{1,0:T(8,128)} fusion(bf16[4096,1280]{1,0:T(8,128)(2,1)} %add_convert_fusion.1, bf16[4096,5120]{1,0:T(8,128)(2,1)} %convolution_convert_fusion.1), kind=kOutput, calls=%fused_computation.55 | convolution fusion | flops 53896806400 | bytes 78643200 | tf_op jit(solution)/shard_map/dot_general | solution.py:52
  615.4 115.7 %fusion.7 = bf16[4096,5120]{1,0:T(8,128)(2,1)} fusion(bf16[4096,5120]{1,0:T(8,128)(2,1)} %convolution_convert_fusion.1, bf16[4096,1280]{1,0:T(8,128)(2,1)} %add_convert_fusion.1, bf16[5120,1280]{1,0:T(8,128)(2,1)} %param.13), kind=kOutput, calls=%fused_computation.19 | convolution fusion | flops 54169436160 | bytes 107479040 | tf_op jit(solution)/shard_map/dot_general | solution.py:53
  731.0 62.9 %convolution_bitcast_fusion = f32[1280,5120]{0,1:T(8,128)} fusion(bf16[4096,5120]{1,0:T(8,128)(2,1)} %fusion.7, bf16[4096,1280]{1,0:T(8,128)(2,1)S(1)} %copy-done.3), kind=kOutput, calls=%fused_computation.37 | convolution fusion | flops 53687091200 | bytes 78643200 | tf_op jit(solution)/shard_map/dot_general | solution.py:55
  796.0 28.6 %reduce-scatter.21.cloned.1.call-done = f32[640,5120]{0,1:T(8,128)} async-done(((f32[1280,5120]{0,1:T(8,128)}), f32[640,5120]{0,1:T(8,128)}) %reduce-scatter.21.cloned.1.call-update) | async-done | bytes 13107216 | tf_op jit(solution)/shard_map/reduce_scatter | solution.py:26
  824.6 13.9 copy.37
  839.0 136.2 %reduce-scatter.33.cloned.1.call-done = f32[1280,1280]{1,0:T(8,128)} async-done(((f32[2560,1280]{1,0:T(8,128)}), f32[1280,1280]{1,0:T(8,128)}) %reduce-scatter.33.cloned.1.call-update) | async-done | bytes 6553616 | tf_op jit(solution)/shard_map/reduce_scatter | solution.py:26
  975.2 149.4 %reduce-scatter.41.cloned.1.call-done = f32[320,5120]{1,0:T(8,128)} async-done(((f32[640,5120]{1,0:T(8,128)}), f32[320,5120]{1,0:T(8,128)}) %reduce-scatter.41.cloned.1.call-update) | async-done | bytes 6553616
  1124.7 149.5 %reduce-scatter.25.cloned.1.call-done = f32[1280,1280]{1,0:T(8,128)} async-done(((f32[2560,1280]{1,0:T(8,128)}), f32[1280,1280]{1,0:T(8,128)}) %reduce-scatter.25.cloned.1.call-update) | async-done | bytes 6553616 | tf_op jit(solution)/shard_map/reduce_scatter | solution.py:26
  1274.3 150.1 %reduce-scatter.37.cloned.1.call-done = f32[320,5120]{1,0:T(8,128)} async-done(((f32[640,5120]{1,0:T(8,128)}), f32[320,5120]{1,0:T(8,128)}) %reduce-scatter.37.cloned.1.call-update) | async-done | bytes 6553616
  1424.5 79.3 %reduce-scatter.35.cloned.1.call-done = f32[640,1280]{1,0:T(8,128)} async-done(((f32[1280,1280]{1,0:T(8,128)}), f32[640,1280]{1,0:T(8,128)}) %reduce-scatter.35.cloned.1.call-update) | async-done | bytes 3276816 | tf_op jit(solution)/shard_map/reduce_scatter | solution.py:26
  1503.8 5.5 subtract_convert_fusion.2
  1512.1 3.0 copy.46
  1515.2 5.4 copy.32
  1520.6 62.5 %reduce-scatter.43.cloned.1.call-done = f32[160,5120]{1,0:T(8,128)} async-done(((f32[320,5120]{1,0:T(8,128)}), f32[160,5120]{1,0:T(8,128)}) %reduce-scatter.43.cloned.1.call-update) | async-done | bytes 3276816
  1583.1 5.4 copy.44
  1588.5 8.5 subtract_convert_fusion
  1597.0 4.1 copy.34
  1601.2 61.3 %reduce-scatter.27.cloned.1.call-done = f32[640,1280]{1,0:T(8,128)} async-done(((f32[1280,1280]{1,0:T(8,128)}), f32[640,1280]{1,0:T(8,128)}) %reduce-scatter.27.cloned.1.call-update) | async-done | bytes 3276816 | tf_op jit(solution)/shard_map/reduce_scatter | solution.py:26
  1662.5 6.4 subtract_convert_fusion.3
  1671.7 3.0 copy.45
  1674.7 5.4 copy.29
  1680.1 61.6 %reduce-scatter.39.cloned.1.call-done = f32[160,5120]{1,0:T(8,128)} async-done(((f32[320,5120]{1,0:T(8,128)}), f32[160,5120]{1,0:T(8,128)}) %reduce-scatter.39.cloned.1.call-update) | async-done | bytes 3276816
  1741.8 5.4 copy.40
  1747.2 8.5 subtract_convert_fusion.1
  1755.7 4.1 copy.30
  1759.8 27.2 %all-gather.31.cloned.1.call-done = bf16[1280,1280]{1,0:T(8,128)(2,1)} async-done(((bf16[640,1280]{1,0:T(8,128)(2,1)}), bf16[1280,1280]{1,0:T(8,128)(2,1)}) %all-gather.31.cloned.1.call-update) | async-done | bytes 3276816 | tf_op jit(solution)/shard_map/all_gather | solution.py:31
  1787.1 45.0 %all-gather.25.cloned.1.call-done = bf16[320,5120]{1,0:T(8,128)(2,1)} async-done(((bf16[160,5120]{1,0:T(8,128)(2,1)}), bf16[320,5120]{1,0:T(8,128)(2,1)}) %all-gather.25.cloned.1.call-update) | async-done | bytes 3276816 | tf_op jit(solution)/shard_map/all_gather | solution.py:31
  1832.1 45.6 %all-gather.19.cloned.1.call-done = bf16[1280,1280]{1,0:T(8,128)(2,1)} async-done(((bf16[640,1280]{1,0:T(8,128)(2,1)}), bf16[1280,1280]{1,0:T(8,128)(2,1)}) %all-gather.19.cloned.1.call-update) | async-done | bytes 3276816 | tf_op jit(solution)/shard_map/all_gather | solution.py:31
  1877.8 45.6 %all-gather.13.cloned.1.call-done = bf16[320,5120]{1,0:T(8,128)(2,1)} async-done(((bf16[160,5120]{1,0:T(8,128)(2,1)}), bf16[320,5120]{1,0:T(8,128)(2,1)}) %all-gather.13.cloned.1.call-update) | async-done | bytes 3276816 | tf_op jit(solution)/shard_map/all_gather | solution.py:31
  1923.4 82.5 %all-gather.33.cloned.1.call-done = bf16[2560,1280]{1,0:T(8,128)(2,1)} async-done(((bf16[1280,1280]{1,0:T(8,128)(2,1)}), bf16[2560,1280]{1,0:T(8,128)(2,1)}) %all-gather.33.cloned.1.call-update) | async-done | bytes 6553616 | tf_op jit(solution)/shard_map/all_gather | solution.py:31
  2006.0 82.6 %all-gather.27.cloned.1.call-done = bf16[640,5120]{1,0:T(8,128)(2,1)} async-done(((bf16[320,5120]{1,0:T(8,128)(2,1)}), bf16[640,5120]{1,0:T(8,128)(2,1)}) %all-gather.27.cloned.1.call-update) | async-done | bytes 6553616 | tf_op jit(solution)/shard_map/all_gather | solution.py:31
  2088.6 82.7 %all-gather.21.cloned.1.call-done = bf16[2560,1280]{1,0:T(8,128)(2,1)} async-done(((bf16[1280,1280]{1,0:T(8,128)(2,1)}), bf16[2560,1280]{1,0:T(8,128)(2,1)}) %all-gather.21.cloned.1.call-update) | async-done | bytes 6553616 | tf_op jit(solution)/shard_map/all_gather | solution.py:31
  2171.6 82.4 %all-gather.15.cloned.1.call-done = bf16[640,5120]{1,0:T(8,128)(2,1)} async-done(((bf16[320,5120]{1,0:T(8,128)(2,1)}), bf16[640,5120]{1,0:T(8,128)(2,1)}) %all-gather.15.cloned.1.call-update) | async-done | bytes 6553616 | tf_op jit(solution)/shard_map/all_gather | solution.py:31
  2254.0 63.5 %add_convert_fusion = bf16[4096,1280]{1,0:T(8,128)(2,1)} fusion(bf16[4096,1280]{1,0:T(8,128)(2,1)} %add_convert_fusion.1, bf16[4096,5120]{1,0:T(8,128)(2,1)} %fusion.7, bf16[1280,5120]{1,0:T(8,128)(2,1)} %param.12), kind=kOutput, calls=%fused_computation.38 | convolution fusion | flops 53702819840 | bytes 76021760 | tf_op jit(solution)/shard_map/dot_general | solution.py:56
  2317.5 5.7 copy.36
  2323.2 5.7 copy.35
  2331.2 26.0 %all-gather.17.cloned.1.call-done = bf16[1280,5120]{1,0:T(8,128)(2,1)} async-done(((bf16[640,5120]{1,0:T(8,128)(2,1)}), bf16[1280,5120]{1,0:T(8,128)(2,1)}) %all-gather.17.cloned.1.call-update) | async-done | bytes 13107216 | tf_op jit(solution)/shard_map/all_gather | solution.py:31
  2357.3 12.7 copy.51
  2370.0 6.6 copy.52
  2379.1 6.6 copy.53
  2387.7 4.9 copy.54
  (84 shorter events, 15.8 us)
Async XLA Ops:
  7.2 786.9 %reduce-scatter.31.cloned.1.call-start = ((), (), s32[]{:S(2)}) async-start(), calls=%async_computation.26 | async-start | bytes 39321600 | tf_op jit(solution)/shard_map/reduce_scatter | solution.py:26
  7.2 63.2 %copy-start.2 = (bf16[5120,1280]{1,0:T(8,128)(2,1)S(1)}, bf16[5120,1280]{1,0:T(8,128)(2,1)}, u32[]{:S(2)}) copy-start(bf16[5120,1280]{1,0:T(8,128)(2,1)} %param.13) | copy-start | bytes 39321604
  297.6 497.1 %reduce-scatter.29.cloned.1.call-start = ((), (), s32[]{:S(2)}) async-start(), calls=%async_computation.22 | async-start | bytes 39321600 | tf_op jit(solution)/shard_map/reduce_scatter | solution.py:26
  297.6 115.7 %copy-start.4 = (bf16[4096,1280]{1,0:T(8,128)(2,1)S(1)}, bf16[4096,1280]{1,0:T(8,128)(2,1)}, u32[]{:S(2)}) copy-start(bf16[4096,1280]{1,0:T(8,128)(2,1)} %add_convert_fusion.2) | copy-start | bytes 31457284
  474.8 320.4 %reduce-scatter.23.cloned.1.call-start = ((), (), s32[]{:S(2)}) async-start(), calls=%async_computation.16 | async-start | bytes 39321600 | tf_op jit(solution)/shard_map/reduce_scatter | solution.py:26
  615.3 209.3 %reduce-scatter.21.cloned.1.call-start = ((), (), s32[]{:S(2)}) async-start(), calls=%async_computation.12 | async-start | bytes 39321600 | tf_op jit(solution)/shard_map/reduce_scatter | solution.py:26
  615.4 115.7 %copy-start.3 = (bf16[4096,1280]{1,0:T(8,128)(2,1)S(1)}, bf16[4096,1280]{1,0:T(8,128)(2,1)}, u32[]{:S(2)}) copy-start(bf16[4096,1280]{1,0:T(8,128)(2,1)} %param.10) | copy-start | bytes 31457284
  794.0 181.2 %reduce-scatter.33.cloned.1.call-start = ((), (), s32[]{:S(2)}) async-start(), calls=%async_computation.27 | async-start | bytes 19660800 | tf_op jit(solution)/shard_map/reduce_scatter | solution.py:26
  794.6 330.0 %reduce-scatter.41.cloned.1.call-start = ((), (), s32[]{:S(2)}) async-start(), calls=%async_computation.34 | async-start | bytes 19660800
  795.2 479.1 %reduce-scatter.25.cloned.1.call-start = ((), (), s32[]{:S(2)}) async-start(), calls=%async_computation.17 | async-start | bytes 19660800 | tf_op jit(solution)/shard_map/reduce_scatter | solution.py:26
  795.9 628.5 %reduce-scatter.37.cloned.1.call-start = ((), (), s32[]{:S(2)}) async-start(), calls=%async_computation.32 | async-start | bytes 19660800
  838.5 665.3 %reduce-scatter.35.cloned.1.call-start = ((), (), s32[]{:S(2)}) async-start(), calls=%async_computation.28 | async-start | bytes 9830400 | tf_op jit(solution)/shard_map/reduce_scatter | solution.py:26
  975.2 528.7 %copy-start.1 = (f32[640,1280]{1,0:T(8,128)S(1)}, f32[640,1280]{1,0:T(8,128)}, u32[]{:S(2)}) copy-start(f32[640,1280]{1,0:T(8,128)} %param.19) | copy-start | bytes 9830404
  975.2 607.9 %reduce-scatter.43.cloned.1.call-start = ((), (), s32[]{:S(2)}) async-start(), calls=%async_computation.35 | async-start | bytes 9830400
  1124.7 537.9 %reduce-scatter.27.cloned.1.call-start = ((), (), s32[]{:S(2)}) async-start(), calls=%async_computation.18 | async-start | bytes 9830400 | tf_op jit(solution)/shard_map/reduce_scatter | solution.py:26
  1274.3 467.5 %reduce-scatter.39.cloned.1.call-start = ((), (), s32[]{:S(2)}) async-start(), calls=%async_computation.33 | async-start | bytes 9830400
  1424.5 362.5 %all-gather.31.cloned.1.call-start = ((), (), s32[]{:S(2)}) async-start(), calls=%async_computation.29 | async-start | bytes 4915200 | tf_op jit(solution)/shard_map/all_gather | solution.py:31
  1509.4 322.7 %all-gather.25.cloned.1.call-start = ((), (), s32[]{:S(2)}) async-start(), calls=%async_computation.23 | async-start | bytes 4915200 | tf_op jit(solution)/shard_map/all_gather | solution.py:31
  1601.1 276.5 %all-gather.19.cloned.1.call-start = ((), (), s32[]{:S(2)}) async-start(), calls=%async_computation.19 | async-start | bytes 4915200 | tf_op jit(solution)/shard_map/all_gather | solution.py:31
  1668.9 254.4 %all-gather.13.cloned.1.call-start = ((), (), s32[]{:S(2)}) async-start(), calls=%async_computation.13 | async-start | bytes 4915200 | tf_op jit(solution)/shard_map/all_gather | solution.py:31
  1759.8 246.2 %all-gather.33.cloned.1.call-start = ((), (), s32[]{:S(2)}) async-start(), calls=%async_computation.30 | async-start | bytes 9830400 | tf_op jit(solution)/shard_map/all_gather | solution.py:31
  1787.0 301.5 %all-gather.27.cloned.1.call-start = ((), (), s32[]{:S(2)}) async-start(), calls=%async_computation.24 | async-start | bytes 9830400 | tf_op jit(solution)/shard_map/all_gather | solution.py:31
  1832.1 339.3 %all-gather.21.cloned.1.call-start = ((), (), s32[]{:S(2)}) async-start(), calls=%async_computation.20 | async-start | bytes 9830400 | tf_op jit(solution)/shard_map/all_gather | solution.py:31
  1877.7 376.2 %all-gather.15.cloned.1.call-start = ((), (), s32[]{:S(2)}) async-start(), calls=%async_computation.14 | async-start | bytes 9830400 | tf_op jit(solution)/shard_map/all_gather | solution.py:31
  1923.3 405.6 %all-gather.35.cloned.1.call-start = ((), (), s32[]{:S(2)}) async-start(), calls=%async_computation.31 | async-start | bytes 19660800 | tf_op jit(solution)/shard_map/all_gather | solution.py:31
  2006.0 323.0 %all-gather.29.cloned.1.call-start = ((), (), s32[]{:S(2)}) async-start(), calls=%async_computation.25 | async-start | bytes 19660800 | tf_op jit(solution)/shard_map/all_gather | solution.py:31
  2088.6 242.7 %all-gather.23.cloned.1.call-start = ((), (), s32[]{:S(2)}) async-start(), calls=%async_computation.21 | async-start | bytes 19660800 | tf_op jit(solution)/shard_map/all_gather | solution.py:31
  2171.4 185.9 %all-gather.17.cloned.1.call-start = ((), (), s32[]{:S(2)}) async-start(), calls=%async_computation.15 | async-start | bytes 19660800 | tf_op jit(solution)/shard_map/all_gather | solution.py:31
  2357.2 12.8 copy-start
  2357.2 19.4 slice-start.4
  2357.2 20.5 slice-start.5
  2370.0 9.0 slice-start.6
  2370.0 9.1 slice-start.7
  2370.0 15.7 slice-start
  2370.0 15.7 slice-start.1
  2379.1 8.6 slice-start.2
  2379.1 8.6 slice-start.3
Sparse Core Ops, SparseCore 0:
  297.7 30.4 reduce-scatter.30
  474.9 30.4 reduce-scatter.28
  615.4 30.4 reduce-scatter.22
  794.1 30.4 reduce-scatter.20
  826.7 148.4 reduce-scatter.32
  977.3 147.3 reduce-scatter.40
  1126.9 147.3 reduce-scatter.24
  1277.1 147.3 reduce-scatter.36
  1426.7 77.0 reduce-scatter.34
  1506.0 77.0 reduce-scatter.42
  1585.4 77.0 reduce-scatter.26
  1664.6 77.0 reduce-scatter.38
  1743.3 43.6 all-gather.30
  1788.4 43.6 all-gather.24
  1834.0 43.6 all-gather.18
  1879.6 43.6 all-gather.12
  1924.7 81.2 all-gather.32
  2007.3 81.2 all-gather.26
  2090.1 81.2 all-gather.20
  2172.7 81.2 all-gather.14
  2255.5 23.4 all-gather.34
  2280.5 24.5 all-gather.28
  2306.6 24.5 all-gather.22
  2332.6 24.5 all-gather.16
where the time goes:
time: 2400 us
  waiting for transfers between devices  1400 us (58%)
  matrix products  850 us (35%)
  local copies, waits for them, and re-layouts  102 us (4%)
  other arithmetic  28.8 us (1%)
    all_gather x12, waiting for transfers between devices, all_gather(): w = lax.all_gather(w, ax, axis=0, tiled=True)  522 us
    reduce_scatter x8, waiting for transfers between devices, reduce_scatter(): s = lax.psum_scatter(s, ax, scatter_dimension=0, tiled=True)  455 us
    unnamed x28, waiting for transfers between devices  426 us
    dot_general x1, matrix products, local(): dh3 = jnp.dot(g, w4.T, preferred_element_type=f32).astype(bf)  116 us
    dot_general x1, matrix products, local(): dh1 = jnp.dot(dh2, w2.T, preferred_element_type=f32).astype(bf)  116 us
    unnamed x39, local copies, waits for them, and re-layouts  88.5 us
    dot_general x1, matrix products, local(): s4 = reduce_scatter(jnp.dot(h3.T, g, preferred_element_type=f32))  86.1 us
    dot_general x1, matrix products, local(): jnp.dot(h1, w2, preferred_element_type=f32) + x.astype(f32)  77.9 us
  transfers between devices with their start and end apart: 24, of which 19 were waited for; matrix products, arithmetic and copies ran while one was open for 27% of the time, Pallas kernels for 0%

commit v1 on v0

v1 whole, which is shorter than its diff:
```python
import functools

import jax
import jax.numpy as jnp
from jax import lax
from jax.experimental import pallas as pl
from jax.experimental.pallas import tpu as pltpu
from jax.sharding import PartitionSpec as P


LR = 0.0005
MU = 0.9
DATA = ("dx", "dy", "dz")
C = 0.7978845608028654
CA = C * 0.044715
SWAP = [(0, 1), (1, 0)]
F32, BF = jnp.float32, jnp.bfloat16
VMEM = 60 * 2**20
NT = (((1,), (1,)), ((), ()))
TN = (((0,), (0,)), ((), ()))


def _tanh(z):
    z2 = z * z
    return z2, jnp.tanh(z * (C + CA * z2))


def _gelu(z):
    hz = 0.5 * z
    return hz + hz * _tanh(z)[1]


def _gelu_grad(z):
    z2, t = _tanh(z)
    return (0.5 + 0.5 * t) + ((1.0 - t * t) * z) * (0.5 * C + (1.5 * CA) * z2)


def _cost(m, k, n):
    return pl.CostEstimate(flops=2 * m * k * n, bytes_accessed=2 * (m * k + k * n + 2 * m * n), transcendentals=0)


def _params(dims):
    return pltpu.CompilerParams(vmem_limit_bytes=VMEM, dimension_semantics=("arbitrary",) * dims)


def _zh_body(sub, x_ref, w_ref, z_ref, h_ref):
    for i in range(x_ref.shape[0] // sub):
        s = pl.ds(i * sub, sub)
        z = jnp.dot(x_ref[s, :], w_ref[...], preferred_element_type=F32).astype(BF)
        z_ref[s, :] = z
        h_ref[s, :] = _gelu(z.astype(F32)).astype(BF)


def zh(x, w, bm=2048, bn=1280, sub=256):
    m, k = x.shape
    n = w.shape[1]
    out = pl.BlockSpec((bm, bn), lambda j, i: (i, j))
    return pl.pallas_call(
        functools.partial(_zh_body, sub), grid=(n // bn, m // bm),
        in_specs=[pl.BlockSpec((bm, k), lambda j, i: (i, 0)), pl.BlockSpec((k, bn), lambda j, i: (0, j))],
        out_specs=[out, out], out_shape=[jax.ShapeDtypeStruct((m, n), BF)] * 2,
        cost_estimate=_cost(m, k, n), compiler_params=_params(2))(x, w)


def _dz_body(sub, g_ref, w_ref, z_ref, o_ref):
    for i in range(g_ref.shape[0] // sub):
        s = pl.ds(i * sub, sub)
        dh = lax.dot_general(g_ref[s, :], w_ref[...], NT, preferred_element_type=F32).astype(BF)
        o_ref[s, :] = (_gelu_grad(z_ref[s, :].astype(F32)) * dh.astype(F32)).astype(BF)


def dz_half(g, w, z, half, bm=1024, bn=1280, sub=256):
    m, k = g.shape
    n = w.shape[0] // 2
    off = half * (n // bn)
    return pl.pallas_call(
        functools.partial(_dz_body, sub), grid=(n // bn, m // bm),
        in_specs=[pl.BlockSpec((bm, k), lambda j, i: (i, 0)),
                  pl.BlockSpec((bn, k), lambda j, i: (j + off, 0)),
                  pl.BlockSpec((bm, bn), lambda j, i: (i, j + off))],
        out_specs=pl.BlockSpec((bm, bn), lambda j, i: (i, j)),
        out_shape=jax.ShapeDtypeStruct((m, n), BF),
        cost_estimate=_cost(m, k, n), compiler_params=_params(2))(g, w, z)


def _back_body(sub, a_ref, b_ref, wa_ref, wb_ref, r_ref, *refs):
    o_ref = refs[-1]
    for i in range(a_ref.shape[0] // sub):
        s = pl.ds(i * sub, sub)
        acc = lax.dot_general(a_ref[s, :], wa_ref[...], NT, preferred_element_type=F32)
        acc += lax.dot_general(b_ref[s, :], wb_ref[...], NT, preferred_element_type=F32)
        o_ref[s, :] = (acc + r_ref[s, :].astype(F32)).astype(BF)


def back(a, b, w, r, pieces=1, piece=0, into=None, bm=512, sub=256):
    m, k = a.shape
    n = w.shape[0]
    steps = m // bm // pieces
    off = piece * steps
    rows = pl.BlockSpec((bm, k), lambda i: (i + off, 0))
    out = pl.BlockSpec((bm, n), lambda i: (i + off, 0))
    extra = [] if into is None else [into]
    return pl.pallas_call(
        functools.partial(_back_body, sub), grid=(steps,),
        in_specs=[rows, rows, pl.BlockSpec((n, k), lambda i: (0, 0)), pl.BlockSpec((n, k), lambda i: (0, 1)), out]
        + [pl.BlockSpec(memory_space=pl.ANY)] * len(extra),
        out_specs=out, out_shape=jax.ShapeDtypeStruct((m, n), BF),
        input_output_aliases={5: 0} if extra else {},
        cost_estimate=_cost(m // pieces, 2 * k, n), compiler_params=_params(1))(a, b, w, w, r, *extra)


def _grad_body(h_ref, a_ref, b_ref, *refs):
    s = lax.dot_general(a_ref[...], b_ref[...], TN, preferred_element_type=F32)
    refs[-1][...] = s if len(refs) == 1 else s + refs[0][...]


def grad(half, a, b, start, cols, bm, bn, recv=None):
    k = a.shape[0]
    rows = a.shape[1] // 2
    tiles = rows // bm
    out = pl.BlockSpec((bm, bn), lambda i, j, h: (i, j))
    specs = [pl.BlockSpec((k, bm), lambda i, j, h: (0, i + h[0] * tiles)),
             pl.BlockSpec((pl.Element(k), pl.Element(bn)), lambda i, j, h: (0, pl.multiple_of(start + j * bn, 128)))]
    args = [half, a, b]
    if recv is not None:
        specs.append(out)
        args.append(recv)
    return pl.pallas_call(
        _grad_body,
        grid_spec=pltpu.PrefetchScalarGridSpec(num_scalar_prefetch=1, grid=(tiles, cols // bn), in_specs=specs,
                                               out_specs=out),
        out_shape=jax.ShapeDtypeStruct((rows, cols), F32),
        cost_estimate=_cost(rows, k, cols), compiler_params=_params(2))(*args)


def _copy_body(*refs):
    refs[-1][...] = refs[0][...]


def copy(w, shape=None, half=0, into=None, steps=8):
    rows, cols = w.shape
    block = pl.BlockSpec((rows // steps, cols), lambda i: (i, 0))
    return pl.pallas_call(
        _copy_body, grid=(steps,),
        in_specs=[block] + ([] if into is None else [pl.BlockSpec(memory_space=pl.ANY)]),
        out_specs=pl.BlockSpec((rows // steps, cols), lambda i: (i, half)),
        out_shape=jax.ShapeDtypeStruct(shape or w.shape, w.dtype),
        input_output_aliases={} if into is None else {1: 0},
        cost_estimate=pl.CostEstimate(flops=rows * cols * 64, bytes_accessed=4 * rows * cols, transcendentals=0),
        compiler_params=_params(1))(w, *([] if into is None else [into]))


class Chunk:
    def __init__(self, s):
        self.j, self.k = lax.axis_index("dy"), lax.axis_index("dz")
        rows, cols = s.shape
        self.size = rows // 8, cols
        self.s = s.reshape(2, 2, 2, rows // 8, cols)
        self.out = self.cut(1 - self.j, 0, 0, (1, 2)), self.cut(0, 1 - self.k, 1, (2, 1))

    def cut(self, j, k, part, n):
        r, c = self.size
        return lax.dynamic_slice(self.s, (j, k, part, 0, 0), (*n, 1, r, c)).reshape(n[0] * n[1], r, c)

    def send(self, stage, vals):
        axes = ("dy", "dz") if stage == 1 else ("dz", "dy")
        self.flight = []
        for v, ax in zip(vals, axes):
            self.flight.append(lax.ppermute(v, ax, SWAP))

    def second(self, vals):
        j, k = self.j, self.k
        self.ra, self.rb = vals
        pick = lax.dynamic_index_in_dim
        self.out = (self.cut(j, 1 - k, 0, (1, 1)) + pick(self.ra, 1 - k, 0),
                    self.cut(1 - j, k, 1, (1, 1)) + pick(self.rb, 1 - j, 0))

    def total(self, vals):
        j, k = self.j, self.k
        pick = lax.dynamic_index_in_dim
        a = self.cut(j, k, 0, (1, 1)) + pick(self.ra, k, 0) + vals[0]
        b = self.cut(j, k, 1, (1, 1)) + pick(self.rb, j, 0) + vals[1]
        return jnp.concatenate([a[0], b[0]], axis=0)


def solution(mesh):
    ndy, ndz = mesh.shape["dy"], mesh.shape["dz"]
    n = mesh.shape["dx"] * ndy * ndz

    def dot(a, b):
        return jnp.dot(a, b, preferred_element_type=F32)

    def local(x, g, w1, w2, w3, w4, m1, m2, m3, m4):
        core = lax.axis_index("dx")
        own = core.astype(jnp.int32).reshape(1)
        other = 1 - own
        tall = dict(a=dict(start=0, cols=512, bm=640, bn=512), b=dict(start=512, cols=768, bm=640, bn=768))
        whole = dict(a=dict(start=0, cols=2560, bm=640, bn=512))
        whole["b"] = whole["a"]

        def gate(*vals):
            return lax.optimization_barrier(vals)

        def send(s):
            return lax.ppermute(s, "dx", SWAP)

        def part(layer, which, a, b, recv=None):
            half, _ = (other, "p") if recv is None else (own, "o")
            sizes = (tall if layer in "24" else whole)[which]
            return grad(half, a, b, **sizes, recv=recv)

        def update(w, m, s, start=0):
            rows, cols = s.shape
            idx = (core * ndy + lax.axis_index("dy")) * ndz + lax.axis_index("dz")
            m_new = MU * lax.slice_in_dim(m, start, start + cols, axis=1) + s / n
            w_loc = lax.dynamic_slice(w, (idx * rows, start), (rows, cols)).astype(F32)
            return (w_loc - LR * m_new).astype(BF), m_new

        def both(ca, cb, vals):
            return jnp.concatenate([ca.total(vals[:2]), cb.total(vals[2:])], axis=1)

        def gather(w):
            return lax.all_gather(w, DATA, axis=0, tiled=True)

        z1, h1 = zh(x, w1)
        h2 = (dot(h1, w2) + x.astype(F32)).astype(BF)
        z3, h3 = zh(h2, w3)

        h3, p = gate(h3, part("4", "a", h3, g))
        d4a = send(p)
        h3, p = gate(h3, part("4", "b", h3, g))
        d4b = send(p)
        c4a = Chunk(part("4", "a", h3, g, d4a))
        h3, *v = gate(h3, *c4a.out)
        c4a.send(1, v)
        c4b = Chunk(part("4", "b", h3, g, d4b))
        g_, *v = gate(g, *c4b.out)
        c4b.send(1, v)
        dza = dz_half(g_, w4, z3, 0)
        dza, *v = gate(dza, *c4a.flight, *c4b.flight)
        c4a.second(v[:2])
        c4b.second(v[2:])
        dza, *v = gate(dza, *c4a.out, *c4b.out)
        c4a.send(2, v[:2])
        c4b.send(2, v[2:])
        g_, p = gate(g_, part("3", "a", h2, dza))
        d3a = send(p)
        dzb = dz_half(g_, w4, z3, 1)
        dzb, *v = gate(dzb, *c4a.flight, *c4b.flight)
        w4l, m4n = update(w4, m4, both(c4a, c4b, v))
        dzb, w4l, m4n = gate(dzb, w4l, m4n)
        w4g = gather(w4l)
        dza, p = gate(dza, part("3", "b", h2, dzb))
        d3b = send(p)
        c3a = Chunk(part("3", "a", h2, dza, d3a))
        dzb, *v = gate(dzb, *c3a.out)
        c3a.send(1, v)
        c3b = Chunk(part("3", "b", h2, dzb, d3b))
        dzb, *v = gate(dzb, *c3b.out)
        c3b.send(1, v)
        dh2 = back(dza, dzb, w3, g)
        dh2, *v = gate(dh2, *c3a.flight, *c3b.flight)
        c3a.second(v[:2])
        c3b.second(v[2:])
        dh2, *v = gate(dh2, *c3a.out, *c3b.out)
        c3a.send(2, v[:2])
        c3b.send(2, v[2:])
        dh2, p = gate(dh2, part("2", "a", h1, dh2))
        d2a = send(p)
        p = part("2", "b", h1, dh2)
        dh2, p, *v = gate(dh2, p, *c3a.flight, *c3b.flight)
        d2b = send(p)
        w3l, m3n = update(w3, m3, both(c3a, c3b, v))
        dh2, w3l, m3n = gate(dh2, w3l, m3n)
        w3g = gather(w3l)
        c2a = Chunk(part("2", "a", h1, dh2, d2a))
        dh2, *v = gate(dh2, *c2a.out)
        c2a.send(1, v)
        c2b = Chunk(part("2", "b", h1, dh2, d2b))
        dh2, *v = gate(dh2, *c2b.out)
        c2b.send(1, v)
        dza = dz_half(dh2, w2, z1, 0)
        p = part("1", "a", x, dza)
        dh2, p, *v = gate(dh2, p, *c2a.flight, *c2b.flight)
        d1a = send(p)
        c2a.second(v[:2])
        c2b.second(v[2:])
        dh2, *v = gate(dh2, *c2a.out, *c2b.out)
        c2a.send(2, v[:2])
        c2b.send(2, v[2:])
        dzb = dz_half(dh2, w2, z1, 1)
        dzb, *v = gate(dzb, *c2a.flight, *c2b.flight)
        w2l, m2n = update(w2, m2, both(c2a, c2b, v))
        dzb, w2l, m2n = gate(dzb, w2l, m2n)
        w2g = gather(w2l)
        dza, p = gate(dza, part("1", "b", x, dzb))
        d1b = send(p)
        c1a = Chunk(part("1", "a", x, dza, d1a))
        dzb, *v = gate(dzb, *c1a.out)
        c1a.send(1, v)
        c1b = Chunk(part("1", "b", x, dzb, d1b))
        dzb, *v = gate(dzb, *c1b.out)
        c1b.send(1, v)
        top = back(dza, dzb, w1, dh2, 2, 0)
        top, *v = gate(top, *c1a.flight)
        c1a.second(v)
        top, *v = gate(top, *c1a.out)
        c1a.send(2, v)
        dx = back(dza, dzb, w1, dh2, 2, 1, top)
        dx, w4g, *v = gate(dx, w4g, *c1b.flight)
        c1b.second(v)
        w4g, *v = gate(w4g, *c1b.out)
        c1b.send(2, v)
        w4g, *v = gate(w4g, *c1a.flight)
        wa, ma = update(w1, m1, c1a.total(v))
        w4g, wa = gate(w4g, wa)
        ga = gather(wa)
        w4n = copy(w4g)
        w4n, w3g, *v = gate(w4n, w3g, *c1b.flight)
        wb, mb = update(w1, m1, c1b.total(v), start=wa.shape[1])
        w3g, wb = gate(w3g, wb)
        gb = gather(wb)
        w3n = copy(w3g)
        w3n, w2g = gate(w3n, w2g)
        w2n = copy(w2g)
        w2n, ga = gate(w2n, ga)
        half = copy(ga, w1.shape, 0)
        half, gb = gate(half, gb)
        w1n = copy(gb, w1.shape, 1, half)
        m1n = jnp.concatenate([ma, mb], axis=1)
        return (dx, w1n, w2n, w3n, w4n, m1n, m2n, m3n, m4n)

    row, rep = P(DATA, None), P()
    return jax.shard_map(local, mesh=mesh,
                         in_specs=(row, row, rep, rep, rep, rep, row, row, row, row),
                         out_specs=(row, rep, rep, rep, rep, row, row, row, row),
                         check_vma=False)
```

time: 2400 us -> 1150 us (0.48)
  waiting for transfers between devices: 1400 us -> 79.4 us
  Pallas kernels: 0 us -> 843 us
  matrix products: 850 us -> 63.2 us
  local copies, waits for them, and re-layouts: 102 us -> 41.9 us
  starting transfers between devices: 1.52 us -> 36.4 us
  other arithmetic: 28.8 us -> 62.7 us
    pallas_call x0 -> x30, Pallas kernels: none -> 843 us  [the longest x16 325 us: grad(): pl.pallas_call(_grad_body, grid_spec=pltpu.PrefetchScalarGridSpec(num_sca...]
    dot_general x11 -> x1, matrix products: 850 us -> 63.2 us  [dot(): return jnp.dot(a, b, preferred_element_type=F32)]
    all_gather x12 -> x5, waiting for transfers between devices: 522 us -> 23.9 us  [gather(): return lax.all_gather(w, DATA, axis=0, tiled=True)]
    reduce_scatter x8 -> x0, waiting for transfers between devices: 455 us -> none  [reduce_scatter(): s = lax.psum_scatter(s, ax, scatter_dimension=0, tiled=True)]
    unnamed x28 -> x5, waiting for transfers between devices: 426 us -> 0.08 us
    unnamed x39 -> x10, local copies, waits for them, and re-layouts: 88.5 us -> 2.58 us
    ppermute x0 -> x40, waiting for transfers between devices: none -> 55.5 us  [the longest x8 39.6 us: send(): return lax.ppermute(s, 'dx', SWAP)]
    reshape x0 -> x16, local copies, waits for them, and re-layouts: none -> 39.3 us  [cut(): lax.dynamic_slice(self.s, (j, k, part, 0, 0), (*n, 1, r, c))]
  transfers between devices with their start and end apart: 24 -> 45, of which waited for: 19 -> 5; matrix products, arithmetic and copies ran while one was open for 27% -> 8% of each run, Pallas kernels for 0% -> 57%
where the time goes in v1:
time: 1150 us; the launch traced here: 1140 us
  Pallas kernels  843 us (73%)
  waiting for transfers between devices  79.4 us (7%)
  matrix products  63.2 us (5%)
  other arithmetic  62.7 us (5%)
  local copies, waits for them, and re-layouts  41.9 us (4%)
  starting transfers between devices  36.4 us (3%)
  between operations  14.6 us (1%)
    pallas_call x16, Pallas kernels, grad(): pl.pallas_call(_grad_body, grid_spec=pltpu.PrefetchScalarGridSpec(num_sca...  325 us
    pallas_call x4, Pallas kernels, dz_half(): pl.pallas_call(functools.partial(_dz_body, sub), grid=(n // bn, m // bm),...  180 us
    pallas_call x2, Pallas kernels, zh(): pl.pallas_call(functools.partial(_zh_body, sub), grid=(n // bn, m // bm),...  149 us
    pallas_call x3, Pallas kernels, back(): pl.pallas_call(functools.partial(_back_body, sub), grid=(steps,), in_spec...  137 us
    dot_general x1, matrix products, dot(): return jnp.dot(a, b, preferred_element_type=F32)  63.2 us
    pallas_call x5, Pallas kernels, copy(): pl.pallas_call(_copy_body, grid=(steps,), in_specs=[block] + ([] if into...  51.2 us
    ppermute x8, waiting for transfers between devices, send(): return lax.ppermute(s, 'dx', SWAP)  39.6 us
    reshape x16, local copies, waits for them, and re-layouts, cut(): lax.dynamic_slice(self.s, (j, k, part, 0, 0), (*n, 1, r, c))  39.3 us
  transfers between devices with their start and end apart: 45, of which 5 were waited for; matrix products, arithmetic and copies ran while one was open for 8% of the time, Pallas kernels for 57%

profile of v1, /device:TPU:0, one launch (start us, length us, event | category | flops | bytes accessed | tf_op | source)
XLA Modules:
  0.0 1140.9 jit_solution(12978892485193373776)
XLA Ops:
  7.2 74.4 %shard_map.169 = (bf16[4096,5120]{1,0:T(8,128)(2,1)}, bf16[4096,5120]{1,0:T(8,128)(2,1)}) custom-call(bf16[4096,1280]{1,0:T(8,128)(2,1)} %a_ref.7, bf16[1280,5120]{1,0:T(8,128)(2,1)} %wb_ref.5), custom_call_target="tpu_custom_call" | custom-call | flops 53687091200 | bytes 107479040 | tf_op jit(solution)/shard_map/pallas_call | solution.py:58
  81.7 63.2 %add_convert_fusion.x_ref.a_ref = bf16[4096,1280]{1,0:T(8,128)(2,1)} fusion(bf16[4096,1280]{1,0:T(8,128)(2,1)} %a_ref.7, bf16[4096,5120]{1,0:T(8,128)(2,1)} %get-tuple-element.135.a_ref, bf16[5120,1280]{1,0:T(8,128)(2,1)} %w_ref.11), kind=kOutput, calls=%fused_computation | convolution fusion | flops 53702819840 | bytes 76021760 | tf_op jit(solution)/shard_map/dot_general | solution.py:191
  144.8 74.8 %shard_map.170 = (bf16[4096,5120]{1,0:T(8,128)(2,1)}, bf16[4096,5120]{1,0:T(8,128)(2,1)}) custom-call(bf16[4096,1280]{1,0:T(8,128)(2,1)} %add_convert_fusion.x_ref.a_ref, bf16[1280,5120]{1,0:T(8,128)(2,1)} %wb_ref.3), custom_call_target="tpu_custom_call" | custom-call | flops 53687091200 | bytes 107479040 | tf_op jit(solution)/shard_map/pallas_call | solution.py:58
  219.7 16.6 %shard_map.171 = f32[2560,512]{1,0:T(8,128)} custom-call(s32[1]{0:T(128)S(6)} %sub.16.h_ref, bf16[4096,5120]{1,0:T(8,128)(2,1)} %get-tuple-element.140.a_ref, bf16[4096,1280]{1,0:T(8,128)(2,1)} %r_ref.1), custom_call_target="tpu_custom_call" | custom-call | flops 10737418240 | bytes 30408704 | tf_op jit(solution)/shard_map/pallas_call | solution.py:128
  236.3 23.0 %shard_map.172 = f32[2560,768]{1,0:T(8,128)} custom-call(s32[1]{0:T(128)S(6)} %sub.16.h_ref, bf16[4096,5120]{1,0:T(8,128)(2,1)} %get-tuple-element.140.a_ref, bf16[4096,1280]{1,0:T(8,128)(2,1)} %r_ref.1), custom_call_target="tpu_custom_call" | custom-call | flops 16106127360 | bytes 35127296 | tf_op jit(solution)/shard_map/pallas_call | solution.py:128
  259.9 19.9 %collective-permute-done.refs_0_ = f32[2560,512]{1,0:T(8,128)} collective-permute-done((f32[2560,512]{1,0:T(8,128)}, f32[2560,512]{1,0:T(8,128)}, u32[]{:S(2)}, u32[]{:S(2)}) %collective-permute-start) | collective-permute-done | bytes 5242912 | tf_op jit(solution)/shard_map/ppermute | solution.py:205
  279.8 17.5 %shard_map.173 = f32[2560,512]{1,0:T(8,128)} custom-call(s32[1]{0:T(128)} %bitcast.h_ref, bf16[4096,5120]{1,0:T(8,128)(2,1)} %get-tuple-element.140.a_ref, bf16[4096,1280]{1,0:T(8,128)(2,1)} %r_ref.1, f32[2560,512]{1,0:T(8,128)} %collective-permute-done.refs_0_), custom_call_target="tpu_custom_call" | custom-call | flops 10737418240 | bytes 30408704 | tf_op jit(solution)/shard_map/pallas_call | solution.py:128
  302.2 3.1 collective-permute-start.2
  307.2 23.5 %shard_map.174 = f32[2560,768]{1,0:T(8,128)} custom-call(s32[1]{0:T(128)} %bitcast.h_ref, bf16[4096,5120]{1,0:T(8,128)(2,1)} %get-tuple-element.140.a_ref, bf16[4096,1280]{1,0:T(8,128)(2,1)} %r_ref.1, f32[2560,768]{1,0:T(8,128)} %collective-permute-done.1.refs_0_), custom_call_target="tpu_custom_call" | custom-call | flops 16106127360 | bytes 35127296 | tf_op jit(solution)/shard_map/pallas_call | solution.py:128
  330.7 2.9 dynamic-slice_bitcast_fusion.2
  333.7 2.9 dynamic-slice_bitcast_fusion.3
  337.2 44.8 %shard_map.175.b_ref.a_ref = bf16[4096,2560]{1,0:T(8,128)(2,1)} custom-call(bf16[4096,1280]{1,0:T(8,128)(2,1)} %r_ref.1, bf16[5120,1280]{1,0:T(8,128)(2,1)} %w_ref.9, bf16[4096,5120]{1,0:T(8,128)(2,1)} %get-tuple-element.143.z_ref), custom_call_target="tpu_custom_call" | custom-call | flops 26843545600 | bytes 58982400 | tf_op jit(solution)/shard_map/pallas_call | solution.py:76
  382.0 3.0 bitcast_add_fusion.30
  385.1 3.0 bitcast_add_fusion.6
  392.1 19.8 %shard_map.176 = f32[640,2560]{1,0:T(8,128)} custom-call(s32[1]{0:T(128)S(6)} %sub.16.h_ref, bf16[4096,1280]{1,0:T(8,128)(2,1)} %add_convert_fusion.x_ref.a_ref, bf16[4096,2560]{1,0:T(8,128)(2,1)} %shard_map.175.b_ref.a_ref), custom_call_target="tpu_custom_call" | custom-call | flops 13421772800 | bytes 32768000 | tf_op jit(solution)/shard_map/pallas_call | solution.py:128
  411.9 44.9 %shard_map.177.b_ref = bf16[4096,2560]{1,0:T(8,128)(2,1)} custom-call(bf16[4096,1280]{1,0:T(8,128)(2,1)} %r_ref.1, bf16[5120,1280]{1,0:T(8,128)(2,1)} %w_ref.9, bf16[4096,5120]{1,0:T(8,128)(2,1)} %get-tuple-element.143.z_ref), custom_call_target="tpu_custom_call" | custom-call | flops 26843545600 | bytes 58982400 | tf_op jit(solution)/shard_map/pallas_call | solution.py:76
  462.5 4.6 subtract_convert_fusion.2
  467.1 19.9 %shard_map.178 = f32[640,2560]{1,0:T(8,128)} custom-call(s32[1]{0:T(128)S(6)} %sub.16.h_ref, bf16[4096,1280]{1,0:T(8,128)(2,1)} %add_convert_fusion.x_ref.a_ref, bf16[4096,2560]{1,0:T(8,128)(2,1)} %shard_map.177.b_ref), custom_call_target="tpu_custom_call" | custom-call | flops 13421772800 | bytes 32768000 | tf_op jit(solution)/shard_map/pallas_call | solution.py:128
  487.5 21.7 %shard_map.179 = f32[640,2560]{1,0:T(8,128)} custom-call(s32[1]{0:T(128)} %bitcast.h_ref, bf16[4096,1280]{1,0:T(8,128)(2,1)} %add_convert_fusion.x_ref.a_ref, bf16[4096,2560]{1,0:T(8,128)(2,1)} %shard_map.175.b_ref.a_ref, f32[640,2560]{1,0:T(8,128)} %collective-permute-done.10.refs_0_), custom_call_target="tpu_custom_call" | custom-call | flops 13421772800 | bytes 32768000 | tf_op jit(solution)/shard_map/pallas_call | solution.py:128
  515.8 20.1 %shard_map.180 = f32[640,2560]{1,0:T(8,128)} custom-call(s32[1]{0:T(128)} %bitcast.h_ref, bf16[4096,1280]{1,0:T(8,128)(2,1)} %add_convert_fusion.x_ref.a_ref, bf16[4096,2560]{1,0:T(8,128)(2,1)} %shard_map.177.b_ref, f32[640,2560]{1,0:T(8,128)} %collective-permute-done.11.refs_0_), custom_call_target="tpu_custom_call" | custom-call | flops 13421772800 | bytes 32768000 | tf_op jit(solution)/shard_map/pallas_call | solution.py:128
  542.1 64.4 %shard_map.181.b_ref.g_ref.r_ref = bf16[4096,1280]{1,0:T(8,128)(2,1)} custom-call(bf16[4096,2560]{1,0:T(8,128)(2,1)} %shard_map.175.b_ref.a_ref, bf16[4096,2560]{1,0:T(8,128)(2,1)} %shard_map.177.b_ref, bf16[1280,5120]{1,0:T(8,128)(2,1)} %wb_ref.3, bf16[1280,5120]{1,0:T(8,128)(2,1)} %wb_ref.3, bf16[4096,1280]{1,0:T(8,128)(2,1)} %r_ref.1), custom_call_target="tpu_custom_call" | custom-call | flops 53687091200 | bytes 76021760 | tf_op jit(solution)/shard_map/pallas_call | solution.py:103
  606.5 4.4 bitcast_add_fusion.20
  614.9 16.9 %shard_map.182 = f32[2560,512]{1,0:T(8,128)} custom-call(s32[1]{0:T(128)S(6)} %sub.16.h_ref, bf16[4096,5120]{1,0:T(8,128)(2,1)} %get-tuple-element.135.a_ref, bf16[4096,1280]{1,0:T(8,128)(2,1)} %shard_map.181.b_ref.g_ref.r_ref), custom_call_target="tpu_custom_call" | custom-call | flops 10737418240 | bytes 30408704 | tf_op jit(solution)/shard_map/pallas_call | solution.py:128
  631.9 22.8 %shard_map.183 = f32[2560,768]{1,0:T(8,128)} custom-call(s32[1]{0:T(128)S(6)} %sub.16.h_ref, bf16[4096,5120]{1,0:T(8,128)(2,1)} %get-tuple-element.135.a_ref, bf16[4096,1280]{1,0:T(8,128)(2,1)} %shard_map.181.b_ref.g_ref.r_ref), custom_call_target="tpu_custom_call" | custom-call | flops 16106127360 | bytes 35127296 | tf_op jit(solution)/shard_map/pallas_call | solution.py:128
  659.8 4.5 subtract_convert_fusion.1
  664.9 19.7 %collective-permute-done.20.refs_0_ = f32[2560,512]{1,0:T(8,128)} collective-permute-done((f32[2560,512]{1,0:T(8,128)}, f32[2560,512]{1,0:T(8,128)}, u32[]{:S(2)}, u32[]{:S(2)}) %collective-permute-start.20) | collective-permute-done | bytes 5242912 | tf_op jit(solution)/shard_map/ppermute | solution.py:205
  684.7 19.1 %shard_map.184 = f32[2560,512]{1,0:T(8,128)} custom-call(s32[1]{0:T(128)} %bitcast.h_ref, bf16[4096,5120]{1,0:T(8,128)(2,1)} %get-tuple-element.135.a_ref, bf16[4096,1280]{1,0:T(8,128)(2,1)} %shard_map.181.b_ref.g_ref.r_ref, f32[2560,512]{1,0:T(8,128)} %collective-permute-done.20.refs_0_), custom_call_target="tpu_custom_call" | custom-call | flops 10737418240 | bytes 30408704 | tf_op jit(solution)/shard_map/pallas_call | solution.py:128
  712.0 23.4 %shard_map.185 = f32[2560,768]{1,0:T(8,128)} custom-call(s32[1]{0:T(128)} %bitcast.h_ref, bf16[4096,5120]{1,0:T(8,128)(2,1)} %get-tuple-element.135.a_ref, bf16[4096,1280]{1,0:T(8,128)(2,1)} %shard_map.181.b_ref.g_ref.r_ref, f32[2560,768]{1,0:T(8,128)} %collective-permute-done.21.refs_0_), custom_call_target="tpu_custom_call" | custom-call | flops 16106127360 | bytes 35127296 | tf_op jit(solution)/shard_map/pallas_call | solution.py:128
  735.4 3.0 dynamic-slice_bitcast_fusion
  742.3 44.9 %shard_map.186.b_ref.a_ref = bf16[4096,2560]{1,0:T(8,128)(2,1)} custom-call(bf16[4096,1280]{1,0:T(8,128)(2,1)} %shard_map.181.b_ref.g_ref.r_ref, bf16[5120,1280]{1,0:T(8,128)(2,1)} %w_ref.11, bf16[4096,5120]{1,0:T(8,128)(2,1)} %get-tuple-element.195.z_ref), custom_call_target="tpu_custom_call" | custom-call | flops 26843545600 | bytes 58982400 | tf_op jit(solution)/shard_map/pallas_call | solution.py:76
  787.3 19.6 %shard_map.187 = f32[640,2560]{1,0:T(8,128)} custom-call(s32[1]{0:T(128)S(6)} %sub.16.h_ref, bf16[4096,1280]{1,0:T(8,128)(2,1)} %a_ref.7, bf16[4096,2560]{1,0:T(8,128)(2,1)} %shard_map.186.b_ref.a_ref), custom_call_target="tpu_custom_call" | custom-call | flops 13421772800 | bytes 32768000 | tf_op jit(solution)/shard_map/pallas_call | solution.py:128
  806.9 3.0 bitcast_add_fusion.26
  809.9 3.0 bitcast_add_fusion.2
  817.0 44.9 %shard_map.188.b_ref = bf16[4096,2560]{1,0:T(8,128)(2,1)} custom-call(bf16[4096,1280]{1,0:T(8,128)(2,1)} %shard_map.181.b_ref.g_ref.r_ref, bf16[5120,1280]{1,0:T(8,128)(2,1)} %w_ref.11, bf16[4096,5120]{1,0:T(8,128)(2,1)} %get-tuple-element.195.z_ref), custom_call_target="tpu_custom_call" | custom-call | flops 26843545600 | bytes 58982400 | tf_op jit(solution)/shard_map/pallas_call | solution.py:76
  867.5 4.5 subtract_convert_fusion
  872.1 19.9 %shard_map.189 = f32[640,2560]{1,0:T(8,128)} custom-call(s32[1]{0:T(128)S(6)} %sub.16.h_ref, bf16[4096,1280]{1,0:T(8,128)(2,1)} %a_ref.7, bf16[4096,2560]{1,0:T(8,128)(2,1)} %shard_map.188.b_ref), custom_call_target="tpu_custom_call" | custom-call | flops 13421772800 | bytes 32768000 | tf_op jit(solution)/shard_map/pallas_call | solution.py:128
  892.4 21.2 %shard_map.190 = f32[640,2560]{1,0:T(8,128)} custom-call(s32[1]{0:T(128)} %bitcast.h_ref, bf16[4096,1280]{1,0:T(8,128)(2,1)} %a_ref.7, bf16[4096,2560]{1,0:T(8,128)(2,1)} %shard_map.186.b_ref.a_ref, f32[640,2560]{1,0:T(8,128)} %collective-permute-done.30.refs_0_), custom_call_target="tpu_custom_call" | custom-call | flops 13421772800 | bytes 32768000 | tf_op jit(solution)/shard_map/pallas_call | solution.py:128
  922.5 20.3 %shard_map.191 = f32[640,2560]{1,0:T(8,128)} custom-call(s32[1]{0:T(128)} %bitcast.h_ref, bf16[4096,1280]{1,0:T(8,128)(2,1)} %a_ref.7, bf16[4096,2560]{1,0:T(8,128)(2,1)} %shard_map.188.b_ref, f32[640,2560]{1,0:T(8,128)} %collective-permute-done.31.refs_0_), custom_call_target="tpu_custom_call" | custom-call | flops 13421772800 | bytes 32768000 | tf_op jit(solution)/shard_map/pallas_call | solution.py:128
  946.8 36.4 %shard_map.192.refs_0_ = bf16[4096,1280]{1,0:T(8,128)(2,1)} custom-call(bf16[4096,2560]{1,0:T(8,128)(2,1)} %shard_map.186.b_ref.a_ref, bf16[4096,2560]{1,0:T(8,128)(2,1)} %shard_map.188.b_ref, bf16[1280,5120]{1,0:T(8,128)(2,1)} %wb_ref.5, bf16[1280,5120]{1,0:T(8,128)(2,1)} %wb_ref.5, bf16[4096,1280]{1,0:T(8,128)(2,1)} %shard_map.181.b_ref.g_ref.r_ref), custom_call_target="tpu_custom_call" | custom-call | flops 26843545600 | bytes 44564480 | tf_op jit(solution)/shard_map/pallas_call | solution.py:103
  983.2 3.2 bitcast_add_fusion.14
  989.6 36.6 %shard_map.193 = bf16[4096,1280]{1,0:T(8,128)(2,1)} custom-call(bf16[4096,2560]{1,0:T(8,128)(2,1)} %shard_map.186.b_ref.a_ref, bf16[4096,2560]{1,0:T(8,128)(2,1)} %shard_map.188.b_ref, bf16[1280,5120]{1,0:T(8,128)(2,1)} %wb_ref.5, bf16[1280,5120]{1,0:T(8,128)(2,1)} %wb_ref.5, ...), custom_call_target="tpu_custom_call", output_to_operand_aliasing={{}: (5, {})} | custom-call | flops 26843545600 | bytes 44564480 | tf_op jit(solution)/shard_map/pallas_call | solution.py:103
  1035.2 11.8 %shard_map.194 = bf16[5120,1280]{1,0:T(8,128)(2,1)} custom-call(bf16[5120,1280]{1,0:T(8,128)(2,1)} %all-gather.6.cloned.1.call-done.refs_0_), custom_call_target="tpu_custom_call" | custom-call | flops 419430400 | bytes 26214400 | tf_op jit(solution)/shard_map/pallas_call | solution.py:143
  1047.0 14.9 %collective-permute-done.38 = f32[1,80,2560]{2,1,0:T(8,128)} collective-permute-done((f32[1,80,2560]{2,1,0:T(8,128)S(1)}, f32[1,80,2560]{2,1,0:T(8,128)}, u32[]{:S(2)}, u32[]{:S(2)}) %collective-permute-start.38) | collective-permute-done | bytes 819232 | tf_op jit(solution)/shard_map/ppermute | solution.py:169
  1068.7 11.8 %shard_map.195 = bf16[1280,5120]{1,0:T(8,128)(2,1)} custom-call(bf16[1280,5120]{1,0:T(8,128)(2,1)} %all-gather.8.cloned.1.call-done.refs_0_), custom_call_target="tpu_custom_call" | custom-call | flops 419430400 | bytes 26214400 | tf_op jit(solution)/shard_map/pallas_call | solution.py:143
  1082.4 11.8 %shard_map.196 = bf16[5120,1280]{1,0:T(8,128)(2,1)} custom-call(bf16[5120,1280]{1,0:T(8,128)(2,1)} %all-gather.10.cloned.1.call-done.refs_0_), custom_call_target="tpu_custom_call" | custom-call | flops 419430400 | bytes 26214400 | tf_op jit(solution)/shard_map/pallas_call | solution.py:143
  1094.2 7.9 shard_map.197.refs_1_
  1102.2 23.9 %all-gather.14.cloned.1.call-done.refs_0_ = bf16[1280,2560]{1,0:T(8,128)(2,1)} async-done(((bf16[160,2560]{1,0:T(8,128)(2,1)}), bf16[1280,2560]{1,0:T(8,128)(2,1)}) %all-gather.14.cloned.1.call-update) | async-done | bytes 6553616 | tf_op jit(solution)/shard_map/all_gather | solution.py:223
  1126.0 7.9 shard_map.198
  (125 shorter events, 96.8 us)
Async XLA Ops:
  7.2 1019.0 %all-gather.6.cloned.1.call-start = ((), (), s32[]{:S(2)}) async-start(), calls=%async_computation | async-start | bytes 14745600 | tf_op jit(solution)/shard_map/all_gather | solution.py:223
  259.3 47.9 %collective-permute-start.1 = (f32[2560,768]{1,0:T(8,128)}, f32[2560,768]{1,0:T(8,128)}, u32[]{:S(2)}, u32[]{:S(2)}) collective-permute-start(f32[2560,768]{1,0:T(8,128)} %shard_map.172), channel_id=1, source_target_pairs={{0,1},{1,0},{2,3},{3,2},{4,5},{5,4},{6,7},{7,6}} | collective-permute-start | bytes 23592968 | tf_op jit(solution)/shard_map/ppermute | solution.py:205
  259.9 19.9 %collective-permute-start = (f32[2560,512]{1,0:T(8,128)}, f32[2560,512]{1,0:T(8,128)}, u32[]{:S(2)}, u32[]{:S(2)}) collective-permute-start(f32[2560,512]{1,0:T(8,128)} %shard_map.171), channel_id=1, source_target_pairs={{0,1},{1,0},{2,3},{3,2},{4,5},{5,4},{6,7},{7,6}} | collective-permute-start | bytes 15728648 | tf_op jit(solution)/shard_map/ppermute | solution.py:205
  302.2 79.8 %collective-permute-start.2 = (f32[2,320,512]{2,1,0:T(8,128)}, f32[2,320,512]{2,1,0:T(8,128)}, u32[]{:S(2)}, u32[]{:S(2)}) collective-permute-start(f32[2,320,512]{2,1,0:T(8,128)} %dynamic-slice_bitcast_fusion.15), channel_id=1, source_target_pairs={{0,2},{2,0},{1,3},{3,1},{4,6},{6,4},{5,7},{7,5}} | collective-permute-start | bytes 3932168 | tf_op jit(solution)/shard_map/ppermute | solution.py:169
  305.3 76.7 %collective-permute-start.3 = (f32[2,320,512]{2,1,0:T(8,128)}, f32[2,320,512]{2,1,0:T(8,128)}, u32[]{:S(2)}, u32[]{:S(2)}) collective-permute-start(f32[2,320,512]{2,1,0:T(8,128)} %dynamic-slice_bitcast_fusion.14), channel_id=1, source_target_pairs={{0,4},{4,0},{1,5},{5,1},{2,6},{6,2},{3,7},{7,3}} | collective-permute-start | bytes 3932168 | tf_op jit(solution)/shard_map/ppermute | solution.py:169
  336.6 45.4 %collective-permute-start.4 = (f32[2,320,768]{2,1,0:T(8,128)}, f32[2,320,768]{2,1,0:T(8,128)S(1)}, u32[]{:S(2)}, u32[]{:S(2)}) collective-permute-start(f32[2,320,768]{2,1,0:T(8,128)} %dynamic-slice_bitcast_fusion.3), channel_id=1, source_target_pairs={{0,2},{2,0},{1,3},{3,1},{4,6},{6,4},{5,7},{7,5}} | collective-permute-start | bytes 5898248 | tf_op jit(solution)/shard_map/ppermute | solution.py:169
  337.2 44.9 %collective-permute-start.5 = (f32[2,320,768]{2,1,0:T(8,128)}, f32[2,320,768]{2,1,0:T(8,128)S(1)}, u32[]{:S(2)}, u32[]{:S(2)}) collective-permute-start(f32[2,320,768]{2,1,0:T(8,128)} %dynamic-slice_bitcast_fusion.2), channel_id=1, source_target_pairs={{0,4},{4,0},{1,5},{5,1},{2,6},{6,2},{3,7},{7,3}} | collective-permute-start | bytes 5898248 | tf_op jit(solution)/shard_map/ppermute | solution.py:169
  388.1 68.8 %collective-permute-start.6 = (f32[1,320,512]{2,1,0:T(8,128)}, f32[1,320,512]{2,1,0:T(8,128)}, u32[]{:S(2)}, u32[]{:S(2)}) collective-permute-start(f32[1,320,512]{2,1,0:T(8,128)} %get-tuple-element.155), channel_id=1, source_target_pairs={{0,4},{4,0},{1,5},{5,1},{2,6},{6,2},{3,7},{7,3}} | collective-permute-start | bytes 1966088 | tf_op jit(solution)/shard_map/ppermute | solution.py:169
  390.1 66.8 %collective-permute-start.7 = (f32[1,320,512]{2,1,0:T(8,128)}, f32[1,320,512]{2,1,0:T(8,128)}, u32[]{:S(2)}, u32[]{:S(2)}) collective-permute-start(f32[1,320,512]{2,1,0:T(8,128)} %get-tuple-element.156), channel_id=1, source_target_pairs={{0,2},{2,0},{1,3},{3,1},{4,6},{6,4},{5,7},{7,5}} | collective-permute-start | bytes 1966088 | tf_op jit(solution)/shard_map/ppermute | solution.py:169
  391.5 65.3 %collective-permute-start.8 = (f32[1,320,768]{2,1,0:T(8,128)}, f32[1,320,768]{2,1,0:T(8,128)}, u32[]{:S(2)}, u32[]{:S(2)}) collective-permute-start(f32[1,320,768]{2,1,0:T(8,128)} %get-tuple-element.157), channel_id=1, source_target_pairs={{0,4},{4,0},{1,5},{5,1},{2,6},{6,2},{3,7},{7,3}} | collective-permute-start | bytes 2949128 | tf_op jit(solution)/shard_map/ppermute | solution.py:169
  391.7 65.2 %collective-permute-start.9 = (f32[1,320,768]{2,1,0:T(8,128)}, f32[1,320,768]{2,1,0:T(8,128)}, u32[]{:S(2)}, u32[]{:S(2)}) collective-permute-start(f32[1,320,768]{2,1,0:T(8,128)} %get-tuple-element.158), channel_id=1, source_target_pairs={{0,2},{2,0},{1,3},{3,1},{4,6},{6,4},{5,7},{7,5}} | collective-permute-start | bytes 2949128 | tf_op jit(solution)/shard_map/ppermute | solution.py:169
  459.4 3.1 copy-start
  467.1 595.7 %all-gather.8.cloned.1.call-start = ((), (), s32[]{:S(2)}) async-start(), calls=%async_computation.1 | async-start | bytes 14745600 | tf_op jit(solution)/shard_map/all_gather | solution.py:223
  467.1 20.4 %collective-permute-start.10 = (f32[640,2560]{1,0:T(8,128)}, f32[640,2560]{1,0:T(8,128)}, u32[]{:S(2)}, u32[]{:S(2)}) collective-permute-start(f32[640,2560]{1,0:T(8,128)} %shard_map.176), channel_id=1, source_target_pairs={{0,1},{1,0},{2,3},{3,2},{4,5},{5,4},{6,7},{7,6}} | collective-permute-start | bytes 19660808 | tf_op jit(solution)/shard_map/ppermute | solution.py:205
  487.1 28.7 %collective-permute-start.11 = (f32[640,2560]{1,0:T(8,128)}, f32[640,2560]{1,0:T(8,128)}, u32[]{:S(2)}, u32[]{:S(2)}) collective-permute-start(f32[640,2560]{1,0:T(8,128)} %shard_map.178), channel_id=1, source_target_pairs={{0,1},{1,0},{2,3},{3,2},{4,5},{5,4},{6,7},{7,6}} | collective-permute-start | bytes 19660808 | tf_op jit(solution)/shard_map/ppermute | solution.py:205
  512.5 93.9 %collective-permute-start.12 = (f32[2,80,2560]{2,1,0:T(8,128)S(1)}, f32[2,80,2560]{2,1,0:T(8,128)}, u32[]{:S(2)}, u32[]{:S(2)}) collective-permute-start(f32[2,80,2560]{2,1,0:T(8,128)S(1)} %dynamic-slice_bitcast_fusion.11), channel_id=1, source_target_pairs={{0,2},{2,0},{1,3},{3,1},{4,6},{6,4},{5,7},{7,5}} | collective-permute-start | bytes 4915208 | tf_op jit(solution)/shard_map/ppermute | solution.py:169
  514.2 92.3 %collective-permute-start.13 = (f32[2,80,2560]{2,1,0:T(8,128)S(1)}, f32[2,80,2560]{2,1,0:T(8,128)}, u32[]{:S(2)}, u32[]{:S(2)}) collective-permute-start(f32[2,80,2560]{2,1,0:T(8,128)S(1)} %dynamic-slice_bitcast_fusion.10), channel_id=1, source_target_pairs={{0,4},{4,0},{1,5},{5,1},{2,6},{6,2},{3,7},{7,3}} | collective-permute-start | bytes 4915208 | tf_op jit(solution)/shard_map/ppermute | solution.py:169
  541.3 65.2 %collective-permute-start.14 = (f32[2,80,2560]{2,1,0:T(8,128)}, f32[2,80,2560]{2,1,0:T(8,128)}, u32[]{:S(2)}, u32[]{:S(2)}) collective-permute-start(f32[2,80,2560]{2,1,0:T(8,128)} %dynamic-slice_bitcast_fusion.9), channel_id=1, source_target_pairs={{0,2},{2,0},{1,3},{3,1},{4,6},{6,4},{5,7},{7,5}} | collective-permute-start | bytes 4915208 | tf_op jit(solution)/shard_map/ppermute | solution.py:169
  542.0 64.5 %collective-permute-start.15 = (f32[2,80,2560]{2,1,0:T(8,128)}, f32[2,80,2560]{2,1,0:T(8,128)}, u32[]{:S(2)}, u32[]{:S(2)}) collective-permute-start(f32[2,80,2560]{2,1,0:T(8,128)} %dynamic-slice_bitcast_fusion.8), channel_id=1, source_target_pairs={{0,4},{4,0},{1,5},{5,1},{2,6},{6,2},{3,7},{7,3}} | collective-permute-start | bytes 4915208 | tf_op jit(solution)/shard_map/ppermute | solution.py:169
  610.9 43.7 %collective-permute-start.16 = (f32[1,80,2560]{2,1,0:T(8,128)}, f32[1,80,2560]{2,1,0:T(8,128)S(1)}, u32[]{:S(2)}, u32[]{:S(2)}) collective-permute-start(f32[1,80,2560]{2,1,0:T(8,128)} %get-tuple-element.181), channel_id=1, source_target_pairs={{0,4},{4,0},{1,5},{5,1},{2,6},{6,2},{3,7},{7,3}} | collective-permute-start | bytes 2457608 | tf_op jit(solution)/shard_map/ppermute | solution.py:169
  612.8 41.9 %collective-permute-start.17 = (f32[1,80,2560]{2,1,0:T(8,128)}, f32[1,80,2560]{2,1,0:T(8,128)S(1)}, u32[]{:S(2)}, u32[]{:S(2)}) collective-permute-start(f32[1,80,2560]{2,1,0:T(8,128)} %get-tuple-element.182), channel_id=1, source_target_pairs={{0,2},{2,0},{1,3},{3,1},{4,6},{6,4},{5,7},{7,5}} | collective-permute-start | bytes 2457608 | tf_op jit(solution)/shard_map/ppermute | solution.py:169
  614.1 40.5 %collective-permute-start.18 = (f32[1,80,2560]{2,1,0:T(8,128)}, f32[1,80,2560]{2,1,0:T(8,128)S(1)}, u32[]{:S(2)}, u32[]{:S(2)}) collective-permute-start(f32[1,80,2560]{2,1,0:T(8,128)} %get-tuple-element.183), channel_id=1, source_target_pairs={{0,4},{4,0},{1,5},{5,1},{2,6},{6,2},{3,7},{7,3}} | collective-permute-start | bytes 2457608 | tf_op jit(solution)/shard_map/ppermute | solution.py:169
  614.8 39.9 %collective-permute-start.19 = (f32[1,80,2560]{2,1,0:T(8,128)S(1)}, f32[1,80,2560]{2,1,0:T(8,128)S(1)}, u32[]{:S(2)}, u32[]{:S(2)}) collective-permute-start(f32[1,80,2560]{2,1,0:T(8,128)S(1)} %get-tuple-element.184), channel_id=1, source_target_pairs={{0,2},{2,0},{1,3},{3,1},{4,6},{6,4},{5,7},{7,5}} | collective-permute-start | bytes 2457608 | tf_op jit(solution)/shard_map/ppermute | solution.py:169
  664.3 418.1 %all-gather.10.cloned.1.call-start = ((), (), s32[]{:S(2)}) async-start(), calls=%async_computation.2 | async-start | bytes 14745600 | tf_op jit(solution)/shard_map/all_gather | solution.py:223
  664.4 47.6 %collective-permute-start.21 = (f32[2560,768]{1,0:T(8,128)}, f32[2560,768]{1,0:T(8,128)}, u32[]{:S(2)}, u32[]{:S(2)}) collective-permute-start(f32[2560,768]{1,0:T(8,128)} %shard_map.183), channel_id=1, source_target_pairs={{0,1},{1,0},{2,3},{3,2},{4,5},{5,4},{6,7},{7,6}} | collective-permute-start | bytes 23592968 | tf_op jit(solution)/shard_map/ppermute | solution.py:205
  664.4 20.2 %collective-permute-start.20 = (f32[2560,512]{1,0:T(8,128)}, f32[2560,512]{1,0:T(8,128)}, u32[]{:S(2)}, u32[]{:S(2)}) collective-permute-start(f32[2560,512]{1,0:T(8,128)} %shard_map.182), channel_id=1, source_target_pairs={{0,1},{1,0},{2,3},{3,2},{4,5},{5,4},{6,7},{7,6}} | collective-permute-start | bytes 15728648 | tf_op jit(solution)/shard_map/ppermute | solution.py:205
  708.9 97.9 %collective-permute-start.22 = (f32[2,320,512]{2,1,0:T(8,128)}, f32[2,320,512]{2,1,0:T(8,128)}, u32[]{:S(2)}, u32[]{:S(2)}) collective-permute-start(f32[2,320,512]{2,1,0:T(8,128)} %dynamic-slice_bitcast_fusion.13), channel_id=1, source_target_pairs={{0,2},{2,0},{1,3},{3,1},{4,6},{6,4},{5,7},{7,5}} | collective-permute-start | bytes 3932168 | tf_op jit(solution)/shard_map/ppermute | solution.py:169
  710.7 96.2 %collective-permute-start.23 = (f32[2,320,512]{2,1,0:T(8,128)}, f32[2,320,512]{2,1,0:T(8,128)}, u32[]{:S(2)}, u32[]{:S(2)}) collective-permute-start(f32[2,320,512]{2,1,0:T(8,128)} %dynamic-slice_bitcast_fusion.12), channel_id=1, source_target_pairs={{0,4},{4,0},{1,5},{5,1},{2,6},{6,2},{3,7},{7,3}} | collective-permute-start | bytes 3932168 | tf_op jit(solution)/shard_map/ppermute | solution.py:169
  741.3 65.5 %collective-permute-start.24 = (f32[2,320,768]{2,1,0:T(8,128)}, f32[2,320,768]{2,1,0:T(8,128)S(1)}, u32[]{:S(2)}, u32[]{:S(2)}) collective-permute-start(f32[2,320,768]{2,1,0:T(8,128)} %dynamic-slice_bitcast_fusion.1), channel_id=1, source_target_pairs={{0,2},{2,0},{1,3},{3,1},{4,6},{6,4},{5,7},{7,5}} | collective-permute-start | bytes 5898248 | tf_op jit(solution)/shard_map/ppermute | solution.py:169
  742.0 64.8 %collective-permute-start.25 = (f32[2,320,768]{2,1,0:T(8,128)}, f32[2,320,768]{2,1,0:T(8,128)S(1)}, u32[]{:S(2)}, u32[]{:S(2)}) collective-permute-start(f32[2,320,768]{2,1,0:T(8,128)} %dynamic-slice_bitcast_fusion), channel_id=1, source_target_pairs={{0,4},{4,0},{1,5},{5,1},{2,6},{6,2},{3,7},{7,3}} | collective-permute-start | bytes 5898248 | tf_op jit(solution)/shard_map/ppermute | solution.py:169
  812.9 48.9 %collective-permute-start.26 = (f32[1,320,512]{2,1,0:T(8,128)}, f32[1,320,512]{2,1,0:T(8,128)}, u32[]{:S(2)}, u32[]{:S(2)}) collective-permute-start(f32[1,320,512]{2,1,0:T(8,128)} %get-tuple-element.206), channel_id=1, source_target_pairs={{0,4},{4,0},{1,5},{5,1},{2,6},{6,2},{3,7},{7,3}} | collective-permute-start | bytes 1966088 | tf_op jit(solution)/shard_map/ppermute | solution.py:169
  814.6 47.2 %collective-permute-start.27 = (f32[1,320,512]{2,1,0:T(8,128)}, f32[1,320,512]{2,1,0:T(8,128)}, u32[]{:S(2)}, u32[]{:S(2)}) collective-permute-start(f32[1,320,512]{2,1,0:T(8,128)} %get-tuple-element.207), channel_id=1, source_target_pairs={{0,2},{2,0},{1,3},{3,1},{4,6},{6,4},{5,7},{7,5}} | collective-permute-start | bytes 1966088 | tf_op jit(solution)/shard_map/ppermute | solution.py:169
  815.9 45.9 %collective-permute-start.28 = (f32[1,320,768]{2,1,0:T(8,128)}, f32[1,320,768]{2,1,0:T(8,128)}, u32[]{:S(2)}, u32[]{:S(2)}) collective-permute-start(f32[1,320,768]{2,1,0:T(8,128)} %get-tuple-element.208), channel_id=1, source_target_pairs={{0,4},{4,0},{1,5},{5,1},{2,6},{6,2},{3,7},{7,3}} | collective-permute-start | bytes 2949128 | tf_op jit(solution)/shard_map/ppermute | solution.py:169
  816.8 45.1 %collective-permute-start.29 = (f32[1,320,768]{2,1,0:T(8,128)}, f32[1,320,768]{2,1,0:T(8,128)}, u32[]{:S(2)}, u32[]{:S(2)}) collective-permute-start(f32[1,320,768]{2,1,0:T(8,128)} %get-tuple-element.209), channel_id=1, source_target_pairs={{0,2},{2,0},{1,3},{3,1},{4,6},{6,4},{5,7},{7,5}} | collective-permute-start | bytes 2949128 | tf_op jit(solution)/shard_map/ppermute | solution.py:169
  872.0 222.2 %all-gather.12.cloned.1.call-start = ((), (), s32[]{:S(2)}) async-start(), calls=%async_computation.3 | async-start | bytes 7372800 | tf_op jit(solution)/shard_map/all_gather | solution.py:223
  872.1 20.4 %collective-permute-start.30 = (f32[640,2560]{1,0:T(8,128)}, f32[640,2560]{1,0:T(8,128)}, u32[]{:S(2)}, u32[]{:S(2)}) collective-permute-start(f32[640,2560]{1,0:T(8,128)} %shard_map.187), channel_id=1, source_target_pairs={{0,1},{1,0},{2,3},{3,2},{4,5},{5,4},{6,7},{7,6}} | collective-permute-start | bytes 19660808 | tf_op jit(solution)/shard_map/ppermute | solution.py:205
  892.0 30.5 %collective-permute-start.31 = (f32[640,2560]{1,0:T(8,128)}, f32[640,2560]{1,0:T(8,128)}, u32[]{:S(2)}, u32[]{:S(2)}) collective-permute-start(f32[640,2560]{1,0:T(8,128)} %shard_map.189), channel_id=1, source_target_pairs={{0,1},{1,0},{2,3},{3,2},{4,5},{5,4},{6,7},{7,6}} | collective-permute-start | bytes 19660808 | tf_op jit(solution)/shard_map/ppermute | solution.py:205
  919.2 64.0 %collective-permute-start.32 = (f32[2,80,2560]{2,1,0:T(8,128)}, f32[2,80,2560]{2,1,0:T(8,128)}, u32[]{:S(2)}, u32[]{:S(2)}) collective-permute-start(f32[2,80,2560]{2,1,0:T(8,128)} %dynamic-slice_bitcast_fusion.7), channel_id=1, source_target_pairs={{0,2},{2,0},{1,3},{3,1},{4,6},{6,4},{5,7},{7,5}} | collective-permute-start | bytes 4915208 | tf_op jit(solution)/shard_map/ppermute | solution.py:169
  921.0 62.3 %collective-permute-start.33 = (f32[2,80,2560]{2,1,0:T(8,128)}, f32[2,80,2560]{2,1,0:T(8,128)}, u32[]{:S(2)}, u32[]{:S(2)}) collective-permute-start(f32[2,80,2560]{2,1,0:T(8,128)} %dynamic-slice_bitcast_fusion.6), channel_id=1, source_target_pairs={{0,4},{4,0},{1,5},{5,1},{2,6},{6,2},{3,7},{7,3}} | collective-permute-start | bytes 4915208 | tf_op jit(solution)/shard_map/ppermute | solution.py:169
  945.9 80.3 %collective-permute-start.34 = (f32[2,80,2560]{2,1,0:T(8,128)S(1)}, f32[2,80,2560]{2,1,0:T(8,128)}, u32[]{:S(2)}, u32[]{:S(2)}) collective-permute-start(f32[2,80,2560]{2,1,0:T(8,128)S(1)} %dynamic-slice_bitcast_fusion.5), channel_id=1, source_target_pairs={{0,2},{2,0},{1,3},{3,1},{4,6},{6,4},{5,7},{7,5}} | collective-permute-start | bytes 4915208 | tf_op jit(solution)/shard_map/ppermute | solution.py:169
  946.5 79.7 %collective-permute-start.35 = (f32[2,80,2560]{2,1,0:T(8,128)S(1)}, f32[2,80,2560]{2,1,0:T(8,128)}, u32[]{:S(2)}, u32[]{:S(2)}) collective-permute-start(f32[2,80,2560]{2,1,0:T(8,128)S(1)} %dynamic-slice_bitcast_fusion.4), channel_id=1, source_target_pairs={{0,4},{4,0},{1,5},{5,1},{2,6},{6,2},{3,7},{7,3}} | collective-permute-start | bytes 4915208 | tf_op jit(solution)/shard_map/ppermute | solution.py:169
  986.5 41.8 %collective-permute-start.36 = (f32[1,80,2560]{2,1,0:T(8,128)}, f32[1,80,2560]{2,1,0:T(8,128)}, u32[]{:S(2)}, u32[]{:S(2)}) collective-permute-start(f32[1,80,2560]{2,1,0:T(8,128)} %get-tuple-element.235), channel_id=1, source_target_pairs={{0,4},{4,0},{1,5},{5,1},{2,6},{6,2},{3,7},{7,3}} | collective-permute-start | bytes 2457608 | tf_op jit(solution)/shard_map/ppermute | solution.py:169
  988.3 40.1 %collective-permute-start.37 = (f32[1,80,2560]{2,1,0:T(8,128)}, f32[1,80,2560]{2,1,0:T(8,128)}, u32[]{:S(2)}, u32[]{:S(2)}) collective-permute-start(f32[1,80,2560]{2,1,0:T(8,128)} %get-tuple-element.236), channel_id=1, source_target_pairs={{0,2},{2,0},{1,3},{3,1},{4,6},{6,4},{5,7},{7,5}} | collective-permute-start | bytes 2457608 | tf_op jit(solution)/shard_map/ppermute | solution.py:169
  1028.3 3.4 copy-start.3
  1034.2 91.9 %all-gather.14.cloned.1.call-start = ((), (), s32[]{:S(2)}) async-start(), calls=%async_computation.4 | async-start | bytes 7372800 | tf_op jit(solution)/shard_map/all_gather | solution.py:223
  1034.2 27.7 %collective-permute-start.38 = (f32[1,80,2560]{2,1,0:T(8,128)S(1)}, f32[1,80,2560]{2,1,0:T(8,128)}, u32[]{:S(2)}, u32[]{:S(2)}) collective-permute-start(f32[1,80,2560]{2,1,0:T(8,128)S(1)} %get-tuple-element.242), channel_id=1, source_target_pairs={{0,4},{4,0},{1,5},{5,1},{2,6},{6,2},{3,7},{7,3}} | collective-permute-start | bytes 2457608 | tf_op jit(solution)/shard_map/ppermute | solution.py:169
  1034.8 28.0 %collective-permute-start.39 = (f32[1,80,2560]{2,1,0:T(8,128)S(1)}, f32[1,80,2560]{2,1,0:T(8,128)}, u32[]{:S(2)}, u32[]{:S(2)}) collective-permute-start(f32[1,80,2560]{2,1,0:T(8,128)S(1)} %get-tuple-element.243), channel_id=1, source_target_pairs={{0,2},{2,0},{1,3},{3,1},{4,6},{6,4},{5,7},{7,5}} | collective-permute-start | bytes 2457608 | tf_op jit(solution)/shard_map/ppermute | solution.py:169
  1062.8 3.4 copy-start.4
  (2 other events, 6.0 us)
Sparse Core Ops, SparseCore 0:
  467.2 89.4 all-gather.5
  664.5 89.4 all-gather.7
  872.1 86.2 all-gather.9
  1034.3 49.0 all-gather.11
  1085.0 40.9 all-gather.13

commit v2 on v1

--- a/solution.py
+++ b/solution.py
@@ -15,7 +15,7 @@
 CA = C * 0.044715
 SWAP = [(0, 1), (1, 0)]
 F32, BF = jnp.float32, jnp.bfloat16
-VMEM = 60 * 2**20
+CUTS = (pl.ds(0, 768), pl.ds(768, 512))
 NT = (((1,), (1,)), ((), ()))
 TN = (((0,), (0,)), ((), ()))
 
@@ -39,16 +39,17 @@
     return pl.CostEstimate(flops=2 * m * k * n, bytes_accessed=2 * (m * k + k * n + 2 * m * n), transcendentals=0)
 
 
-def _params(dims):
-    return pltpu.CompilerParams(vmem_limit_bytes=VMEM, dimension_semantics=("arbitrary",) * dims)
+def _params(dims, mib=60):
+    return pltpu.CompilerParams(vmem_limit_bytes=mib * 2**20, dimension_semantics=("arbitrary",) * dims)
 
 
 def _zh_body(sub, x_ref, w_ref, z_ref, h_ref):
     for i in range(x_ref.shape[0] // sub):
         s = pl.ds(i * sub, sub)
-        z = jnp.dot(x_ref[s, :], w_ref[...], preferred_element_type=F32).astype(BF)
-        z_ref[s, :] = z
-        h_ref[s, :] = _gelu(z.astype(F32)).astype(BF)
+        for c in CUTS:
+            z = jnp.dot(x_ref[s, :], w_ref[:, c], preferred_element_type=F32).astype(BF)
+            z_ref[s, c] = z
+            h_ref[s, c] = _gelu(z.astype(F32)).astype(BF)
 
 
 def zh(x, w, bm=2048, bn=1280, sub=256):
@@ -59,14 +60,15 @@
         functools.partial(_zh_body, sub), grid=(n // bn, m // bm),
         in_specs=[pl.BlockSpec((bm, k), lambda j, i: (i, 0)), pl.BlockSpec((k, bn), lambda j, i: (0, j))],
         out_specs=[out, out], out_shape=[jax.ShapeDtypeStruct((m, n), BF)] * 2,
-        cost_estimate=_cost(m, k, n), compiler_params=_params(2))(x, w)
+        cost_estimate=_cost(m, k, n), compiler_params=_params(2, 44))(x, w)
 
 
 def _dz_body(sub, g_ref, w_ref, z_ref, o_ref):
     for i in range(g_ref.shape[0] // sub):
         s = pl.ds(i * sub, sub)
-        dh = lax.dot_general(g_ref[s, :], w_ref[...], NT, preferred_element_type=F32).astype(BF)
-        o_ref[s, :] = (_gelu_grad(z_ref[s, :].astype(F32)) * dh.astype(F32)).astype(BF)
+        for c in CUTS:
+            dh = lax.dot_general(g_ref[s, :], w_ref[c, :], NT, preferred_element_type=F32).astype(BF)
+            o_ref[s, c] = (_gelu_grad(z_ref[s, c].astype(F32)) * dh.astype(F32)).astype(BF)
 
 
 def dz_half(g, w, z, half, bm=1024, bn=1280, sub=256):
@@ -109,28 +111,55 @@
         cost_estimate=_cost(m // pieces, 2 * k, n), compiler_params=_params(1))(a, b, w, w, r, *extra)
 
 
-def _grad_body(h_ref, a_ref, b_ref, *refs):
+def _grad_body(at_ref, a_ref, b_ref, *refs):
     s = lax.dot_general(a_ref[...], b_ref[...], TN, preferred_element_type=F32)
-    refs[-1][...] = s if len(refs) == 1 else s + refs[0][...]
-
-
-def grad(half, a, b, start, cols, bm, bn, recv=None):
+    if len(refs) == 1:
+        refs[0][...] = s
+        return
+    r_ref, o_ref, first_ref, second_ref = refs
+    o_ref[...] = s + r_ref[...]
+    part = first_ref.shape[1]
+    far_j, far_k = 1 - at_ref[1], 1 - at_ref[2]
+    if first_ref.shape[0] == 2:
+        for i in range(2):
+            first_ref[i] = o_ref[pl.ds(pl.multiple_of((far_j * 2 + i) * 2 * part, 8), part), :]
+            second_ref[i] = o_ref[pl.ds(pl.multiple_of((i * 2 + far_k) * 2 * part + part, 8), part), :]
+    else:
+        i = pl.program_id(0)
+
+        @pl.when(i // 2 == far_j)
+        def _():
+            first_ref[0] = o_ref[:part, :]
+
+        @pl.when(i % 2 == far_k)
+        def _():
+            second_ref[0] = o_ref[part:, :]
+
+
+def grad(at, a, b, start, cols, bm, bn, mib, recv=None):
     k = a.shape[0]
     rows = a.shape[1] // 2
     tiles = rows // bm
-    out = pl.BlockSpec((bm, bn), lambda i, j, h: (i, j))
-    specs = [pl.BlockSpec((k, bm), lambda i, j, h: (0, i + h[0] * tiles)),
-             pl.BlockSpec((pl.Element(k), pl.Element(bn)), lambda i, j, h: (0, pl.multiple_of(start + j * bn, 128)))]
-    args = [half, a, b]
+    out = pl.BlockSpec((bm, bn), lambda i, j, t: (i, j))
+    shape = jax.ShapeDtypeStruct((rows, cols), F32)
+    specs = [pl.BlockSpec((k, bm), lambda i, j, t: (0, i + t[0] * tiles)),
+             pl.BlockSpec((pl.Element(k), pl.Element(bn)), lambda i, j, t: (0, pl.multiple_of(start + j * bn, 128)))]
+    args = [at, a, b]
     if recv is not None:
         specs.append(out)
         args.append(recv)
+        if tiles == 1:
+            one = two = pl.BlockSpec((2, rows // 8, bn), lambda i, j, t: (0, 0, j))
+        else:
+            one = pl.BlockSpec((1, rows // 8, bn), lambda i, j, t: (jnp.clip(i - 2 * (1 - t[1]), 0, 1), 0, j))
+            two = pl.BlockSpec((1, rows // 8, bn), lambda i, j, t: (i // 2, 0, j))
+        out = [out, one, two]
+        shape = [shape] + [jax.ShapeDtypeStruct((2, rows // 8, cols), F32)] * 2
     return pl.pallas_call(
         _grad_body,
         grid_spec=pltpu.PrefetchScalarGridSpec(num_scalar_prefetch=1, grid=(tiles, cols // bn), in_specs=specs,
                                                out_specs=out),
-        out_shape=jax.ShapeDtypeStruct((rows, cols), F32),
-        cost_estimate=_cost(rows, k, cols), compiler_params=_params(2))(*args)
+        out_shape=shape, cost_estimate=_cost(rows, k, cols), compiler_params=_params(2, mib))(*args)
 
 
 def _copy_body(*refs):
@@ -151,12 +180,12 @@
 
 
 class Chunk:
-    def __init__(self, s):
+    def __init__(self, parts):
+        s, *self.out = parts
         self.j, self.k = lax.axis_index("dy"), lax.axis_index("dz")
         rows, cols = s.shape
         self.size = rows // 8, cols
         self.s = s.reshape(2, 2, 2, rows // 8, cols)
-        self.out = self.cut(1 - self.j, 0, 0, (1, 2)), self.cut(0, 1 - self.k, 1, (2, 1))
 
     def cut(self, j, k, part, n):
         r, c = self.size
@@ -192,8 +221,9 @@
 
     def local(x, g, w1, w2, w3, w4, m1, m2, m3, m4):
         core = lax.axis_index("dx")
-        own = core.astype(jnp.int32).reshape(1)
-        other = 1 - own
+        spot = [core, lax.axis_index("dy"), lax.axis_index("dz")]
+        own = jnp.stack(spot).astype(jnp.int32)
+        other = jnp.stack([1 - core, *spot[1:]]).astype(jnp.int32)
         tall = dict(a=dict(start=0, cols=512, bm=640, bn=512), b=dict(start=512, cols=768, bm=640, bn=768))
         whole = dict(a=dict(start=0, cols=2560, bm=640, bn=512))
         whole["b"] = whole["a"]
@@ -207,7 +237,7 @@
         def part(layer, which, a, b, recv=None):
             half, _ = (other, "p") if recv is None else (own, "o")
             sizes = (tall if layer in "24" else whole)[which]
-            return grad(half, a, b, **sizes, recv=recv)
+            return grad(half, a, b, **sizes, mib=38 if layer == "4" else 60, recv=recv)
 
         def update(w, m, s, start=0):
             rows, cols = s.shape
@@ -236,20 +266,22 @@
         c4b = Chunk(part("4", "b", h3, g, d4b))
         g_, *v = gate(g, *c4b.out)
         c4b.send(1, v)
+        g_, *v = gate(g_, *c4a.flight)
+        c4a.second(v)
+        g_, *v = gate(g_, *c4a.out)
+        c4a.send(2, v)
         dza = dz_half(g_, w4, z3, 0)
-        dza, *v = gate(dza, *c4a.flight, *c4b.flight)
-        c4a.second(v[:2])
-        c4b.second(v[2:])
-        dza, *v = gate(dza, *c4a.out, *c4b.out)
-        c4a.send(2, v[:2])
-        c4b.send(2, v[2:])
+        dza, *v = gate(dza, *c4b.flight)
+        c4b.second(v)
+        dza, *v = gate(dza, *c4b.out)
+        c4b.send(2, v)
         g_, p = gate(g_, part("3", "a", h2, dza))
         d3a = send(p)
+        g_, *v = gate(g_, *c4a.flight, *c4b.flight)
+        w4l, m4n = update(w4, m4, both(c4a, c4b, v))
+        g_, w4l, m4n = gate(g_, w4l, m4n)
+        w4g = gather(w4l)
         dzb = dz_half(g_, w4, z3, 1)
-        dzb, *v = gate(dzb, *c4a.flight, *c4b.flight)
-        w4l, m4n = update(w4, m4, both(c4a, c4b, v))
-        dzb, w4l, m4n = gate(dzb, w4l, m4n)
-        w4g = gather(w4l)
         dza, p = gate(dza, part("3", "b", h2, dzb))
         d3b = send(p)
         c3a = Chunk(part("3", "a", h2, dza, d3a))
@@ -258,21 +290,24 @@
         c3b = Chunk(part("3", "b", h2, dzb, d3b))
         dzb, *v = gate(dzb, *c3b.out)
         c3b.send(1, v)
-        dh2 = back(dza, dzb, w3, g)
-        dh2, *v = gate(dh2, *c3a.flight, *c3b.flight)
-        c3a.second(v[:2])
-        c3b.second(v[2:])
-        dh2, *v = gate(dh2, *c3a.out, *c3b.out)
-        c3a.send(2, v[:2])
-        c3b.send(2, v[2:])
+        top = back(dza, dzb, w3, g, 2, 0)
+        top, *v = gate(top, *c3a.flight)
+        c3a.second(v)
+        top, *v = gate(top, *c3a.out)
+        c3a.send(2, v)
+        dh2 = back(dza, dzb, w3, g, 2, 1, top)
+        dh2, *v = gate(dh2, *c3b.flight)
+        c3b.second(v)
+        dh2, *v = gate(dh2, *c3b.out)
+        c3b.send(2, v)
         dh2, p = gate(dh2, part("2", "a", h1, dh2))
         d2a = send(p)
-        p = part("2", "b", h1, dh2)
-        dh2, p, *v = gate(dh2, p, *c3a.flight, *c3b.flight)
-        d2b = send(p)
+        dh2, *v = gate(dh2, *c3a.flight, *c3b.flight)
         w3l, m3n = update(w3, m3, both(c3a, c3b, v))
         dh2, w3l, m3n = gate(dh2, w3l, m3n)
         w3g = gather(w3l)
+        dh2, p = gate(dh2, part("2", "b", h1, dh2))
+        d2b = send(p)
         c2a = Chunk(part("2", "a", h1, dh2, d2a))
         dh2, *v = gate(dh2, *c2a.out)
         c2a.send(1, v)
@@ -293,37 +328,38 @@
         w2l, m2n = update(w2, m2, both(c2a, c2b, v))
         dzb, w2l, m2n = gate(dzb, w2l, m2n)
         w2g = gather(w2l)
-        dza, p = gate(dza, part("1", "b", x, dzb))
-        d1b = send(p)
         c1a = Chunk(part("1", "a", x, dza, d1a))
         dzb, *v = gate(dzb, *c1a.out)
         c1a.send(1, v)
+        dza, w4g, p = gate(dza, w4g, part("1", "b", x, dzb))
+        d1b = send(p)
+        w4n = copy(w4g)
+        dzb, d1b, w4n = gate(dzb, d1b, w4n)
         c1b = Chunk(part("1", "b", x, dzb, d1b))
         dzb, *v = gate(dzb, *c1b.out)
         c1b.send(1, v)
+        dzb, *v = gate(dzb, *c1a.flight)
+        c1a.second(v)
+        dzb, *v = gate(dzb, *c1a.out)
+        c1a.send(2, v)
         top = back(dza, dzb, w1, dh2, 2, 0)
         top, *v = gate(top, *c1a.flight)
-        c1a.second(v)
-        top, *v = gate(top, *c1a.out)
-        c1a.send(2, v)
-        dx = back(dza, dzb, w1, dh2, 2, 1, top)
-        dx, w4g, *v = gate(dx, w4g, *c1b.flight)
+        wa, ma = update(w1, m1, c1a.total(v))
+        top, wa = gate(top, wa)
+        ga = gather(wa)
+        top, w3g, *v = gate(top, w3g, *c1b.flight)
         c1b.second(v)
-        w4g, *v = gate(w4g, *c1b.out)
+        top, w3g, *v = gate(top, w3g, *c1b.out)
         c1b.send(2, v)
-        w4g, *v = gate(w4g, *c1a.flight)
-        wa, ma = update(w1, m1, c1a.total(v))
-        w4g, wa = gate(w4g, wa)
-        ga = gather(wa)
-        w4n = copy(w4g)
-        w4n, w3g, *v = gate(w4n, w3g, *c1b.flight)
-        wb, mb = update(w1, m1, c1b.total(v), start=wa.shape[1])
-        w3g, wb = gate(w3g, wb)
-        gb = gather(wb)
         w3n = copy(w3g)
         w3n, w2g = gate(w3n, w2g)
         w2n = copy(w2g)
-        w2n, ga = gate(w2n, ga)
+        top, w2n, *v = gate(top, w2n, *c1b.flight)
+        wb, mb = update(w1, m1, c1b.total(v), start=wa.shape[1])
+        top, wb = gate(top, wb)
+        gb = gather(wb)
+        dx = back(dza, dzb, w1, dh2, 2, 1, top)
+        dx, ga = gate(dx, ga)
         half = copy(ga, w1.shape, 0)
         half, gb = gate(half, gb)
         w1n = copy(gb, w1.shape, 1, half)

time: 1150 us -> 1180 us (1.026)
  waiting for transfers between devices: 79.4 us -> 140 us
  local copies, waits for them, and re-layouts: 41.9 us -> 5.34 us
  Pallas kernels: 843 us -> 858 us
    ppermute x32, waiting for transfers between devices: 15.9 us -> 83.5 us  [send(): self.flight.append(lax.ppermute(v, ax, SWAP))]
    reshape x16 -> x0, local copies, waits for them, and re-layouts: 39.3 us -> none  [cut(): lax.dynamic_slice(self.s, (j, k, part, 0, 0), (*n, 1, r, c))]
    all_gather x5, waiting for transfers between devices: 23.9 us -> 0.01 us  [gather(): return lax.all_gather(w, DATA, axis=0, tiled=True)]
    ppermute x8, waiting for transfers between devices: 39.6 us -> 56.8 us  [send(): return lax.ppermute(s, 'dx', SWAP)]
    pallas_call x3 -> x4, Pallas kernels: 137 us -> 146 us  [back(): pl.pallas_call(functools.partial(_back_body, sub), grid=(steps,), in_spec...]
  transfers between devices with their start and end apart: 45 -> 45, of which waited for: 5 -> 11; matrix products, arithmetic and copies ran while one was open for 8% -> 4% of each run, Pallas kernels for 57% -> 56%
where the time goes in v2:
time: 1180 us
  Pallas kernels  858 us (73%)
  waiting for transfers between devices  140 us (12%)
  other arithmetic  62.4 us (5%)
  matrix products  59.7 us (5%)
  starting transfers between devices  37.1 us (3%)
  between operations  14.3 us (1%)
    pallas_call x16, Pallas kernels, grad(): pl.pallas_call(_grad_body, grid_spec=pltpu.PrefetchScalarGridSpec(num_sca...  332 us
    pallas_call x4, Pallas kernels, dz_half(): pl.pallas_call(functools.partial(_dz_body, sub), grid=(n // bn, m // bm),...  180 us
    pallas_call x2, Pallas kernels, zh(): pl.pallas_call(functools.partial(_zh_body, sub), grid=(n // bn, m // bm),...  149 us
    pallas_call x4, Pallas kernels, back(): pl.pallas_call(functools.partial(_back_body, sub), grid=(steps,), in_spec...  146 us
    ppermute x32, waiting for transfers between devices, send(): self.flight.append(lax.ppermute(v, ax, SWAP))  83.5 us
    dot_general x1, matrix products, dot(): return jnp.dot(a, b, preferred_element_type=F32)  59.7 us
    ppermute x8, waiting for transfers between devices, send(): return lax.ppermute(s, 'dx', SWAP)  56.8 us
    pallas_call x5, Pallas kernels, copy(): pl.pallas_call(_copy_body, grid=(steps,), in_specs=[block] + ([] if into...  50.9 us
  transfers between devices with their start and end apart: 45, of which 11 were waited for; matrix products, arithmetic and copies ran while one was open for 4% of the time, Pallas kernels for 56%

profile of v2, /device:TPU:0, one launch (start us, length us, event | category | flops | bytes accessed | tf_op | source)
XLA Modules:
  0.0 1177.7 jit_solution(17324205915144663382)
XLA Ops:
  7.2 74.0 %shard_map.169 = (bf16[4096,5120]{1,0:T(8,128)(2,1)}, bf16[4096,5120]{1,0:T(8,128)(2,1)}) custom-call(bf16[4096,1280]{1,0:T(8,128)(2,1)} %a_ref.7, bf16[1280,5120]{1,0:T(8,128)(2,1)} %wb_ref.7), custom_call_target="tpu_custom_call" | custom-call | flops 53687091200 | bytes 107479040 | tf_op jit(solution)/shard_map/pallas_call | solution.py:59
  81.3 59.7 %add_convert_fusion.x_ref.a_ref = bf16[4096,1280]{1,0:T(8,128)(2,1)} fusion(bf16[4096,1280]{1,0:T(8,128)(2,1)} %a_ref.7, bf16[4096,5120]{1,0:T(8,128)(2,1)} %get-tuple-element.169.a_ref, bf16[5120,1280]{1,0:T(8,128)(2,1)S(1)} %copy-done.13), kind=kOutput, calls=%fused_computation | convolution fusion | flops 53702819840 | bytes 76021760 | tf_op jit(solution)/shard_map/dot_general | solution.py:220
  141.0 74.7 %shard_map.170 = (bf16[4096,5120]{1,0:T(8,128)(2,1)}, bf16[4096,5120]{1,0:T(8,128)(2,1)}) custom-call(bf16[4096,1280]{1,0:T(8,128)(2,1)} %add_convert_fusion.x_ref.a_ref, bf16[1280,5120]{1,0:T(8,128)(2,1)} %wb_ref.5), custom_call_target="tpu_custom_call" | custom-call | flops 53687091200 | bytes 107479040 | tf_op jit(solution)/shard_map/pallas_call | solution.py:59
  215.8 15.8 %shard_map.171 = f32[2560,512]{1,0:T(8,128)} custom-call(s32[3]{0:T(128)S(1)} %add_add_fusion.1.at_ref, bf16[4096,5120]{1,0:T(8,128)(2,1)} %get-tuple-element.176.a_ref, bf16[4096,1280]{1,0:T(8,128)(2,1)S(1)} %copy-done), custom_call_target="tpu_custom_call" | custom-call | flops 10737418240 | bytes 30408704 | tf_op jit(solution)/shard_map/pallas_call | solution.py:158
  231.6 23.5 %shard_map.172 = f32[2560,768]{1,0:T(8,128)} custom-call(s32[3]{0:T(128)S(1)} %add_add_fusion.1.at_ref, bf16[4096,5120]{1,0:T(8,128)(2,1)} %get-tuple-element.176.a_ref, bf16[4096,1280]{1,0:T(8,128)(2,1)} %r_ref.3), custom_call_target="tpu_custom_call" | custom-call | flops 16106127360 | bytes 35127296 | tf_op jit(solution)/shard_map/pallas_call | solution.py:158
  256.0 19.8 %collective-permute-done.refs_0_ = f32[2560,512]{1,0:T(8,128)} collective-permute-done((f32[2560,512]{1,0:T(8,128)}, f32[2560,512]{1,0:T(8,128)}, u32[]{:S(2)}, u32[]{:S(2)}) %collective-permute-start) | collective-permute-done | bytes 5242912 | tf_op jit(solution)/shard_map/ppermute | solution.py:235
  275.8 16.6 %shard_map.173 = (f32[2560,512]{1,0:T(8,128)S(1)}, f32[2,320,512]{2,1,0:T(8,128)S(1)}, f32[2,320,512]{2,1,0:T(8,128)S(1)}) custom-call(s32[3]{0:T(128)S(1)} %add_add_fusion.at_ref, bf16[4096,5120]{1,0:T(8,128)(2,1)} %get-tuple-element.176.a_ref, bf16[4096,1280]{1,0:T(8,128)(2,1)} %r_ref.3, f32[2560,512]{1,0:T(8,128)} %collective-permute-done.refs_0_), custom_call_target="tpu_custom_call" | custom-call | flops 10737418240 | bytes 30408704 | tf_op jit(solution)/shard_map/pallas_call | solution.py:158
  296.8 23.9 %shard_map.174 = (f32[2560,768]{1,0:T(8,128)S(1)}, f32[2,320,768]{2,1,0:T(8,128)}, f32[2,320,768]{2,1,0:T(8,128)S(1)}) custom-call(s32[3]{0:T(128)S(1)} %add_add_fusion.at_ref, bf16[4096,5120]{1,0:T(8,128)(2,1)} %get-tuple-element.176.a_ref, bf16[4096,1280]{1,0:T(8,128)(2,1)} %r_ref.3, f32[2560,768]{1,0:T(8,128)} %collective-permute-done.1.refs_0_), custom_call_target="tpu_custom_call" | custom-call | flops 16106127360 | bytes 35127296 | tf_op jit(solution)/shard_map/pallas_call | solution.py:158
  320.7 3.2 copy-done.1
  331.4 44.9 %shard_map.175.b_ref.a_ref = bf16[4096,2560]{1,0:T(8,128)(2,1)} custom-call(bf16[4096,1280]{1,0:T(8,128)(2,1)} %r_ref.3, bf16[5120,1280]{1,0:T(8,128)(2,1)} %w_ref.9, bf16[4096,5120]{1,0:T(8,128)(2,1)} %get-tuple-element.188.z_ref), custom_call_target="tpu_custom_call" | custom-call | flops 26843545600 | bytes 58982400 | tf_op jit(solution)/shard_map/pallas_call | solution.py:78
  376.3 3.3 bitcast_add_fusion.6
  381.8 20.1 %shard_map.176 = f32[640,2560]{1,0:T(8,128)} custom-call(s32[3]{0:T(128)} %copy-done.3, bf16[4096,1280]{1,0:T(8,128)(2,1)} %add_convert_fusion.x_ref.a_ref, bf16[4096,2560]{1,0:T(8,128)(2,1)} %shard_map.175.b_ref.a_ref), custom_call_target="tpu_custom_call" | custom-call | flops 13421772800 | bytes 32768000 | tf_op jit(solution)/shard_map/pallas_call | solution.py:158
  402.0 4.7 collective-permute-done.8
  412.4 4.5 subtract_convert_fusion.2
  417.0 45.2 %shard_map.177.b_ref = bf16[4096,2560]{1,0:T(8,128)(2,1)} custom-call(bf16[4096,1280]{1,0:T(8,128)(2,1)} %r_ref.3, bf16[5120,1280]{1,0:T(8,128)(2,1)} %w_ref.9, bf16[4096,5120]{1,0:T(8,128)(2,1)} %get-tuple-element.188.z_ref), custom_call_target="tpu_custom_call" | custom-call | flops 26843545600 | bytes 58982400 | tf_op jit(solution)/shard_map/pallas_call | solution.py:78
  462.3 20.2 %shard_map.178 = f32[640,2560]{1,0:T(8,128)} custom-call(s32[3]{0:T(128)} %copy-done.3, bf16[4096,1280]{1,0:T(8,128)(2,1)} %add_convert_fusion.x_ref.a_ref, bf16[4096,2560]{1,0:T(8,128)(2,1)} %shard_map.177.b_ref), custom_call_target="tpu_custom_call" | custom-call | flops 13421772800 | bytes 32768000 | tf_op jit(solution)/shard_map/pallas_call | solution.py:158
  482.9 21.6 %shard_map.179 = (f32[640,2560]{1,0:T(8,128)}, f32[2,80,2560]{2,1,0:T(8,128)}, f32[2,80,2560]{2,1,0:T(8,128)}) custom-call(s32[3]{0:T(128)} %copy-done.4, bf16[4096,1280]{1,0:T(8,128)(2,1)} %add_convert_fusion.x_ref.a_ref, bf16[4096,2560]{1,0:T(8,128)(2,1)} %shard_map.175.b_ref.a_ref, f32[640,2560]{1,0:T(8,128)} %collective-permute-done.10.refs_0_), custom_call_target="tpu_custom_call" | custom-call | flops 13421772800 | bytes 32768000 | tf_op jit(solution)/shard_map/pallas_call | solution.py:158
  507.5 21.4 %shard_map.180 = (f32[640,2560]{1,0:T(8,128)}, f32[2,80,2560]{2,1,0:T(8,128)}, f32[2,80,2560]{2,1,0:T(8,128)}) custom-call(s32[3]{0:T(128)} %copy-done.4, bf16[4096,1280]{1,0:T(8,128)(2,1)} %add_convert_fusion.x_ref.a_ref, bf16[4096,2560]{1,0:T(8,128)(2,1)} %shard_map.177.b_ref, f32[640,2560]{1,0:T(8,128)} %collective-permute-done.11.refs_0_), custom_call_target="tpu_custom_call" | custom-call | flops 13421772800 | bytes 32768000 | tf_op jit(solution)/shard_map/pallas_call | solution.py:158
  530.0 36.5 %shard_map.181.refs_0_ = bf16[4096,1280]{1,0:T(8,128)(2,1)} custom-call(bf16[4096,2560]{1,0:T(8,128)(2,1)} %shard_map.175.b_ref.a_ref, bf16[4096,2560]{1,0:T(8,128)(2,1)} %shard_map.177.b_ref, bf16[1280,5120]{1,0:T(8,128)(2,1)} %wb_ref.5, bf16[1280,5120]{1,0:T(8,128)(2,1)} %wb_ref.5, bf16[4096,1280]{1,0:T(8,128)(2,1)} %r_ref.3), custom_call_target="tpu_custom_call" | custom-call | flops 26843545600 | bytes 44564480 | tf_op jit(solution)/shard_map/pallas_call | solution.py:105
  572.0 36.4 %shard_map.182.b_ref.g_ref.r_ref = bf16[4096,1280]{1,0:T(8,128)(2,1)} custom-call(bf16[4096,2560]{1,0:T(8,128)(2,1)} %shard_map.175.b_ref.a_ref, bf16[4096,2560]{1,0:T(8,128)(2,1)} %shard_map.177.b_ref, bf16[1280,5120]{1,0:T(8,128)(2,1)} %wb_ref.5, bf16[1280,5120]{1,0:T(8,128)(2,1)} %wb_ref.5, ...), custom_call_target="tpu_custom_call", output_to_operand_aliasing={{}: (5, {})} | custom-call | flops 26843545600 | bytes 44564480 | tf_op jit(solution)/shard_map/pallas_call | solution.py:105
  608.4 3.2 bitcast_add_fusion.20
  612.7 17.4 %shard_map.183 = f32[2560,512]{1,0:T(8,128)} custom-call(s32[3]{0:T(128)} %copy-done.3, bf16[4096,5120]{1,0:T(8,128)(2,1)} %get-tuple-element.169.a_ref, bf16[4096,1280]{1,0:T(8,128)(2,1)} %shard_map.182.b_ref.g_ref.r_ref), custom_call_target="tpu_custom_call" | custom-call | flops 10737418240 | bytes 30408704 | tf_op jit(solution)/shard_map/pallas_call | solution.py:158
  630.7 4.5 fusion.24
  635.2 4.5 subtract_convert_fusion.1
  639.8 24.0 %shard_map.184 = f32[2560,768]{1,0:T(8,128)} custom-call(s32[3]{0:T(128)} %copy-done.3, bf16[4096,5120]{1,0:T(8,128)(2,1)} %get-tuple-element.169.a_ref, bf16[4096,1280]{1,0:T(8,128)(2,1)} %shard_map.182.b_ref.g_ref.r_ref), custom_call_target="tpu_custom_call" | custom-call | flops 16106127360 | bytes 35127296 | tf_op jit(solution)/shard_map/pallas_call | solution.py:158
  664.2 26.2 %collective-permute-done.20.refs_0_ = f32[2560,512]{1,0:T(8,128)} collective-permute-done((f32[2560,512]{1,0:T(8,128)}, f32[2560,512]{1,0:T(8,128)}, u32[]{:S(2)}, u32[]{:S(2)}) %collective-permute-start.20) | collective-permute-done | bytes 5242912 | tf_op jit(solution)/shard_map/ppermute | solution.py:235
  690.4 19.0 %shard_map.185 = (f32[2560,512]{1,0:T(8,128)}, f32[2,320,512]{2,1,0:T(8,128)}, f32[2,320,512]{2,1,0:T(8,128)}) custom-call(s32[3]{0:T(128)} %copy-done.4, bf16[4096,5120]{1,0:T(8,128)(2,1)} %get-tuple-element.169.a_ref, bf16[4096,1280]{1,0:T(8,128)(2,1)} %shard_map.182.b_ref.g_ref.r_ref, f32[2560,512]{1,0:T(8,128)} %collective-permute-done.20.refs_0_), custom_call_target="tpu_custom_call" | custom-call | flops 10737418240 | bytes 30408704 | tf_op jit(solution)/shard_map/pallas_call | solution.py:158
  711.2 25.2 %shard_map.186 = (f32[2560,768]{1,0:T(8,128)}, f32[2,320,768]{2,1,0:T(8,128)}, f32[2,320,768]{2,1,0:T(8,128)}) custom-call(s32[3]{0:T(128)} %copy-done.4, bf16[4096,5120]{1,0:T(8,128)(2,1)} %get-tuple-element.169.a_ref, bf16[4096,1280]{1,0:T(8,128)(2,1)} %shard_map.182.b_ref.g_ref.r_ref, f32[2560,768]{1,0:T(8,128)} %collective-permute-done.21.refs_0_), custom_call_target="tpu_custom_call" | custom-call | flops 16106127360 | bytes 35127296 | tf_op jit(solution)/shard_map/pallas_call | solution.py:158
  738.7 45.1 %shard_map.187.b_ref.a_ref = bf16[4096,2560]{1,0:T(8,128)(2,1)} custom-call(bf16[4096,1280]{1,0:T(8,128)(2,1)} %shard_map.182.b_ref.g_ref.r_ref, bf16[5120,1280]{1,0:T(8,128)(2,1)} %w_ref.11, bf16[4096,5120]{1,0:T(8,128)(2,1)} %get-tuple-element.250.z_ref), custom_call_target="tpu_custom_call" | custom-call | flops 26843545600 | bytes 58982400 | tf_op jit(solution)/shard_map/pallas_call | solution.py:78
  783.8 20.2 %shard_map.188 = f32[640,2560]{1,0:T(8,128)} custom-call(s32[3]{0:T(128)} %copy-done.3, bf16[4096,1280]{1,0:T(8,128)(2,1)} %a_ref.7, bf16[4096,2560]{1,0:T(8,128)(2,1)} %shard_map.187.b_ref.a_ref), custom_call_target="tpu_custom_call" | custom-call | flops 13421772800 | bytes 32768000 | tf_op jit(solution)/shard_map/pallas_call | solution.py:158
  804.0 3.0 bitcast_add_fusion.26
  807.0 3.0 bitcast_add_fusion.2
  814.1 44.8 %shard_map.189.b_ref = bf16[4096,2560]{1,0:T(8,128)(2,1)} custom-call(bf16[4096,1280]{1,0:T(8,128)(2,1)} %shard_map.182.b_ref.g_ref.r_ref, bf16[5120,1280]{1,0:T(8,128)(2,1)} %w_ref.11, bf16[4096,5120]{1,0:T(8,128)(2,1)} %get-tuple-element.250.z_ref), custom_call_target="tpu_custom_call" | custom-call | flops 26843545600 | bytes 58982400 | tf_op jit(solution)/shard_map/pallas_call | solution.py:78
  864.6 4.5 subtract_convert_fusion
  869.2 10.9 collective-permute-done.30.refs_0_
  880.0 21.7 %shard_map.190 = (f32[640,2560]{1,0:T(8,128)}, f32[2,80,2560]{2,1,0:T(8,128)}, f32[2,80,2560]{2,1,0:T(8,128)}) custom-call(s32[3]{0:T(128)} %copy-done.4, bf16[4096,1280]{1,0:T(8,128)(2,1)} %a_ref.7, bf16[4096,2560]{1,0:T(8,128)(2,1)} %shard_map.187.b_ref.a_ref, f32[640,2560]{1,0:T(8,128)} %collective-permute-done.30.refs_0_), custom_call_target="tpu_custom_call" | custom-call | flops 13421772800 | bytes 32768000 | tf_op jit(solution)/shard_map/pallas_call | solution.py:158
  901.7 20.1 %shard_map.191 = f32[640,2560]{1,0:T(8,128)} custom-call(s32[3]{0:T(128)} %copy-done.3, bf16[4096,1280]{1,0:T(8,128)(2,1)} %a_ref.7, bf16[4096,2560]{1,0:T(8,128)(2,1)} %shard_map.189.b_ref), custom_call_target="tpu_custom_call" | custom-call | flops 13421772800 | bytes 32768000 | tf_op jit(solution)/shard_map/pallas_call | solution.py:158
  923.9 11.7 shard_map.192
  935.6 21.5 %shard_map.193 = (f32[640,2560]{1,0:T(8,128)}, f32[2,80,2560]{2,1,0:T(8,128)}, f32[2,80,2560]{2,1,0:T(8,128)}) custom-call(s32[3]{0:T(128)} %copy-done.4, bf16[4096,1280]{1,0:T(8,128)(2,1)} %a_ref.7, bf16[4096,2560]{1,0:T(8,128)(2,1)} %shard_map.189.b_ref, f32[640,2560]{1,0:T(8,128)} %collective-permute-done.31.refs_0_), custom_call_target="tpu_custom_call" | custom-call | flops 13421772800 | bytes 32768000 | tf_op jit(solution)/shard_map/pallas_call | solution.py:158
  957.1 13.4 %collective-permute-done.32 = f32[2,80,2560]{2,1,0:T(8,128)S(1)} collective-permute-done((f32[2,80,2560]{2,1,0:T(8,128)}, f32[2,80,2560]{2,1,0:T(8,128)S(1)}, u32[]{:S(2)}, u32[]{:S(2)}) %collective-permute-start.32) | collective-permute-done | bytes 1638432 | tf_op jit(solution)/shard_map/ppermute | solution.py:198
  975.3 36.4 %shard_map.194.refs_0_ = bf16[4096,1280]{1,0:T(8,128)(2,1)} custom-call(bf16[4096,2560]{1,0:T(8,128)(2,1)} %shard_map.187.b_ref.a_ref, bf16[4096,2560]{1,0:T(8,128)(2,1)} %shard_map.189.b_ref, bf16[1280,5120]{1,0:T(8,128)(2,1)} %wb_ref.7, bf16[1280,5120]{1,0:T(8,128)(2,1)} %wb_ref.7, bf16[4096,1280]{1,0:T(8,128)(2,1)} %shard_map.182.b_ref.g_ref.r_ref), custom_call_target="tpu_custom_call" | custom-call | flops 26843545600 | bytes 44564480 | tf_op jit(solution)/shard_map/pallas_call | solution.py:105
  1019.2 61.3 %collective-permute-done.36 = f32[2,80,2560]{2,1,0:T(8,128)S(1)} collective-permute-done((f32[2,80,2560]{2,1,0:T(8,128)}, f32[2,80,2560]{2,1,0:T(8,128)S(1)}, u32[]{:S(2)}, u32[]{:S(2)}) %collective-permute-start.36) | collective-permute-done | bytes 1638432 | tf_op jit(solution)/shard_map/ppermute | solution.py:198
  1082.0 3.0 bitcast_add_fusion.10
  1086.9 11.7 shard_map.195
  1098.6 11.7 shard_map.196
  1117.8 37.2 %shard_map.197 = bf16[4096,1280]{1,0:T(8,128)(2,1)} custom-call(bf16[4096,2560]{1,0:T(8,128)(2,1)} %shard_map.187.b_ref.a_ref, bf16[4096,2560]{1,0:T(8,128)(2,1)} %shard_map.189.b_ref, bf16[1280,5120]{1,0:T(8,128)(2,1)} %wb_ref.7, bf16[1280,5120]{1,0:T(8,128)(2,1)} %wb_ref.7, ...), custom_call_target="tpu_custom_call", output_to_operand_aliasing={{}: (5, {})} | custom-call | flops 26843545600 | bytes 44564480 | tf_op jit(solution)/shard_map/pallas_call | solution.py:105
  1155.0 7.9 shard_map.198.refs_1_
  1163.0 7.9 shard_map.199
  (130 shorter events, 72.1 us)
Async XLA Ops:
  7.2 914.6 %all-gather.6.cloned.1.call-start = ((), (), s32[]{:S(2)}) async-start(), calls=%async_computation | async-start | bytes 14745600 | tf_op jit(solution)/shard_map/all_gather | solution.py:253
  7.2 74.0 %copy-start.13 = (bf16[5120,1280]{1,0:T(8,128)(2,1)S(1)}, bf16[5120,1280]{1,0:T(8,128)(2,1)}, u32[]{:S(2)}) copy-start(bf16[5120,1280]{1,0:T(8,128)(2,1)} %w_ref.11) | copy-start | bytes 39321604
  141.0 74.8 %copy-start = (bf16[4096,1280]{1,0:T(8,128)(2,1)S(1)}, bf16[4096,1280]{1,0:T(8,128)(2,1)}, u32[]{:S(2)}) copy-start(bf16[4096,1280]{1,0:T(8,128)(2,1)} %r_ref.3) | copy-start | bytes 31457284
  255.1 41.7 %collective-permute-start.1 = (f32[2560,768]{1,0:T(8,128)}, f32[2560,768]{1,0:T(8,128)}, u32[]{:S(2)}, u32[]{:S(2)}) collective-permute-start(f32[2560,768]{1,0:T(8,128)} %shard_map.172), channel_id=1, source_target_pairs={{0,1},{1,0},{2,3},{3,2},{4,5},{5,4},{6,7},{7,6}} | collective-permute-start | bytes 23592968 | tf_op jit(solution)/shard_map/ppermute | solution.py:235
  255.9 19.9 %collective-permute-start = (f32[2560,512]{1,0:T(8,128)}, f32[2560,512]{1,0:T(8,128)}, u32[]{:S(2)}, u32[]{:S(2)}) collective-permute-start(f32[2560,512]{1,0:T(8,128)} %shard_map.171), channel_id=1, source_target_pairs={{0,1},{1,0},{2,3},{3,2},{4,5},{5,4},{6,7},{7,6}} | collective-permute-start | bytes 15728648 | tf_op jit(solution)/shard_map/ppermute | solution.py:235
  256.0 40.8 %copy-start.4 = (s32[3]{0:T(128)}, s32[3]{0:T(128)S(1)}, u32[]{:S(2)}) copy-start(s32[3]{0:T(128)S(1)} %add_add_fusion.at_ref) | copy-start | bytes 40
  292.4 32.0 %collective-permute-start.2 = (f32[2,320,512]{2,1,0:T(8,128)S(1)}, f32[2,320,512]{2,1,0:T(8,128)S(1)}, u32[]{:S(2)}, u32[]{:S(2)}) collective-permute-start(f32[2,320,512]{2,1,0:T(8,128)S(1)} %get-tuple-element.181), channel_id=1, source_target_pairs={{0,2},{2,0},{1,3},{3,1},{4,6},{6,4},{5,7},{7,5}} | collective-permute-start | bytes 3932168 | tf_op jit(solution)/shard_map/ppermute | solution.py:198
  295.2 30.5 %collective-permute-start.3 = (f32[2,320,512]{2,1,0:T(8,128)S(1)}, f32[2,320,512]{2,1,0:T(8,128)S(1)}, u32[]{:S(2)}, u32[]{:S(2)}) collective-permute-start(f32[2,320,512]{2,1,0:T(8,128)S(1)} %get-tuple-element.182), channel_id=1, source_target_pairs={{0,4},{4,0},{1,5},{5,1},{2,6},{6,2},{3,7},{7,3}} | collective-permute-start | bytes 3932168 | tf_op jit(solution)/shard_map/ppermute | solution.py:198
  327.3 49.0 %collective-permute-start.4 = (f32[2,320,768]{2,1,0:T(8,128)}, f32[2,320,768]{2,1,0:T(8,128)S(1)}, u32[]{:S(2)}, u32[]{:S(2)}) collective-permute-start(f32[2,320,768]{2,1,0:T(8,128)} %get-tuple-element.189), channel_id=1, source_target_pairs={{0,2},{2,0},{1,3},{3,1},{4,6},{6,4},{5,7},{7,5}} | collective-permute-start | bytes 5898248 | tf_op jit(solution)/shard_map/ppermute | solution.py:198
  327.7 48.5 %collective-permute-start.5 = (f32[2,320,768]{2,1,0:T(8,128)S(1)}, f32[2,320,768]{2,1,0:T(8,128)}, u32[]{:S(2)}, u32[]{:S(2)}) collective-permute-start(f32[2,320,768]{2,1,0:T(8,128)S(1)} %get-tuple-element.190), channel_id=1, source_target_pairs={{0,4},{4,0},{1,5},{5,1},{2,6},{6,2},{3,7},{7,3}} | collective-permute-start | bytes 5898248 | tf_op jit(solution)/shard_map/ppermute | solution.py:198
  329.5 72.4 %collective-permute-start.6 = (f32[1,320,512]{2,1,0:T(8,128)}, f32[1,320,512]{2,1,0:T(8,128)}, u32[]{:S(2)}, u32[]{:S(2)}) collective-permute-start(f32[1,320,512]{2,1,0:T(8,128)} %get-tuple-element.197), channel_id=1, source_target_pairs={{0,4},{4,0},{1,5},{5,1},{2,6},{6,2},{3,7},{7,3}} | collective-permute-start | bytes 1966088 | tf_op jit(solution)/shard_map/ppermute | solution.py:198
  329.8 72.2 %collective-permute-start.7 = (f32[1,320,512]{2,1,0:T(8,128)}, f32[1,320,512]{2,1,0:T(8,128)}, u32[]{:S(2)}, u32[]{:S(2)}) collective-permute-start(f32[1,320,512]{2,1,0:T(8,128)} %get-tuple-element.198), channel_id=1, source_target_pairs={{0,2},{2,0},{1,3},{3,1},{4,6},{6,4},{5,7},{7,5}} | collective-permute-start | bytes 1966088 | tf_op jit(solution)/shard_map/ppermute | solution.py:198
  379.6 27.1 %collective-permute-start.8 = (f32[1,320,768]{2,1,0:T(8,128)}, f32[1,320,768]{2,1,0:T(8,128)}, u32[]{:S(2)}, u32[]{:S(2)}) collective-permute-start(f32[1,320,768]{2,1,0:T(8,128)} %get-tuple-element.199), channel_id=1, source_target_pairs={{0,4},{4,0},{1,5},{5,1},{2,6},{6,2},{3,7},{7,3}} | collective-permute-start | bytes 2949128 | tf_op jit(solution)/shard_map/ppermute | solution.py:198
  381.1 25.6 %collective-permute-start.9 = (f32[1,320,768]{2,1,0:T(8,128)}, f32[1,320,768]{2,1,0:T(8,128)}, u32[]{:S(2)}, u32[]{:S(2)}) collective-permute-start(f32[1,320,768]{2,1,0:T(8,128)} %get-tuple-element.200), channel_id=1, source_target_pairs={{0,2},{2,0},{1,3},{3,1},{4,6},{6,4},{5,7},{7,5}} | collective-permute-start | bytes 2949128 | tf_op jit(solution)/shard_map/ppermute | solution.py:198
  417.0 602.2 %all-gather.8.cloned.1.call-start = ((), (), s32[]{:S(2)}) async-start(), calls=%async_computation.1 | async-start | bytes 14745600 | tf_op jit(solution)/shard_map/all_gather | solution.py:253
  417.0 65.8 %collective-permute-start.10 = (f32[640,2560]{1,0:T(8,128)}, f32[640,2560]{1,0:T(8,128)}, u32[]{:S(2)}, u32[]{:S(2)}) collective-permute-start(f32[640,2560]{1,0:T(8,128)} %shard_map.176), channel_id=1, source_target_pairs={{0,1},{1,0},{2,3},{3,2},{4,5},{5,4},{6,7},{7,6}} | collective-permute-start | bytes 19660808 | tf_op jit(solution)/shard_map/ppermute | solution.py:235
  482.5 25.0 %collective-permute-start.11 = (f32[640,2560]{1,0:T(8,128)}, f32[640,2560]{1,0:T(8,128)}, u32[]{:S(2)}, u32[]{:S(2)}) collective-permute-start(f32[640,2560]{1,0:T(8,128)} %shard_map.178), channel_id=1, source_target_pairs={{0,1},{1,0},{2,3},{3,2},{4,5},{5,4},{6,7},{7,6}} | collective-permute-start | bytes 19660808 | tf_op jit(solution)/shard_map/ppermute | solution.py:235
  504.5 62.0 %collective-permute-start.12 = (f32[2,80,2560]{2,1,0:T(8,128)}, f32[2,80,2560]{2,1,0:T(8,128)S(1)}, u32[]{:S(2)}, u32[]{:S(2)}) collective-permute-start(f32[2,80,2560]{2,1,0:T(8,128)} %get-tuple-element.216), channel_id=1, source_target_pairs={{0,2},{2,0},{1,3},{3,1},{4,6},{6,4},{5,7},{7,5}} | collective-permute-start | bytes 4915208 | tf_op jit(solution)/shard_map/ppermute | solution.py:198
  505.8 60.7 %collective-permute-start.13 = (f32[2,80,2560]{2,1,0:T(8,128)}, f32[2,80,2560]{2,1,0:T(8,128)S(1)}, u32[]{:S(2)}, u32[]{:S(2)}) collective-permute-start(f32[2,80,2560]{2,1,0:T(8,128)} %get-tuple-element.217), channel_id=1, source_target_pairs={{0,4},{4,0},{1,5},{5,1},{2,6},{6,2},{3,7},{7,3}} | collective-permute-start | bytes 4915208 | tf_op jit(solution)/shard_map/ppermute | solution.py:198
  528.9 79.4 %collective-permute-start.14 = (f32[2,80,2560]{2,1,0:T(8,128)}, f32[2,80,2560]{2,1,0:T(8,128)}, u32[]{:S(2)}, u32[]{:S(2)}) collective-permute-start(f32[2,80,2560]{2,1,0:T(8,128)} %get-tuple-element.223), channel_id=1, source_target_pairs={{0,2},{2,0},{1,3},{3,1},{4,6},{6,4},{5,7},{7,5}} | collective-permute-start | bytes 4915208 | tf_op jit(solution)/shard_map/ppermute | solution.py:198
  529.5 78.8 %collective-permute-start.15 = (f32[2,80,2560]{2,1,0:T(8,128)}, f32[2,80,2560]{2,1,0:T(8,128)}, u32[]{:S(2)}, u32[]{:S(2)}) collective-permute-start(f32[2,80,2560]{2,1,0:T(8,128)} %get-tuple-element.224), channel_id=1, source_target_pairs={{0,4},{4,0},{1,5},{5,1},{2,6},{6,2},{3,7},{7,3}} | collective-permute-start | bytes 4915208 | tf_op jit(solution)/shard_map/ppermute | solution.py:198
  569.0 61.1 %collective-permute-start.16 = (f32[1,80,2560]{2,1,0:T(8,128)}, f32[1,80,2560]{2,1,0:T(8,128)}, u32[]{:S(2)}, u32[]{:S(2)}) collective-permute-start(f32[1,80,2560]{2,1,0:T(8,128)} %get-tuple-element.231), channel_id=1, source_target_pairs={{0,4},{4,0},{1,5},{5,1},{2,6},{6,2},{3,7},{7,3}} | collective-permute-start | bytes 2457608 | tf_op jit(solution)/shard_map/ppermute | solution.py:198
  570.6 59.6 %collective-permute-start.17 = (f32[1,80,2560]{2,1,0:T(8,128)S(1)}, f32[1,80,2560]{2,1,0:T(8,128)}, u32[]{:S(2)}, u32[]{:S(2)}) collective-permute-start(f32[1,80,2560]{2,1,0:T(8,128)S(1)} %get-tuple-element.232), channel_id=1, source_target_pairs={{0,2},{2,0},{1,3},{3,1},{4,6},{6,4},{5,7},{7,5}} | collective-permute-start | bytes 2457608 | tf_op jit(solution)/shard_map/ppermute | solution.py:198
  611.6 18.7 %collective-permute-start.18 = (f32[1,80,2560]{2,1,0:T(8,128)}, f32[1,80,2560]{2,1,0:T(8,128)}, u32[]{:S(2)}, u32[]{:S(2)}) collective-permute-start(f32[1,80,2560]{2,1,0:T(8,128)} %get-tuple-element.233), channel_id=1, source_target_pairs={{0,4},{4,0},{1,5},{5,1},{2,6},{6,2},{3,7},{7,3}} | collective-permute-start | bytes 2457608 | tf_op jit(solution)/shard_map/ppermute | solution.py:198
  612.0 18.7 %collective-permute-start.19 = (f32[1,80,2560]{2,1,0:T(8,128)}, f32[1,80,2560]{2,1,0:T(8,128)}, u32[]{:S(2)}, u32[]{:S(2)}) collective-permute-start(f32[1,80,2560]{2,1,0:T(8,128)} %get-tuple-element.234), channel_id=1, source_target_pairs={{0,2},{2,0},{1,3},{3,1},{4,6},{6,4},{5,7},{7,5}} | collective-permute-start | bytes 2457608 | tf_op jit(solution)/shard_map/ppermute | solution.py:198
  639.7 458.9 %all-gather.10.cloned.1.call-start = ((), (), s32[]{:S(2)}) async-start(), calls=%async_computation.2 | async-start | bytes 14745600 | tf_op jit(solution)/shard_map/all_gather | solution.py:253
  663.7 47.4 %collective-permute-start.21 = (f32[2560,768]{1,0:T(8,128)}, f32[2560,768]{1,0:T(8,128)}, u32[]{:S(2)}, u32[]{:S(2)}) collective-permute-start(f32[2560,768]{1,0:T(8,128)} %shard_map.184), channel_id=1, source_target_pairs={{0,1},{1,0},{2,3},{3,2},{4,5},{5,4},{6,7},{7,6}} | collective-permute-start | bytes 23592968 | tf_op jit(solution)/shard_map/ppermute | solution.py:235
  663.7 26.7 %collective-permute-start.20 = (f32[2560,512]{1,0:T(8,128)}, f32[2560,512]{1,0:T(8,128)}, u32[]{:S(2)}, u32[]{:S(2)}) collective-permute-start(f32[2560,512]{1,0:T(8,128)} %shard_map.183), channel_id=1, source_target_pairs={{0,1},{1,0},{2,3},{3,2},{4,5},{5,4},{6,7},{7,6}} | collective-permute-start | bytes 15728648 | tf_op jit(solution)/shard_map/ppermute | solution.py:235
  709.4 94.5 %collective-permute-start.22 = (f32[2,320,512]{2,1,0:T(8,128)}, f32[2,320,512]{2,1,0:T(8,128)}, u32[]{:S(2)}, u32[]{:S(2)}) collective-permute-start(f32[2,320,512]{2,1,0:T(8,128)} %get-tuple-element.252), channel_id=1, source_target_pairs={{0,2},{2,0},{1,3},{3,1},{4,6},{6,4},{5,7},{7,5}} | collective-permute-start | bytes 3932168 | tf_op jit(solution)/shard_map/ppermute | solution.py:198
  709.5 94.4 %collective-permute-start.23 = (f32[2,320,512]{2,1,0:T(8,128)}, f32[2,320,512]{2,1,0:T(8,128)}, u32[]{:S(2)}, u32[]{:S(2)}) collective-permute-start(f32[2,320,512]{2,1,0:T(8,128)} %get-tuple-element.253), channel_id=1, source_target_pairs={{0,4},{4,0},{1,5},{5,1},{2,6},{6,2},{3,7},{7,3}} | collective-permute-start | bytes 3932168 | tf_op jit(solution)/shard_map/ppermute | solution.py:198
  736.4 67.6 %collective-permute-start.24 = (f32[2,320,768]{2,1,0:T(8,128)}, f32[2,320,768]{2,1,0:T(8,128)S(1)}, u32[]{:S(2)}, u32[]{:S(2)}) collective-permute-start(f32[2,320,768]{2,1,0:T(8,128)} %get-tuple-element.254), channel_id=1, source_target_pairs={{0,2},{2,0},{1,3},{3,1},{4,6},{6,4},{5,7},{7,5}} | collective-permute-start | bytes 5898248 | tf_op jit(solution)/shard_map/ppermute | solution.py:198
  737.9 66.1 %collective-permute-start.25 = (f32[2,320,768]{2,1,0:T(8,128)}, f32[2,320,768]{2,1,0:T(8,128)S(1)}, u32[]{:S(2)}, u32[]{:S(2)}) collective-permute-start(f32[2,320,768]{2,1,0:T(8,128)} %get-tuple-element.255), channel_id=1, source_target_pairs={{0,4},{4,0},{1,5},{5,1},{2,6},{6,2},{3,7},{7,3}} | collective-permute-start | bytes 5898248 | tf_op jit(solution)/shard_map/ppermute | solution.py:198
  810.0 48.9 %collective-permute-start.28 = (f32[1,320,768]{2,1,0:T(8,128)}, f32[1,320,768]{2,1,0:T(8,128)}, u32[]{:S(2)}, u32[]{:S(2)}) collective-permute-start(f32[1,320,768]{2,1,0:T(8,128)} %get-tuple-element.266), channel_id=1, source_target_pairs={{0,4},{4,0},{1,5},{5,1},{2,6},{6,2},{3,7},{7,3}} | collective-permute-start | bytes 2949128 | tf_op jit(solution)/shard_map/ppermute | solution.py:198
  811.3 47.6 %collective-permute-start.29 = (f32[1,320,768]{2,1,0:T(8,128)}, f32[1,320,768]{2,1,0:T(8,128)}, u32[]{:S(2)}, u32[]{:S(2)}) collective-permute-start(f32[1,320,768]{2,1,0:T(8,128)} %get-tuple-element.267), channel_id=1, source_target_pairs={{0,2},{2,0},{1,3},{3,1},{4,6},{6,4},{5,7},{7,5}} | collective-permute-start | bytes 2949128 | tf_op jit(solution)/shard_map/ppermute | solution.py:198
  811.8 47.1 %collective-permute-start.26 = (f32[1,320,512]{2,1,0:T(8,128)}, f32[1,320,512]{2,1,0:T(8,128)}, u32[]{:S(2)}, u32[]{:S(2)}) collective-permute-start(f32[1,320,512]{2,1,0:T(8,128)} %get-tuple-element.264), channel_id=1, source_target_pairs={{0,4},{4,0},{1,5},{5,1},{2,6},{6,2},{3,7},{7,3}} | collective-permute-start | bytes 1966088 | tf_op jit(solution)/shard_map/ppermute | solution.py:198
  812.2 46.7 %collective-permute-start.27 = (f32[1,320,512]{2,1,0:T(8,128)}, f32[1,320,512]{2,1,0:T(8,128)}, u32[]{:S(2)}, u32[]{:S(2)}) collective-permute-start(f32[1,320,512]{2,1,0:T(8,128)} %get-tuple-element.265), channel_id=1, source_target_pairs={{0,2},{2,0},{1,3},{3,1},{4,6},{6,4},{5,7},{7,5}} | collective-permute-start | bytes 1966088 | tf_op jit(solution)/shard_map/ppermute | solution.py:198
  869.1 286.0 %all-gather.12.cloned.1.call-start = ((), (), s32[]{:S(2)}) async-start(), calls=%async_computation.3 | async-start | bytes 7372800 | tf_op jit(solution)/shard_map/all_gather | solution.py:253
  869.1 10.9 collective-permute-start.30
  921.8 13.7 %collective-permute-start.31 = (f32[640,2560]{1,0:T(8,128)}, f32[640,2560]{1,0:T(8,128)}, u32[]{:S(2)}, u32[]{:S(2)}) collective-permute-start(f32[640,2560]{1,0:T(8,128)} %shard_map.191), channel_id=1, source_target_pairs={{0,1},{1,0},{2,3},{3,2},{4,5},{5,4},{6,7},{7,6}} | collective-permute-start | bytes 19660808 | tf_op jit(solution)/shard_map/ppermute | solution.py:235
  922.1 48.4 %collective-permute-start.32 = (f32[2,80,2560]{2,1,0:T(8,128)}, f32[2,80,2560]{2,1,0:T(8,128)S(1)}, u32[]{:S(2)}, u32[]{:S(2)}) collective-permute-start(f32[2,80,2560]{2,1,0:T(8,128)} %get-tuple-element.286), channel_id=1, source_target_pairs={{0,2},{2,0},{1,3},{3,1},{4,6},{6,4},{5,7},{7,5}} | collective-permute-start | bytes 4915208 | tf_op jit(solution)/shard_map/ppermute | solution.py:198
  922.2 48.4 %collective-permute-start.33 = (f32[2,80,2560]{2,1,0:T(8,128)}, f32[2,80,2560]{2,1,0:T(8,128)S(1)}, u32[]{:S(2)}, u32[]{:S(2)}) collective-permute-start(f32[2,80,2560]{2,1,0:T(8,128)} %get-tuple-element.287), channel_id=1, source_target_pairs={{0,4},{4,0},{1,5},{5,1},{2,6},{6,2},{3,7},{7,3}} | collective-permute-start | bytes 4915208 | tf_op jit(solution)/shard_map/ppermute | solution.py:198
  973.3 38.4 %collective-permute-start.34 = (f32[1,80,2560]{2,1,0:T(8,128)}, f32[1,80,2560]{2,1,0:T(8,128)S(1)}, u32[]{:S(2)}, u32[]{:S(2)}) collective-permute-start(f32[1,80,2560]{2,1,0:T(8,128)} %get-tuple-element.293), channel_id=1, source_target_pairs={{0,4},{4,0},{1,5},{5,1},{2,6},{6,2},{3,7},{7,3}} | collective-permute-start | bytes 2457608 | tf_op jit(solution)/shard_map/ppermute | solution.py:198
  974.8 36.9 %collective-permute-start.35 = (f32[1,80,2560]{2,1,0:T(8,128)}, f32[1,80,2560]{2,1,0:T(8,128)}, u32[]{:S(2)}, u32[]{:S(2)}) collective-permute-start(f32[1,80,2560]{2,1,0:T(8,128)} %get-tuple-element.294), channel_id=1, source_target_pairs={{0,2},{2,0},{1,3},{3,1},{4,6},{6,4},{5,7},{7,5}} | collective-permute-start | bytes 2457608 | tf_op jit(solution)/shard_map/ppermute | solution.py:198
  1016.8 146.1 %all-gather.14.cloned.1.call-start = ((), (), s32[]{:S(2)}) async-start(), calls=%async_computation.4 | async-start | bytes 7372800 | tf_op jit(solution)/shard_map/all_gather | solution.py:253
  1017.1 63.4 %collective-permute-start.36 = (f32[2,80,2560]{2,1,0:T(8,128)}, f32[2,80,2560]{2,1,0:T(8,128)S(1)}, u32[]{:S(2)}, u32[]{:S(2)}) collective-permute-start(f32[2,80,2560]{2,1,0:T(8,128)} %get-tuple-element.300), channel_id=1, source_target_pairs={{0,2},{2,0},{1,3},{3,1},{4,6},{6,4},{5,7},{7,5}} | collective-permute-start | bytes 4915208 | tf_op jit(solution)/shard_map/ppermute | solution.py:198
  1018.6 63.4 %collective-permute-start.37 = (f32[2,80,2560]{2,1,0:T(8,128)}, f32[2,80,2560]{2,1,0:T(8,128)}, u32[]{:S(2)}, u32[]{:S(2)}) collective-permute-start(f32[2,80,2560]{2,1,0:T(8,128)} %get-tuple-element.301), channel_id=1, source_target_pairs={{0,4},{4,0},{1,5},{5,1},{2,6},{6,2},{3,7},{7,3}} | collective-permute-start | bytes 4915208 | tf_op jit(solution)/shard_map/ppermute | solution.py:198
  1085.0 25.2 %collective-permute-start.38 = (f32[1,80,2560]{2,1,0:T(8,128)}, f32[1,80,2560]{2,1,0:T(8,128)}, u32[]{:S(2)}, u32[]{:S(2)}) collective-permute-start(f32[1,80,2560]{2,1,0:T(8,128)} %get-tuple-element.311), channel_id=1, source_target_pairs={{0,4},{4,0},{1,5},{5,1},{2,6},{6,2},{3,7},{7,3}} | collective-permute-start | bytes 2457608 | tf_op jit(solution)/shard_map/ppermute | solution.py:198
  1085.6 24.7 %collective-permute-start.39 = (f32[1,80,2560]{2,1,0:T(8,128)}, f32[1,80,2560]{2,1,0:T(8,128)}, u32[]{:S(2)}, u32[]{:S(2)}) collective-permute-start(f32[1,80,2560]{2,1,0:T(8,128)} %get-tuple-element.312), channel_id=1, source_target_pairs={{0,2},{2,0},{1,3},{3,1},{4,6},{6,4},{5,7},{7,5}} | collective-permute-start | bytes 2457608 | tf_op jit(solution)/shard_map/ppermute | solution.py:198
  (11 other events, 106.1 us)
Sparse Core Ops, SparseCore 0:
  417.1 70.3 all-gather.5
  639.8 68.9 all-gather.7
  869.2 78.6 all-gather.9
  1017.0 66.1 all-gather.11
  1116.0 41.0 all-gather.13

commit v3 on v2

--- a/solution.py
+++ b/solution.py
@@ -166,7 +166,7 @@
     refs[-1][...] = refs[0][...]
 
 
-def copy(w, shape=None, half=0, into=None, steps=8):
+def copy(w, shape=None, half=0, into=None, steps=5):
     rows, cols = w.shape
     block = pl.BlockSpec((rows // steps, cols), lambda i: (i, 0))
     return pl.pallas_call(
@@ -347,12 +347,12 @@
         wa, ma = update(w1, m1, c1a.total(v))
         top, wa = gate(top, wa)
         ga = gather(wa)
-        top, w3g, *v = gate(top, w3g, *c1b.flight)
+        top, w3g = gate(top, w3g)
+        w3n = copy(w3g)
+        top, w3n, w2g, *v = gate(top, w3n, w2g, *c1b.flight)
         c1b.second(v)
-        top, w3g, *v = gate(top, w3g, *c1b.out)
+        top, w2g, *v = gate(top, w2g, *c1b.out)
         c1b.send(2, v)
-        w3n = copy(w3g)
-        w3n, w2g = gate(w3n, w2g)
         w2n = copy(w2g)
         top, w2n, *v = gate(top, w2n, *c1b.flight)
         wb, mb = update(w1, m1, c1b.total(v), start=wa.shape[1])

time: 1180 us -> 1170 us (level)
  transfers between devices with their start and end apart: 45 -> 45, of which waited for: 11 -> 13; matrix products, arithmetic and copies ran while one was open for 4% -> 4% of each run, Pallas kernels for 56% -> 57%
where the time goes in v3:
time: 1170 us
  Pallas kernels  857 us (73%)
  waiting for transfers between devices  132 us (11%)
  other arithmetic  62.2 us (5%)
  matrix products  59.7 us (5%)
  starting transfers between devices  36.8 us (3%)
  between operations  14.3 us (1%)
    pallas_call x16, Pallas kernels, grad(): pl.pallas_call(_grad_body, grid_spec=pltpu.PrefetchScalarGridSpec(num_sca...  332 us
    pallas_call x4, Pallas kernels, dz_half(): pl.pallas_call(functools.partial(_dz_body, sub), grid=(n // bn, m // bm),...  180 us
    pallas_call x2, Pallas kernels, zh(): pl.pallas_call(functools.partial(_zh_body, sub), grid=(n // bn, m // bm),...  149 us
    pallas_call x4, Pallas kernels, back(): pl.pallas_call(functools.partial(_back_body, sub), grid=(steps,), in_spec...  146 us
    ppermute x32, waiting for transfers between devices, send(): self.flight.append(lax.ppermute(v, ax, SWAP))  75.4 us
    dot_general x1, matrix products, dot(): return jnp.dot(a, b, preferred_element_type=F32)  59.7 us
    ppermute x8, waiting for transfers between devices, send(): return lax.ppermute(s, 'dx', SWAP)  56.8 us
    pallas_call x5, Pallas kernels, copy(): pl.pallas_call(_copy_body, grid=(steps,), in_specs=[block] + ([] if into...  48.9 us
  transfers between devices with their start and end apart: 45, of which 13 were waited for; matrix products, arithmetic and copies ran while one was open for 4% of the time, Pallas kernels for 57%

profile of v3, /device:TPU:0, one launch (start us, length us, event | category | flops | bytes accessed | tf_op | source)
XLA Modules:
  0.0 1166.7 jit_solution(4503202529743622243)
XLA Ops:
  7.2 74.0 %shard_map.169 = (bf16[4096,5120]{1,0:T(8,128)(2,1)}, bf16[4096,5120]{1,0:T(8,128)(2,1)}) custom-call(bf16[4096,1280]{1,0:T(8,128)(2,1)} %a_ref.7, bf16[1280,5120]{1,0:T(8,128)(2,1)} %wb_ref.7), custom_call_target="tpu_custom_call" | custom-call | flops 53687091200 | bytes 107479040 | tf_op jit(solution)/shard_map/pallas_call | solution.py:59
  81.3 59.7 %add_convert_fusion.x_ref.a_ref = bf16[4096,1280]{1,0:T(8,128)(2,1)} fusion(bf16[4096,1280]{1,0:T(8,128)(2,1)} %a_ref.7, bf16[4096,5120]{1,0:T(8,128)(2,1)} %get-tuple-element.170.a_ref, bf16[5120,1280]{1,0:T(8,128)(2,1)S(1)} %copy-done.13), kind=kOutput, calls=%fused_computation | convolution fusion | flops 53702819840 | bytes 76021760 | tf_op jit(solution)/shard_map/dot_general | solution.py:220
  141.0 74.7 %shard_map.170 = (bf16[4096,5120]{1,0:T(8,128)(2,1)}, bf16[4096,5120]{1,0:T(8,128)(2,1)}) custom-call(bf16[4096,1280]{1,0:T(8,128)(2,1)} %add_convert_fusion.x_ref.a_ref, bf16[1280,5120]{1,0:T(8,128)(2,1)} %wb_ref.5), custom_call_target="tpu_custom_call" | custom-call | flops 53687091200 | bytes 107479040 | tf_op jit(solution)/shard_map/pallas_call | solution.py:59
  215.8 15.8 %shard_map.171 = f32[2560,512]{1,0:T(8,128)} custom-call(s32[3]{0:T(128)S(1)} %add_add_fusion.1.at_ref, bf16[4096,5120]{1,0:T(8,128)(2,1)} %get-tuple-element.177.a_ref, bf16[4096,1280]{1,0:T(8,128)(2,1)S(1)} %copy-done), custom_call_target="tpu_custom_call" | custom-call | flops 10737418240 | bytes 30408704 | tf_op jit(solution)/shard_map/pallas_call | solution.py:158
  231.6 23.5 %shard_map.172 = f32[2560,768]{1,0:T(8,128)} custom-call(s32[3]{0:T(128)S(1)} %add_add_fusion.1.at_ref, bf16[4096,5120]{1,0:T(8,128)(2,1)} %get-tuple-element.177.a_ref, bf16[4096,1280]{1,0:T(8,128)(2,1)} %r_ref.3), custom_call_target="tpu_custom_call" | custom-call | flops 16106127360 | bytes 35127296 | tf_op jit(solution)/shard_map/pallas_call | solution.py:158
  256.0 19.8 %collective-permute-done.refs_0_ = f32[2560,512]{1,0:T(8,128)} collective-permute-done((f32[2560,512]{1,0:T(8,128)}, f32[2560,512]{1,0:T(8,128)}, u32[]{:S(2)}, u32[]{:S(2)}) %collective-permute-start) | collective-permute-done | bytes 5242912 | tf_op jit(solution)/shard_map/ppermute | solution.py:235
  275.8 16.6 %shard_map.173 = (f32[2560,512]{1,0:T(8,128)S(1)}, f32[2,320,512]{2,1,0:T(8,128)S(1)}, f32[2,320,512]{2,1,0:T(8,128)S(1)}) custom-call(s32[3]{0:T(128)S(1)} %add_add_fusion.at_ref, bf16[4096,5120]{1,0:T(8,128)(2,1)} %get-tuple-element.177.a_ref, bf16[4096,1280]{1,0:T(8,128)(2,1)} %r_ref.3, f32[2560,512]{1,0:T(8,128)} %collective-permute-done.refs_0_), custom_call_target="tpu_custom_call" | custom-call | flops 10737418240 | bytes 30408704 | tf_op jit(solution)/shard_map/pallas_call | solution.py:158
  296.8 23.9 %shard_map.174 = (f32[2560,768]{1,0:T(8,128)S(1)}, f32[2,320,768]{2,1,0:T(8,128)}, f32[2,320,768]{2,1,0:T(8,128)S(1)}) custom-call(s32[3]{0:T(128)S(1)} %add_add_fusion.at_ref, bf16[4096,5120]{1,0:T(8,128)(2,1)} %get-tuple-element.177.a_ref, bf16[4096,1280]{1,0:T(8,128)(2,1)} %r_ref.3, f32[2560,768]{1,0:T(8,128)} %collective-permute-done.1.refs_0_), custom_call_target="tpu_custom_call" | custom-call | flops 16106127360 | bytes 35127296 | tf_op jit(solution)/shard_map/pallas_call | solution.py:158
  320.7 3.2 copy-done.1
  331.4 44.9 %shard_map.175.b_ref.a_ref = bf16[4096,2560]{1,0:T(8,128)(2,1)} custom-call(bf16[4096,1280]{1,0:T(8,128)(2,1)} %r_ref.3, bf16[5120,1280]{1,0:T(8,128)(2,1)} %w_ref.9, bf16[4096,5120]{1,0:T(8,128)(2,1)} %get-tuple-element.189.z_ref), custom_call_target="tpu_custom_call" | custom-call | flops 26843545600 | bytes 58982400 | tf_op jit(solution)/shard_map/pallas_call | solution.py:78
  376.3 3.3 bitcast_add_fusion.6
  381.8 20.1 %shard_map.176 = f32[640,2560]{1,0:T(8,128)} custom-call(s32[3]{0:T(128)} %copy-done.3, bf16[4096,1280]{1,0:T(8,128)(2,1)} %add_convert_fusion.x_ref.a_ref, bf16[4096,2560]{1,0:T(8,128)(2,1)} %shard_map.175.b_ref.a_ref), custom_call_target="tpu_custom_call" | custom-call | flops 13421772800 | bytes 32768000 | tf_op jit(solution)/shard_map/pallas_call | solution.py:158
  402.0 4.7 collective-permute-done.8
  412.4 4.5 subtract_convert_fusion.2
  417.0 45.2 %shard_map.177.b_ref = bf16[4096,2560]{1,0:T(8,128)(2,1)} custom-call(bf16[4096,1280]{1,0:T(8,128)(2,1)} %r_ref.3, bf16[5120,1280]{1,0:T(8,128)(2,1)} %w_ref.9, bf16[4096,5120]{1,0:T(8,128)(2,1)} %get-tuple-element.189.z_ref), custom_call_target="tpu_custom_call" | custom-call | flops 26843545600 | bytes 58982400 | tf_op jit(solution)/shard_map/pallas_call | solution.py:78
  462.3 20.2 %shard_map.178 = f32[640,2560]{1,0:T(8,128)} custom-call(s32[3]{0:T(128)} %copy-done.3, bf16[4096,1280]{1,0:T(8,128)(2,1)} %add_convert_fusion.x_ref.a_ref, bf16[4096,2560]{1,0:T(8,128)(2,1)} %shard_map.177.b_ref), custom_call_target="tpu_custom_call" | custom-call | flops 13421772800 | bytes 32768000 | tf_op jit(solution)/shard_map/pallas_call | solution.py:158
  482.9 21.6 %shard_map.179 = (f32[640,2560]{1,0:T(8,128)}, f32[2,80,2560]{2,1,0:T(8,128)}, f32[2,80,2560]{2,1,0:T(8,128)}) custom-call(s32[3]{0:T(128)} %copy-done.4, bf16[4096,1280]{1,0:T(8,128)(2,1)} %add_convert_fusion.x_ref.a_ref, bf16[4096,2560]{1,0:T(8,128)(2,1)} %shard_map.175.b_ref.a_ref, f32[640,2560]{1,0:T(8,128)} %collective-permute-done.10.refs_0_), custom_call_target="tpu_custom_call" | custom-call | flops 13421772800 | bytes 32768000 | tf_op jit(solution)/shard_map/pallas_call | solution.py:158
  507.5 21.4 %shard_map.180 = (f32[640,2560]{1,0:T(8,128)}, f32[2,80,2560]{2,1,0:T(8,128)}, f32[2,80,2560]{2,1,0:T(8,128)}) custom-call(s32[3]{0:T(128)} %copy-done.4, bf16[4096,1280]{1,0:T(8,128)(2,1)} %add_convert_fusion.x_ref.a_ref, bf16[4096,2560]{1,0:T(8,128)(2,1)} %shard_map.177.b_ref, f32[640,2560]{1,0:T(8,128)} %collective-permute-done.11.refs_0_), custom_call_target="tpu_custom_call" | custom-call | flops 13421772800 | bytes 32768000 | tf_op jit(solution)/shard_map/pallas_call | solution.py:158
  530.0 36.5 %shard_map.181.refs_0_ = bf16[4096,1280]{1,0:T(8,128)(2,1)} custom-call(bf16[4096,2560]{1,0:T(8,128)(2,1)} %shard_map.175.b_ref.a_ref, bf16[4096,2560]{1,0:T(8,128)(2,1)} %shard_map.177.b_ref, bf16[1280,5120]{1,0:T(8,128)(2,1)} %wb_ref.5, bf16[1280,5120]{1,0:T(8,128)(2,1)} %wb_ref.5, bf16[4096,1280]{1,0:T(8,128)(2,1)} %r_ref.3), custom_call_target="tpu_custom_call" | custom-call | flops 26843545600 | bytes 44564480 | tf_op jit(solution)/shard_map/pallas_call | solution.py:105
  572.0 36.4 %shard_map.182.b_ref.g_ref.r_ref = bf16[4096,1280]{1,0:T(8,128)(2,1)} custom-call(bf16[4096,2560]{1,0:T(8,128)(2,1)} %shard_map.175.b_ref.a_ref, bf16[4096,2560]{1,0:T(8,128)(2,1)} %shard_map.177.b_ref, bf16[1280,5120]{1,0:T(8,128)(2,1)} %wb_ref.5, bf16[1280,5120]{1,0:T(8,128)(2,1)} %wb_ref.5, ...), custom_call_target="tpu_custom_call", output_to_operand_aliasing={{}: (5, {})} | custom-call | flops 26843545600 | bytes 44564480 | tf_op jit(solution)/shard_map/pallas_call | solution.py:105
  608.4 3.2 bitcast_add_fusion.20
  612.7 17.4 %shard_map.183 = f32[2560,512]{1,0:T(8,128)} custom-call(s32[3]{0:T(128)} %copy-done.3, bf16[4096,5120]{1,0:T(8,128)(2,1)} %get-tuple-element.170.a_ref, bf16[4096,1280]{1,0:T(8,128)(2,1)} %shard_map.182.b_ref.g_ref.r_ref), custom_call_target="tpu_custom_call" | custom-call | flops 10737418240 | bytes 30408704 | tf_op jit(solution)/shard_map/pallas_call | solution.py:158
  630.7 4.5 fusion.24
  635.2 4.5 subtract_convert_fusion.1
  639.8 24.0 %shard_map.184 = f32[2560,768]{1,0:T(8,128)} custom-call(s32[3]{0:T(128)} %copy-done.3, bf16[4096,5120]{1,0:T(8,128)(2,1)} %get-tuple-element.170.a_ref, bf16[4096,1280]{1,0:T(8,128)(2,1)} %shard_map.182.b_ref.g_ref.r_ref), custom_call_target="tpu_custom_call" | custom-call | flops 16106127360 | bytes 35127296 | tf_op jit(solution)/shard_map/pallas_call | solution.py:158
  664.2 26.2 %collective-permute-done.20.refs_0_ = f32[2560,512]{1,0:T(8,128)} collective-permute-done((f32[2560,512]{1,0:T(8,128)}, f32[2560,512]{1,0:T(8,128)}, u32[]{:S(2)}, u32[]{:S(2)}) %collective-permute-start.20) | collective-permute-done | bytes 5242912 | tf_op jit(solution)/shard_map/ppermute | solution.py:235
  690.4 19.0 %shard_map.185 = (f32[2560,512]{1,0:T(8,128)}, f32[2,320,512]{2,1,0:T(8,128)}, f32[2,320,512]{2,1,0:T(8,128)}) custom-call(s32[3]{0:T(128)} %copy-done.4, bf16[4096,5120]{1,0:T(8,128)(2,1)} %get-tuple-element.170.a_ref, bf16[4096,1280]{1,0:T(8,128)(2,1)} %shard_map.182.b_ref.g_ref.r_ref, f32[2560,512]{1,0:T(8,128)} %collective-permute-done.20.refs_0_), custom_call_target="tpu_custom_call" | custom-call | flops 10737418240 | bytes 30408704 | tf_op jit(solution)/shard_map/pallas_call | solution.py:158
  711.2 25.2 %shard_map.186 = (f32[2560,768]{1,0:T(8,128)}, f32[2,320,768]{2,1,0:T(8,128)}, f32[2,320,768]{2,1,0:T(8,128)}) custom-call(s32[3]{0:T(128)} %copy-done.4, bf16[4096,5120]{1,0:T(8,128)(2,1)} %get-tuple-element.170.a_ref, bf16[4096,1280]{1,0:T(8,128)(2,1)} %shard_map.182.b_ref.g_ref.r_ref, f32[2560,768]{1,0:T(8,128)} %collective-permute-done.21.refs_0_), custom_call_target="tpu_custom_call" | custom-call | flops 16106127360 | bytes 35127296 | tf_op jit(solution)/shard_map/pallas_call | solution.py:158
  738.7 45.1 %shard_map.187.b_ref.a_ref = bf16[4096,2560]{1,0:T(8,128)(2,1)} custom-call(bf16[4096,1280]{1,0:T(8,128)(2,1)} %shard_map.182.b_ref.g_ref.r_ref, bf16[5120,1280]{1,0:T(8,128)(2,1)} %w_ref.11, bf16[4096,5120]{1,0:T(8,128)(2,1)} %get-tuple-element.251.z_ref), custom_call_target="tpu_custom_call" | custom-call | flops 26843545600 | bytes 58982400 | tf_op jit(solution)/shard_map/pallas_call | solution.py:78
  783.8 20.2 %shard_map.188 = f32[640,2560]{1,0:T(8,128)} custom-call(s32[3]{0:T(128)} %copy-done.3, bf16[4096,1280]{1,0:T(8,128)(2,1)} %a_ref.7, bf16[4096,2560]{1,0:T(8,128)(2,1)} %shard_map.187.b_ref.a_ref), custom_call_target="tpu_custom_call" | custom-call | flops 13421772800 | bytes 32768000 | tf_op jit(solution)/shard_map/pallas_call | solution.py:158
  804.0 3.0 bitcast_add_fusion.26
  807.0 3.0 bitcast_add_fusion.2
  814.1 44.8 %shard_map.189.b_ref = bf16[4096,2560]{1,0:T(8,128)(2,1)} custom-call(bf16[4096,1280]{1,0:T(8,128)(2,1)} %shard_map.182.b_ref.g_ref.r_ref, bf16[5120,1280]{1,0:T(8,128)(2,1)} %w_ref.11, bf16[4096,5120]{1,0:T(8,128)(2,1)} %get-tuple-element.251.z_ref), custom_call_target="tpu_custom_call" | custom-call | flops 26843545600 | bytes 58982400 | tf_op jit(solution)/shard_map/pallas_call | solution.py:78
  864.6 4.5 subtract_convert_fusion
  869.2 10.9 collective-permute-done.30.refs_0_
  880.0 21.7 %shard_map.190 = (f32[640,2560]{1,0:T(8,128)}, f32[2,80,2560]{2,1,0:T(8,128)}, f32[2,80,2560]{2,1,0:T(8,128)}) custom-call(s32[3]{0:T(128)} %copy-done.4, bf16[4096,1280]{1,0:T(8,128)(2,1)} %a_ref.7, bf16[4096,2560]{1,0:T(8,128)(2,1)} %shard_map.187.b_ref.a_ref, f32[640,2560]{1,0:T(8,128)} %collective-permute-done.30.refs_0_), custom_call_target="tpu_custom_call" | custom-call | flops 13421772800 | bytes 32768000 | tf_op jit(solution)/shard_map/pallas_call | solution.py:158
  901.7 20.1 %shard_map.191 = f32[640,2560]{1,0:T(8,128)} custom-call(s32[3]{0:T(128)} %copy-done.3, bf16[4096,1280]{1,0:T(8,128)(2,1)} %a_ref.7, bf16[4096,2560]{1,0:T(8,128)(2,1)} %shard_map.189.b_ref), custom_call_target="tpu_custom_call" | custom-call | flops 13421772800 | bytes 32768000 | tf_op jit(solution)/shard_map/pallas_call | solution.py:158
  923.9 11.3 shard_map.192
  935.2 21.5 %shard_map.193 = (f32[640,2560]{1,0:T(8,128)}, f32[2,80,2560]{2,1,0:T(8,128)}, f32[2,80,2560]{2,1,0:T(8,128)}) custom-call(s32[3]{0:T(128)} %copy-done.4, bf16[4096,1280]{1,0:T(8,128)(2,1)} %a_ref.7, bf16[4096,2560]{1,0:T(8,128)(2,1)} %shard_map.189.b_ref, f32[640,2560]{1,0:T(8,128)} %collective-permute-done.31.refs_0_), custom_call_target="tpu_custom_call" | custom-call | flops 13421772800 | bytes 32768000 | tf_op jit(solution)/shard_map/pallas_call | solution.py:158
  956.7 13.8 %collective-permute-done.32 = f32[2,80,2560]{2,1,0:T(8,128)S(1)} collective-permute-done((f32[2,80,2560]{2,1,0:T(8,128)}, f32[2,80,2560]{2,1,0:T(8,128)S(1)}, u32[]{:S(2)}, u32[]{:S(2)}) %collective-permute-start.32) | collective-permute-done | bytes 1638432 | tf_op jit(solution)/shard_map/ppermute | solution.py:198
  975.3 36.4 %shard_map.194.refs_0_ = bf16[4096,1280]{1,0:T(8,128)(2,1)} custom-call(bf16[4096,2560]{1,0:T(8,128)(2,1)} %shard_map.187.b_ref.a_ref, bf16[4096,2560]{1,0:T(8,128)(2,1)} %shard_map.189.b_ref, bf16[1280,5120]{1,0:T(8,128)(2,1)} %wb_ref.7, bf16[1280,5120]{1,0:T(8,128)(2,1)} %wb_ref.7, bf16[4096,1280]{1,0:T(8,128)(2,1)} %shard_map.182.b_ref.g_ref.r_ref), custom_call_target="tpu_custom_call" | custom-call | flops 26843545600 | bytes 44564480 | tf_op jit(solution)/shard_map/pallas_call | solution.py:105
  1019.0 11.7 %shard_map.195 = bf16[1280,5120]{1,0:T(8,128)(2,1)} custom-call(bf16[1280,5120]{1,0:T(8,128)(2,1)} %all-gather.8.cloned.1.call-done.refs_0_), custom_call_target="tpu_custom_call" | custom-call | flops 419430400 | bytes 26214400 | tf_op jit(solution)/shard_map/pallas_call | solution.py:172
  1030.6 49.4 %collective-permute-done.36 = f32[2,80,2560]{2,1,0:T(8,128)S(1)} collective-permute-done((f32[2,80,2560]{2,1,0:T(8,128)}, f32[2,80,2560]{2,1,0:T(8,128)S(1)}, u32[]{:S(2)}, u32[]{:S(2)}) %collective-permute-start.36) | collective-permute-done | bytes 1638432 | tf_op jit(solution)/shard_map/ppermute | solution.py:198
  1081.8 3.0 bitcast_add_fusion.10
  1086.7 11.3 shard_map.196
  1108.1 37.2 %shard_map.197 = bf16[4096,1280]{1,0:T(8,128)(2,1)} custom-call(bf16[4096,2560]{1,0:T(8,128)(2,1)} %shard_map.187.b_ref.a_ref, bf16[4096,2560]{1,0:T(8,128)(2,1)} %shard_map.189.b_ref, bf16[1280,5120]{1,0:T(8,128)(2,1)} %wb_ref.7, bf16[1280,5120]{1,0:T(8,128)(2,1)} %wb_ref.7, ...), custom_call_target="tpu_custom_call", output_to_operand_aliasing={{}: (5, {})} | custom-call | flops 26843545600 | bytes 44564480 | tf_op jit(solution)/shard_map/pallas_call | solution.py:105
  1145.4 7.3 shard_map.198.refs_1_
  1152.7 7.3 shard_map.199
  (130 shorter events, 74.7 us)
Async XLA Ops:
  7.2 914.6 %all-gather.6.cloned.1.call-start = ((), (), s32[]{:S(2)}) async-start(), calls=%async_computation | async-start | bytes 14745600 | tf_op jit(solution)/shard_map/all_gather | solution.py:253
  7.2 74.0 %copy-start.13 = (bf16[5120,1280]{1,0:T(8,128)(2,1)S(1)}, bf16[5120,1280]{1,0:T(8,128)(2,1)}, u32[]{:S(2)}) copy-start(bf16[5120,1280]{1,0:T(8,128)(2,1)} %w_ref.11) | copy-start | bytes 39321604
  141.0 74.8 %copy-start = (bf16[4096,1280]{1,0:T(8,128)(2,1)S(1)}, bf16[4096,1280]{1,0:T(8,128)(2,1)}, u32[]{:S(2)}) copy-start(bf16[4096,1280]{1,0:T(8,128)(2,1)} %r_ref.3) | copy-start | bytes 31457284
  255.1 41.7 %collective-permute-start.1 = (f32[2560,768]{1,0:T(8,128)}, f32[2560,768]{1,0:T(8,128)}, u32[]{:S(2)}, u32[]{:S(2)}) collective-permute-start(f32[2560,768]{1,0:T(8,128)} %shard_map.172), channel_id=1, source_target_pairs={{0,1},{1,0},{2,3},{3,2},{4,5},{5,4},{6,7},{7,6}} | collective-permute-start | bytes 23592968 | tf_op jit(solution)/shard_map/ppermute | solution.py:235
  255.9 19.9 %collective-permute-start = (f32[2560,512]{1,0:T(8,128)}, f32[2560,512]{1,0:T(8,128)}, u32[]{:S(2)}, u32[]{:S(2)}) collective-permute-start(f32[2560,512]{1,0:T(8,128)} %shard_map.171), channel_id=1, source_target_pairs={{0,1},{1,0},{2,3},{3,2},{4,5},{5,4},{6,7},{7,6}} | collective-permute-start | bytes 15728648 | tf_op jit(solution)/shard_map/ppermute | solution.py:235
  256.0 40.8 %copy-start.4 = (s32[3]{0:T(128)}, s32[3]{0:T(128)S(1)}, u32[]{:S(2)}) copy-start(s32[3]{0:T(128)S(1)} %add_add_fusion.at_ref) | copy-start | bytes 40
  292.4 32.0 %collective-permute-start.2 = (f32[2,320,512]{2,1,0:T(8,128)S(1)}, f32[2,320,512]{2,1,0:T(8,128)S(1)}, u32[]{:S(2)}, u32[]{:S(2)}) collective-permute-start(f32[2,320,512]{2,1,0:T(8,128)S(1)} %get-tuple-element.182), channel_id=1, source_target_pairs={{0,2},{2,0},{1,3},{3,1},{4,6},{6,4},{5,7},{7,5}} | collective-permute-start | bytes 3932168 | tf_op jit(solution)/shard_map/ppermute | solution.py:198
  295.2 30.5 %collective-permute-start.3 = (f32[2,320,512]{2,1,0:T(8,128)S(1)}, f32[2,320,512]{2,1,0:T(8,128)S(1)}, u32[]{:S(2)}, u32[]{:S(2)}) collective-permute-start(f32[2,320,512]{2,1,0:T(8,128)S(1)} %get-tuple-element.183), channel_id=1, source_target_pairs={{0,4},{4,0},{1,5},{5,1},{2,6},{6,2},{3,7},{7,3}} | collective-permute-start | bytes 3932168 | tf_op jit(solution)/shard_map/ppermute | solution.py:198
  327.3 49.0 %collective-permute-start.4 = (f32[2,320,768]{2,1,0:T(8,128)}, f32[2,320,768]{2,1,0:T(8,128)S(1)}, u32[]{:S(2)}, u32[]{:S(2)}) collective-permute-start(f32[2,320,768]{2,1,0:T(8,128)} %get-tuple-element.190), channel_id=1, source_target_pairs={{0,2},{2,0},{1,3},{3,1},{4,6},{6,4},{5,7},{7,5}} | collective-permute-start | bytes 5898248 | tf_op jit(solution)/shard_map/ppermute | solution.py:198
  327.7 48.5 %collective-permute-start.5 = (f32[2,320,768]{2,1,0:T(8,128)S(1)}, f32[2,320,768]{2,1,0:T(8,128)}, u32[]{:S(2)}, u32[]{:S(2)}) collective-permute-start(f32[2,320,768]{2,1,0:T(8,128)S(1)} %get-tuple-element.191), channel_id=1, source_target_pairs={{0,4},{4,0},{1,5},{5,1},{2,6},{6,2},{3,7},{7,3}} | collective-permute-start | bytes 5898248 | tf_op jit(solution)/shard_map/ppermute | solution.py:198
  329.5 72.4 %collective-permute-start.6 = (f32[1,320,512]{2,1,0:T(8,128)}, f32[1,320,512]{2,1,0:T(8,128)}, u32[]{:S(2)}, u32[]{:S(2)}) collective-permute-start(f32[1,320,512]{2,1,0:T(8,128)} %get-tuple-element.198), channel_id=1, source_target_pairs={{0,4},{4,0},{1,5},{5,1},{2,6},{6,2},{3,7},{7,3}} | collective-permute-start | bytes 1966088 | tf_op jit(solution)/shard_map/ppermute | solution.py:198
  329.8 72.2 %collective-permute-start.7 = (f32[1,320,512]{2,1,0:T(8,128)}, f32[1,320,512]{2,1,0:T(8,128)}, u32[]{:S(2)}, u32[]{:S(2)}) collective-permute-start(f32[1,320,512]{2,1,0:T(8,128)} %get-tuple-element.199), channel_id=1, source_target_pairs={{0,2},{2,0},{1,3},{3,1},{4,6},{6,4},{5,7},{7,5}} | collective-permute-start | bytes 1966088 | tf_op jit(solution)/shard_map/ppermute | solution.py:198
  379.6 27.1 %collective-permute-start.8 = (f32[1,320,768]{2,1,0:T(8,128)}, f32[1,320,768]{2,1,0:T(8,128)}, u32[]{:S(2)}, u32[]{:S(2)}) collective-permute-start(f32[1,320,768]{2,1,0:T(8,128)} %get-tuple-element.200), channel_id=1, source_target_pairs={{0,4},{4,0},{1,5},{5,1},{2,6},{6,2},{3,7},{7,3}} | collective-permute-start | bytes 2949128 | tf_op jit(solution)/shard_map/ppermute | solution.py:198
  381.1 25.6 %collective-permute-start.9 = (f32[1,320,768]{2,1,0:T(8,128)}, f32[1,320,768]{2,1,0:T(8,128)}, u32[]{:S(2)}, u32[]{:S(2)}) collective-permute-start(f32[1,320,768]{2,1,0:T(8,128)} %get-tuple-element.201), channel_id=1, source_target_pairs={{0,2},{2,0},{1,3},{3,1},{4,6},{6,4},{5,7},{7,5}} | collective-permute-start | bytes 2949128 | tf_op jit(solution)/shard_map/ppermute | solution.py:198
  417.0 602.0 %all-gather.8.cloned.1.call-start = ((), (), s32[]{:S(2)}) async-start(), calls=%async_computation.1 | async-start | bytes 14745600 | tf_op jit(solution)/shard_map/all_gather | solution.py:253
  417.0 65.8 %collective-permute-start.10 = (f32[640,2560]{1,0:T(8,128)}, f32[640,2560]{1,0:T(8,128)}, u32[]{:S(2)}, u32[]{:S(2)}) collective-permute-start(f32[640,2560]{1,0:T(8,128)} %shard_map.176), channel_id=1, source_target_pairs={{0,1},{1,0},{2,3},{3,2},{4,5},{5,4},{6,7},{7,6}} | collective-permute-start | bytes 19660808 | tf_op jit(solution)/shard_map/ppermute | solution.py:235
  482.5 25.0 %collective-permute-start.11 = (f32[640,2560]{1,0:T(8,128)}, f32[640,2560]{1,0:T(8,128)}, u32[]{:S(2)}, u32[]{:S(2)}) collective-permute-start(f32[640,2560]{1,0:T(8,128)} %shard_map.178), channel_id=1, source_target_pairs={{0,1},{1,0},{2,3},{3,2},{4,5},{5,4},{6,7},{7,6}} | collective-permute-start | bytes 19660808 | tf_op jit(solution)/shard_map/ppermute | solution.py:235
  504.5 62.0 %collective-permute-start.12 = (f32[2,80,2560]{2,1,0:T(8,128)}, f32[2,80,2560]{2,1,0:T(8,128)S(1)}, u32[]{:S(2)}, u32[]{:S(2)}) collective-permute-start(f32[2,80,2560]{2,1,0:T(8,128)} %get-tuple-element.217), channel_id=1, source_target_pairs={{0,2},{2,0},{1,3},{3,1},{4,6},{6,4},{5,7},{7,5}} | collective-permute-start | bytes 4915208 | tf_op jit(solution)/shard_map/ppermute | solution.py:198
  505.8 60.7 %collective-permute-start.13 = (f32[2,80,2560]{2,1,0:T(8,128)}, f32[2,80,2560]{2,1,0:T(8,128)S(1)}, u32[]{:S(2)}, u32[]{:S(2)}) collective-permute-start(f32[2,80,2560]{2,1,0:T(8,128)} %get-tuple-element.218), channel_id=1, source_target_pairs={{0,4},{4,0},{1,5},{5,1},{2,6},{6,2},{3,7},{7,3}} | collective-permute-start | bytes 4915208 | tf_op jit(solution)/shard_map/ppermute | solution.py:198
  528.9 79.4 %collective-permute-start.14 = (f32[2,80,2560]{2,1,0:T(8,128)}, f32[2,80,2560]{2,1,0:T(8,128)}, u32[]{:S(2)}, u32[]{:S(2)}) collective-permute-start(f32[2,80,2560]{2,1,0:T(8,128)} %get-tuple-element.224), channel_id=1, source_target_pairs={{0,2},{2,0},{1,3},{3,1},{4,6},{6,4},{5,7},{7,5}} | collective-permute-start | bytes 4915208 | tf_op jit(solution)/shard_map/ppermute | solution.py:198
  529.5 78.8 %collective-permute-start.15 = (f32[2,80,2560]{2,1,0:T(8,128)}, f32[2,80,2560]{2,1,0:T(8,128)}, u32[]{:S(2)}, u32[]{:S(2)}) collective-permute-start(f32[2,80,2560]{2,1,0:T(8,128)} %get-tuple-element.225), channel_id=1, source_target_pairs={{0,4},{4,0},{1,5},{5,1},{2,6},{6,2},{3,7},{7,3}} | collective-permute-start | bytes 4915208 | tf_op jit(solution)/shard_map/ppermute | solution.py:198
  569.0 61.1 %collective-permute-start.16 = (f32[1,80,2560]{2,1,0:T(8,128)}, f32[1,80,2560]{2,1,0:T(8,128)}, u32[]{:S(2)}, u32[]{:S(2)}) collective-permute-start(f32[1,80,2560]{2,1,0:T(8,128)} %get-tuple-element.232), channel_id=1, source_target_pairs={{0,4},{4,0},{1,5},{5,1},{2,6},{6,2},{3,7},{7,3}} | collective-permute-start | bytes 2457608 | tf_op jit(solution)/shard_map/ppermute | solution.py:198
  570.6 59.6 %collective-permute-start.17 = (f32[1,80,2560]{2,1,0:T(8,128)S(1)}, f32[1,80,2560]{2,1,0:T(8,128)}, u32[]{:S(2)}, u32[]{:S(2)}) collective-permute-start(f32[1,80,2560]{2,1,0:T(8,128)S(1)} %get-tuple-element.233), channel_id=1, source_target_pairs={{0,2},{2,0},{1,3},{3,1},{4,6},{6,4},{5,7},{7,5}} | collective-permute-start | bytes 2457608 | tf_op jit(solution)/shard_map/ppermute | solution.py:198
  611.6 18.7 %collective-permute-start.18 = (f32[1,80,2560]{2,1,0:T(8,128)}, f32[1,80,2560]{2,1,0:T(8,128)}, u32[]{:S(2)}, u32[]{:S(2)}) collective-permute-start(f32[1,80,2560]{2,1,0:T(8,128)} %get-tuple-element.234), channel_id=1, source_target_pairs={{0,4},{4,0},{1,5},{5,1},{2,6},{6,2},{3,7},{7,3}} | collective-permute-start | bytes 2457608 | tf_op jit(solution)/shard_map/ppermute | solution.py:198
  612.0 18.7 %collective-permute-start.19 = (f32[1,80,2560]{2,1,0:T(8,128)}, f32[1,80,2560]{2,1,0:T(8,128)}, u32[]{:S(2)}, u32[]{:S(2)}) collective-permute-start(f32[1,80,2560]{2,1,0:T(8,128)} %get-tuple-element.235), channel_id=1, source_target_pairs={{0,2},{2,0},{1,3},{3,1},{4,6},{6,4},{5,7},{7,5}} | collective-permute-start | bytes 2457608 | tf_op jit(solution)/shard_map/ppermute | solution.py:198
  639.7 442.1 %all-gather.10.cloned.1.call-start = ((), (), s32[]{:S(2)}) async-start(), calls=%async_computation.2 | async-start | bytes 14745600 | tf_op jit(solution)/shard_map/all_gather | solution.py:253
  663.7 47.4 %collective-permute-start.21 = (f32[2560,768]{1,0:T(8,128)}, f32[2560,768]{1,0:T(8,128)}, u32[]{:S(2)}, u32[]{:S(2)}) collective-permute-start(f32[2560,768]{1,0:T(8,128)} %shard_map.184), channel_id=1, source_target_pairs={{0,1},{1,0},{2,3},{3,2},{4,5},{5,4},{6,7},{7,6}} | collective-permute-start | bytes 23592968 | tf_op jit(solution)/shard_map/ppermute | solution.py:235
  663.7 26.7 %collective-permute-start.20 = (f32[2560,512]{1,0:T(8,128)}, f32[2560,512]{1,0:T(8,128)}, u32[]{:S(2)}, u32[]{:S(2)}) collective-permute-start(f32[2560,512]{1,0:T(8,128)} %shard_map.183), channel_id=1, source_target_pairs={{0,1},{1,0},{2,3},{3,2},{4,5},{5,4},{6,7},{7,6}} | collective-permute-start | bytes 15728648 | tf_op jit(solution)/shard_map/ppermute | solution.py:235
  709.4 94.5 %collective-permute-start.22 = (f32[2,320,512]{2,1,0:T(8,128)}, f32[2,320,512]{2,1,0:T(8,128)}, u32[]{:S(2)}, u32[]{:S(2)}) collective-permute-start(f32[2,320,512]{2,1,0:T(8,128)} %get-tuple-element.253), channel_id=1, source_target_pairs={{0,2},{2,0},{1,3},{3,1},{4,6},{6,4},{5,7},{7,5}} | collective-permute-start | bytes 3932168 | tf_op jit(solution)/shard_map/ppermute | solution.py:198
  709.5 94.4 %collective-permute-start.23 = (f32[2,320,512]{2,1,0:T(8,128)}, f32[2,320,512]{2,1,0:T(8,128)}, u32[]{:S(2)}, u32[]{:S(2)}) collective-permute-start(f32[2,320,512]{2,1,0:T(8,128)} %get-tuple-element.254), channel_id=1, source_target_pairs={{0,4},{4,0},{1,5},{5,1},{2,6},{6,2},{3,7},{7,3}} | collective-permute-start | bytes 3932168 | tf_op jit(solution)/shard_map/ppermute | solution.py:198
  736.4 67.6 %collective-permute-start.24 = (f32[2,320,768]{2,1,0:T(8,128)}, f32[2,320,768]{2,1,0:T(8,128)S(1)}, u32[]{:S(2)}, u32[]{:S(2)}) collective-permute-start(f32[2,320,768]{2,1,0:T(8,128)} %get-tuple-element.255), channel_id=1, source_target_pairs={{0,2},{2,0},{1,3},{3,1},{4,6},{6,4},{5,7},{7,5}} | collective-permute-start | bytes 5898248 | tf_op jit(solution)/shard_map/ppermute | solution.py:198
  737.9 66.1 %collective-permute-start.25 = (f32[2,320,768]{2,1,0:T(8,128)}, f32[2,320,768]{2,1,0:T(8,128)S(1)}, u32[]{:S(2)}, u32[]{:S(2)}) collective-permute-start(f32[2,320,768]{2,1,0:T(8,128)} %get-tuple-element.256), channel_id=1, source_target_pairs={{0,4},{4,0},{1,5},{5,1},{2,6},{6,2},{3,7},{7,3}} | collective-permute-start | bytes 5898248 | tf_op jit(solution)/shard_map/ppermute | solution.py:198
  810.0 48.9 %collective-permute-start.28 = (f32[1,320,768]{2,1,0:T(8,128)}, f32[1,320,768]{2,1,0:T(8,128)}, u32[]{:S(2)}, u32[]{:S(2)}) collective-permute-start(f32[1,320,768]{2,1,0:T(8,128)} %get-tuple-element.267), channel_id=1, source_target_pairs={{0,4},{4,0},{1,5},{5,1},{2,6},{6,2},{3,7},{7,3}} | collective-permute-start | bytes 2949128 | tf_op jit(solution)/shard_map/ppermute | solution.py:198
  811.3 47.6 %collective-permute-start.29 = (f32[1,320,768]{2,1,0:T(8,128)}, f32[1,320,768]{2,1,0:T(8,128)}, u32[]{:S(2)}, u32[]{:S(2)}) collective-permute-start(f32[1,320,768]{2,1,0:T(8,128)} %get-tuple-element.268), channel_id=1, source_target_pairs={{0,2},{2,0},{1,3},{3,1},{4,6},{6,4},{5,7},{7,5}} | collective-permute-start | bytes 2949128 | tf_op jit(solution)/shard_map/ppermute | solution.py:198
  811.8 47.1 %collective-permute-start.26 = (f32[1,320,512]{2,1,0:T(8,128)}, f32[1,320,512]{2,1,0:T(8,128)}, u32[]{:S(2)}, u32[]{:S(2)}) collective-permute-start(f32[1,320,512]{2,1,0:T(8,128)} %get-tuple-element.265), channel_id=1, source_target_pairs={{0,4},{4,0},{1,5},{5,1},{2,6},{6,2},{3,7},{7,3}} | collective-permute-start | bytes 1966088 | tf_op jit(solution)/shard_map/ppermute | solution.py:198
  812.2 46.7 %collective-permute-start.27 = (f32[1,320,512]{2,1,0:T(8,128)}, f32[1,320,512]{2,1,0:T(8,128)}, u32[]{:S(2)}, u32[]{:S(2)}) collective-permute-start(f32[1,320,512]{2,1,0:T(8,128)} %get-tuple-element.266), channel_id=1, source_target_pairs={{0,2},{2,0},{1,3},{3,1},{4,6},{6,4},{5,7},{7,5}} | collective-permute-start | bytes 1966088 | tf_op jit(solution)/shard_map/ppermute | solution.py:198
  869.1 276.3 %all-gather.12.cloned.1.call-start = ((), (), s32[]{:S(2)}) async-start(), calls=%async_computation.3 | async-start | bytes 7372800 | tf_op jit(solution)/shard_map/all_gather | solution.py:253
  869.1 10.9 collective-permute-start.30
  921.8 13.4 %collective-permute-start.31 = (f32[640,2560]{1,0:T(8,128)}, f32[640,2560]{1,0:T(8,128)}, u32[]{:S(2)}, u32[]{:S(2)}) collective-permute-start(f32[640,2560]{1,0:T(8,128)} %shard_map.191), channel_id=1, source_target_pairs={{0,1},{1,0},{2,3},{3,2},{4,5},{5,4},{6,7},{7,6}} | collective-permute-start | bytes 19660808 | tf_op jit(solution)/shard_map/ppermute | solution.py:235
  922.1 48.4 %collective-permute-start.32 = (f32[2,80,2560]{2,1,0:T(8,128)}, f32[2,80,2560]{2,1,0:T(8,128)S(1)}, u32[]{:S(2)}, u32[]{:S(2)}) collective-permute-start(f32[2,80,2560]{2,1,0:T(8,128)} %get-tuple-element.287), channel_id=1, source_target_pairs={{0,2},{2,0},{1,3},{3,1},{4,6},{6,4},{5,7},{7,5}} | collective-permute-start | bytes 4915208 | tf_op jit(solution)/shard_map/ppermute | solution.py:198
  922.2 48.4 %collective-permute-start.33 = (f32[2,80,2560]{2,1,0:T(8,128)}, f32[2,80,2560]{2,1,0:T(8,128)S(1)}, u32[]{:S(2)}, u32[]{:S(2)}) collective-permute-start(f32[2,80,2560]{2,1,0:T(8,128)} %get-tuple-element.288), channel_id=1, source_target_pairs={{0,4},{4,0},{1,5},{5,1},{2,6},{6,2},{3,7},{7,3}} | collective-permute-start | bytes 4915208 | tf_op jit(solution)/shard_map/ppermute | solution.py:198
  973.3 38.4 %collective-permute-start.34 = (f32[1,80,2560]{2,1,0:T(8,128)}, f32[1,80,2560]{2,1,0:T(8,128)S(1)}, u32[]{:S(2)}, u32[]{:S(2)}) collective-permute-start(f32[1,80,2560]{2,1,0:T(8,128)} %get-tuple-element.294), channel_id=1, source_target_pairs={{0,4},{4,0},{1,5},{5,1},{2,6},{6,2},{3,7},{7,3}} | collective-permute-start | bytes 2457608 | tf_op jit(solution)/shard_map/ppermute | solution.py:198
  974.8 36.9 %collective-permute-start.35 = (f32[1,80,2560]{2,1,0:T(8,128)}, f32[1,80,2560]{2,1,0:T(8,128)}, u32[]{:S(2)}, u32[]{:S(2)}) collective-permute-start(f32[1,80,2560]{2,1,0:T(8,128)} %get-tuple-element.295), channel_id=1, source_target_pairs={{0,2},{2,0},{1,3},{3,1},{4,6},{6,4},{5,7},{7,5}} | collective-permute-start | bytes 2457608 | tf_op jit(solution)/shard_map/ppermute | solution.py:198
  1016.8 135.8 %all-gather.14.cloned.1.call-start = ((), (), s32[]{:S(2)}) async-start(), calls=%async_computation.4 | async-start | bytes 7372800 | tf_op jit(solution)/shard_map/all_gather | solution.py:253
  1016.9 63.2 %collective-permute-start.36 = (f32[2,80,2560]{2,1,0:T(8,128)}, f32[2,80,2560]{2,1,0:T(8,128)S(1)}, u32[]{:S(2)}, u32[]{:S(2)}) collective-permute-start(f32[2,80,2560]{2,1,0:T(8,128)} %get-tuple-element.304), channel_id=1, source_target_pairs={{0,2},{2,0},{1,3},{3,1},{4,6},{6,4},{5,7},{7,5}} | collective-permute-start | bytes 4915208 | tf_op jit(solution)/shard_map/ppermute | solution.py:198
  1018.4 63.4 %collective-permute-start.37 = (f32[2,80,2560]{2,1,0:T(8,128)}, f32[2,80,2560]{2,1,0:T(8,128)}, u32[]{:S(2)}, u32[]{:S(2)}) collective-permute-start(f32[2,80,2560]{2,1,0:T(8,128)} %get-tuple-element.305), channel_id=1, source_target_pairs={{0,4},{4,0},{1,5},{5,1},{2,6},{6,2},{3,7},{7,3}} | collective-permute-start | bytes 4915208 | tf_op jit(solution)/shard_map/ppermute | solution.py:198
  1084.8 16.0 %collective-permute-start.38 = (f32[1,80,2560]{2,1,0:T(8,128)}, f32[1,80,2560]{2,1,0:T(8,128)}, u32[]{:S(2)}, u32[]{:S(2)}) collective-permute-start(f32[1,80,2560]{2,1,0:T(8,128)} %get-tuple-element.313), channel_id=1, source_target_pairs={{0,4},{4,0},{1,5},{5,1},{2,6},{6,2},{3,7},{7,3}} | collective-permute-start | bytes 2457608 | tf_op jit(solution)/shard_map/ppermute | solution.py:198
  1085.4 15.9 %collective-permute-start.39 = (f32[1,80,2560]{2,1,0:T(8,128)}, f32[1,80,2560]{2,1,0:T(8,128)}, u32[]{:S(2)}, u32[]{:S(2)}) collective-permute-start(f32[1,80,2560]{2,1,0:T(8,128)} %get-tuple-element.314), channel_id=1, source_target_pairs={{0,2},{2,0},{1,3},{3,1},{4,6},{6,4},{5,7},{7,5}} | collective-permute-start | bytes 2457608 | tf_op jit(solution)/shard_map/ppermute | solution.py:198
  (11 other events, 108.7 us)
Sparse Core Ops, SparseCore 0:
  417.1 70.3 all-gather.5
  639.8 68.9 all-gather.7
  869.2 78.6 all-gather.9
  1017.0 66.0 all-gather.11
  1106.3 40.9 all-gather.13
